TPU v7x, 32 devices: a whole 2x2x4 slice. The times are simulated.
32 devices in a mesh: space: 8 (over z, core), tracer: 4 (over y, x).
Axes of the slice: x: 2, y: 2, z: 4, core: 2. Of those that a mesh axis runs over, the one named last changes fastest.
Arguments:
- mixing_ratio_field: float32 [256, 2, 128, 256], P('tracer', None, 'space'), may hold values from 0.1 to 10
- eastward_face_cfl: float32 [2, 128, 256], P(None, 'space'), may hold values from 0.05 to 0.45
- northward_face_cfl: float32 [2, 128, 256], P(None, 'space'), may hold values from 0.05 to 0.45
- upward_face_cfl: float32 [2, 128, 256], P(None, 'space'), may hold values from 0.05 to 0.45
- thermal_anomaly: float32 [2, 128, 256], P(None, ('space', 'tracer')), may hold values from 0.8 to 1.2
- radiant_flux: float32 [2, 128, 256], P(None, ('space', 'tracer')), may hold values from 0.2 to 1
- daylight_mask: int32 [2, 128, 2], P(None, ('space', 'tracer')), may hold values from 0 to 1, as said below
- baseline_kinetic_coefficient: float32 [768], replicated, may hold values from 0.02 to 1
- arrhenius_barrier: float32 [768], replicated, may hold values from 0.5 to 3
- photodissociation_factor: float32 [768], replicated, may hold values from 0.02 to 1
- stoichiometry_table: int32 [3, 768], replicated, may hold values from 0 to 255
Outputs:
- result: float32 [256, 2, 128, 256], P(None, None, ('space', 'tracer'))
Inputs may be any that keep to these rules, and one draw needn't show every extreme that they name: For every level l, row x below 64 and block b, daylight_mask[l, x, b] + daylight_mask[l, x + 64, b] == 1: a block and the block 64 rows further along the first dimension are never both sunlit or both dark.
All inputs are finite; a program needn't handle non-finite values.
Results may differ from a plain program's by a relative error of at most 0.0003.
Values sent between devices are 32-bit elements; how exact they have to be, the bound alone decides.
No kernel may reach another device: no remote copies, remote signals or barrier semaphores. Data moves between devices by JAX's collectives and lax.ppermute only.
A program may use at most 128 MiB of HBM per device.

v0:
```python
import functools

import jax
import jax.numpy as jnp
from jax import lax
from jax.experimental import pallas as pl
from jax.experimental.pallas import tpu as pltpu
from jax.sharding import PartitionSpec as P

SECTIONS = 3
DAY_STEPS = 2
LANES = 128
SUB = 8
LOW = 2 * SECTIONS
HIGH = SECTIONS


def flat_rows(cells):
    *lead, rows, width = cells.shape
    sub = min(rows, SUB)
    split = cells.reshape(*lead, rows // sub, sub, width // LANES, LANES)
    return jnp.moveaxis(split, -2, -3).reshape(-1, LANES)


class Sizes:
    def __init__(self, field, groups):
        self.species, self.levels, self.rows, self.width = field.shape
        self.tiles = self.width // LANES
        self.groups = groups
        self.part = self.rows // groups
        self.blocks = self.levels * self.tiles * self.part
        self.stride = self.levels * self.rows * self.tiles
        self.columns = self.levels * self.tiles
        self.low_rows = LOW * self.columns * self.species
        self.high_rows = HIGH * self.columns * self.species
        self.edge_rows = 3 * self.columns * SUB

    def source_row(self, level, row, tile):
        return ((level * (self.rows // SUB) + row // SUB) * self.tiles + tile) * SUB + row % SUB

    def pairs(self):
        return [(level, tile) for level in range(self.levels) for tile in range(self.tiles)]


def pack_kernel(z, x_ref, east_ref, north_ref, up_ref, low_ref, high_ref):
    for offset, rows, out_ref in ((z.rows - LOW, LOW, low_ref), (0, HIGH, high_ref)):
        for row in range(rows):
            for col, (level, tile) in enumerate(z.pairs()):
                for start in range(0, z.species, SUB):
                    source = start * z.stride + z.source_row(level, row + offset, tile)
                    target = (row * z.columns + col) * z.species + start
                    out_ref[pl.ds(target, SUB), :] = x_ref[pl.ds(source, SUB, stride=z.stride), :]
    for out_ref, base, last in ((low_ref, z.low_rows, True), (high_ref, z.high_rows, False)):
        row = z.rows - SUB if last else 0
        for kind, ref in enumerate((east_ref, north_ref, up_ref)):
            for col, (level, tile) in enumerate(z.pairs()):
                target = base + (kind * z.columns + col) * SUB
                source = z.source_row(level, row, tile)
                out_ref[pl.ds(target, SUB), :] = ref[pl.ds(source, SUB), :]


def middle(a, b):
    return jnp.maximum(jnp.minimum(a, b), jnp.minimum(jnp.maximum(a, b), 0.0))


def shift_columns(parts, amount):
    lane = lax.broadcasted_iota(jnp.int32, parts[0].shape, 1)
    rolled = [pltpu.roll(part, amount % LANES, 1) for part in parts]
    count = len(parts)
    if amount > 0:
        return [jnp.where(lane < amount, rolled[i - 1], rolled[i]) for i in range(count)]
    return [jnp.where(lane >= LANES + amount, rolled[(i + 1) % count], rolled[i]) for i in range(count)]


def transport_kernel(z, x_ref, east_ref, north_ref, up_ref, low_ref, high_ref, out_ref, coef, first, second):
    span = z.rows + 2 * SUB

    def coef_row(kind, which, col, j):
        return ((kind * 2 + which) * z.columns + col) * span + j

    for kind, ref in enumerate((east_ref, north_ref, up_ref)):
        for level in range(z.levels):
            for piece in range(span // SUB):
                values = []
                for tile in range(z.tiles):
                    col = level * z.tiles + tile
                    edge = (kind * z.columns + col) * SUB
                    if piece == 0:
                        value = low_ref[pl.ds(z.low_rows + edge, SUB), :]
                    elif piece == span // SUB - 1:
                        value = high_ref[pl.ds(z.high_rows + edge, SUB), :]
                    else:
                        value = ref[pl.ds(z.source_row(level, (piece - 1) * SUB, tile), SUB), :]
                    values.append(value)
                if kind == 1:
                    values = shift_columns(values, -1)
                for tile, value in enumerate(values):
                    col = level * z.tiles + tile
                    coef[pl.ds(coef_row(kind, 0, col, piece * SUB), SUB), :] = value
                    coef[pl.ds(coef_row(kind, 1, col, piece * SUB), SUB), :] = 0.5 * value * (1.0 - value)

    def weights(kind, col, j):
        return [
            jnp.broadcast_to(coef[pl.ds(coef_row(kind, which, col, j), 1), :], (SUB, LANES))
            for which in range(2)
        ]

    def one_tile(index, carry):
        start = pl.multiple_of(index * SUB, SUB)

        def place(j, col):
            return pl.ds((j * z.columns + col) * SUB, SUB)

        def initial(j, col):
            level, tile = divmod(col, z.tiles)
            row = j - SUB
            if row < 0:
                base = ((row + LOW) * z.columns + col) * z.species
                return low_ref[pl.ds(pl.multiple_of(base + start, SUB), SUB), :]
            if row >= z.rows:
                base = ((row - z.rows) * z.columns + col) * z.species
                return high_ref[pl.ds(pl.multiple_of(base + start, SUB), SUB), :]
            return x_ref[pl.ds(start * z.stride + z.source_row(level, row, tile), SUB, stride=z.stride), :]

        cols = range(z.columns)
        for step in range(SECTIONS):
            bottom = SUB - LOW + 2 * step
            top = SUB + z.rows + HIGH - step
            if step == 0:
                read = initial
            else:
                source = (first, second)[(step + 1) % 2]
                read = lambda j, col, source=source: source[place(j, col), :]
            here = [read(bottom + 1, col) for col in cols]
            below = [read(bottom, col) for col in cols]
            rise = [here[col] - below[col] for col in cols]
            into = None
            for j in range(bottom + 1, top - 1):
                above = [read(j + 1, col) for col in cols]
                climb = [above[col] - here[col] for col in cols]
                out = []
                for col in cols:
                    a, b = weights(0, col, j + 1)
                    out.append(a * here[col] + b * middle(rise[col], climb[col]))
                if into is not None:
                    c = [here[col] - (out[col] - into[col]) for col in cols]
                    for level in range(z.levels):
                        mine = slice(level * z.tiles, (level + 1) * z.tiles)
                        row = c[mine]
                        back = [v - w for v, w in zip(row, shift_columns(row, 1))]
                        ahead = shift_columns(back, -1)
                        leave = []
                        for tile in range(z.tiles):
                            a, b = weights(1, level * z.tiles + tile, j)
                            leave.append(a * row[tile] + b * middle(back[tile], ahead[tile]))
                        enter = shift_columns(leave, 1)
                        c[mine] = [row[t] - (leave[t] - enter[t]) for t in range(z.tiles)]
                    for tile in range(z.tiles):
                        column = [c[level * z.tiles + tile] for level in range(z.levels)]
                        steps = [column[0]]
                        steps += [column[k + 1] - column[k] for k in range(z.levels - 1)]
                        steps += [-column[-1]]
                        lift = None
                        for level in range(z.levels):
                            col = level * z.tiles + tile
                            a, b = weights(2, col, j)
                            rising = a * column[level] + b * middle(steps[level], steps[level + 1])
                            net = rising if lift is None else rising - lift
                            lift = rising
                            value = column[level] - net
                            if step < SECTIONS - 1:
                                (first, second)[step % 2][place(j, col), :] = value
                            else:
                                group, part_row = divmod(j - SUB, z.part)
                                target = (level * z.tiles + tile) * z.part + part_row
                                base = (group * z.species + start) * z.blocks + target
                                out_ref[pl.ds(base, SUB, stride=z.blocks), :] = value
                into = out
                rise = climb
                here = above
        return carry

    lax.fori_loop(0, z.species // SUB, one_tile, 0)


def chemistry_kernel(
    species, blocks, c_ref, warm_ref, glow_ref, lit_ref, rate_ref, barrier_ref, photo_ref, table_ref,
    out_ref, made_a, made_b, lost_a, lost_b, lost_c, lost_d,
):
    pieces = blocks // SUB
    reactions = rate_ref.shape[0]
    made = (made_a, made_b)
    lost = ((lost_a, lost_b), (lost_c, lost_d))

    def cell(index, piece):
        return pl.ds(pl.multiple_of(index * blocks, SUB) + piece * SUB, SUB)

    lit = [lit_ref[pl.ds(piece * SUB, SUB), :] == 1 for piece in range(pieces)]
    warm = [warm_ref[pl.ds(piece * SUB, SUB), :] - 1.0 for piece in range(pieces)]
    glow = [jnp.where(lit[p], glow_ref[pl.ds(p * SUB, SUB), :], 0.0) for p in range(pieces)]

    for sub in range(DAY_STEPS):
        source = c_ref if sub == 0 else out_ref
        steps = [jnp.where(lit[p], float(DAY_STEPS), 1.0) for p in range(pieces)]

        def begin(s, carry):
            for p in range(pieces):
                made[0][cell(s, p), :] = steps[p] * source[cell(s, p), :]
                made[1][cell(s, p), :] = jnp.zeros((SUB, LANES), jnp.float32)
                for k in range(2):
                    for side in range(2):
                        fill = steps[p] if k == 0 and side == 0 else jnp.zeros((SUB, LANES), jnp.float32)
                        lost[k][side][cell(s, p), :] = fill
            return carry

        lax.fori_loop(0, species, begin, 0, unroll=4)

        def react(r, parity):
            first, second, product = table_ref[0, r], table_ref[1, r], table_ref[2, r]
            rate, barrier, photo = rate_ref[r], barrier_ref[r], photo_ref[r]
            for p in range(pieces):
                k = rate * jnp.exp(-barrier * warm[p]) + photo * glow[p]
                x = source[cell(first, p), :]
                y = source[cell(second, p), :]
                kx = k * x
                ky = k * y
                made[parity][cell(product, p), :] += kx * y
                lost[parity][0][cell(first, p), :] += ky
                lost[parity][1][cell(second, p), :] += kx

        def two(i, carry):
            react(2 * i, 0)
            react(2 * i + 1, 1)
            return carry

        lax.fori_loop(0, reactions // 2, two, 0, unroll=4)

        def finish(s, carry):
            for p in range(pieces):
                at = cell(s, p)
                top = made[0][at, :] + made[1][at, :]
                bottom = (lost[0][0][at, :] + lost[0][1][at, :]) + (lost[1][0][at, :] + lost[1][1][at, :])
                value = top / bottom
                if sub > 0:
                    value = jnp.where(lit[p], value, source[at, :])
                out_ref[at, :] = value
            return carry

        lax.fori_loop(0, species, finish, 0, unroll=4)


VMEM = pl.BlockSpec(memory_space=pltpu.VMEM)
SMEM = pl.BlockSpec(memory_space=pltpu.SMEM)


def rows_of(count):
    return jax.ShapeDtypeStruct((count, LANES), jnp.float32)


def pack(z, *flat):
    return pl.pallas_call(
        functools.partial(pack_kernel, z),
        out_shape=(rows_of(z.low_rows + z.edge_rows), rows_of(z.high_rows + z.edge_rows)),
        in_specs=[VMEM] * 4,
        out_specs=(VMEM, VMEM),
        name="pack",
    )(*flat)


def transport(z, *flat):
    span = z.rows + 2 * SUB
    return pl.pallas_call(
        functools.partial(transport_kernel, z),
        out_shape=rows_of(z.groups * z.species * z.blocks),
        in_specs=[VMEM] * 6,
        out_specs=VMEM,
        scratch_shapes=[
            pltpu.VMEM((6 * z.columns * span, LANES), jnp.float32),
            pltpu.VMEM((span * z.columns * SUB, LANES), jnp.float32),
            pltpu.VMEM((span * z.columns * SUB, LANES), jnp.float32),
        ],
        name="transport",
    )(*flat)


def chemistry(species, blocks, *args):
    size = (species * blocks, LANES)
    return pl.pallas_call(
        functools.partial(chemistry_kernel, species, blocks),
        out_shape=rows_of(species * blocks),
        in_specs=[VMEM] * 4 + [SMEM] * 4,
        out_specs=VMEM,
        scratch_shapes=[pltpu.VMEM(size, jnp.float32)] * 6,
        name="chemistry",
    )(*args)


def body(
    mixing_ratio_field,
    eastward_face_cfl,
    northward_face_cfl,
    upward_face_cfl,
    thermal_anomaly,
    radiant_flux,
    daylight_mask,
    baseline_kinetic_coefficient,
    arrhenius_barrier,
    photodissociation_factor,
    stoichiometry_table,
):
    groups = lax.axis_size("tracer")
    strips = lax.axis_size("space")
    z = Sizes(mixing_ratio_field, groups)
    flat = [
        flat_rows(a)
        for a in (mixing_ratio_field, eastward_face_cfl, northward_face_cfl, upward_face_cfl)
    ]
    low, high = pack(z, *flat)
    low = lax.ppermute(low, "space", [(i, i + 1) for i in range(strips - 1)])
    high = lax.ppermute(high, "space", [(i + 1, i) for i in range(strips - 1)])
    moved = transport(z, *flat, low, high)
    moved = moved.reshape(groups, z.species * z.blocks, LANES)
    moved = lax.all_to_all(moved, "tracer", split_axis=0, concat_axis=0, tiled=True)
    species = z.species * groups
    lit = jnp.moveaxis(daylight_mask, 2, 1).reshape(z.blocks, 1)
    lit = jnp.broadcast_to(lit, (z.blocks, LANES))
    out = chemistry(
        species,
        z.blocks,
        moved.reshape(species * z.blocks, LANES),
        flat_rows(thermal_anomaly),
        flat_rows(radiant_flux),
        lit,
        baseline_kinetic_coefficient,
        arrhenius_barrier,
        photodissociation_factor,
        stoichiometry_table,
    )
    out = out.reshape(species, z.levels, z.tiles, z.part, LANES)
    return jnp.moveaxis(out, 2, 3).reshape(species, z.levels, z.part, z.width)


def solution(mesh):
    placed = (
        P("tracer", None, "space", None),
        P(None, "space", None),
        P(None, "space", None),
        P(None, "space", None),
        P(None, ("space", "tracer"), None),
        P(None, ("space", "tracer"), None),
        P(None, ("space", "tracer"), None),
        P(),
        P(),
        P(),
        P(),
    )
    return jax.shard_map(
        body,
        mesh=mesh,
        in_specs=placed,
        out_specs=P(None, None, ("space", "tracer"), None),
        check_vma=False,
    )
```

profile of v0, /device:TPU:16, one launch (start us, length us, event | category | flops | bytes accessed | tf_op | source)
XLA Modules:
  0.0 128.5 jit_solution(9723526856558682704)
XLA Ops:
  0.0 3.3 %pack.1 = (f32[1632,128]{1,0:T(8,128)}, f32[864,128]{1,0:T(8,128)}) custom-call(f32[4096,128]{1,0:T(8,128)} %bitcast.38, f32[64,128]{1,0:T(8,128)} %bitcast.42, f32[64,128]{1,0:T(8,128)} %bitcast.44, f32[64,128]{1,0:T(8,128)} %bitcast.46), custom_call_target="tpu_custom_call" | custom-call | tf_op jit(solution)/shard_map/pack/pallas_call | solution.py:261
  3.3 1.9 %collective-permute-start = (f32[1632,128]{1,0:T(8,128)}, f32[1632,128]{1,0:T(8,128)S(1)}, u32[]{:S(2)}, u32[]{:S(2)}) collective-permute-start(f32[1632,128]{1,0:T(8,128)} %get-tuple-element.7), channel_id=1, source_target_pairs={{0,4},{4,8},{8,12},{12,16},{16,20},{20,24},{24,28},{1,5},{5,9},{9,... | collective-permute-start | bytes 2506760 | tf_op jit(solution)/shard_map/ppermute | solution.py:319
  5.2 3.6 %collective-permute-start.1 = (f32[864,128]{1,0:T(8,128)}, f32[864,128]{1,0:T(8,128)S(1)}, u32[]{:S(2)}, u32[]{:S(2)}) collective-permute-start(f32[864,128]{1,0:T(8,128)} %get-tuple-element.8), channel_id=1, source_target_pairs={{4,0},{8,4},{12,8},{16,12},{20,16},{24,20},{28,24},{5,1},{9,5},{13... | collective-permute-start | bytes 1327112 | tf_op jit(solution)/shard_map/ppermute | solution.py:320
  8.9 6.1 %collective-permute-done.1.high_ref = f32[864,128]{1,0:T(8,128)S(1)} collective-permute-done((f32[864,128]{1,0:T(8,128)}, f32[864,128]{1,0:T(8,128)S(1)}, u32[]{:S(2)}, u32[]{:S(2)}) %collective-permute-start.1) | collective-permute-done | bytes 442400 | tf_op jit(solution)/shard_map/ppermute | solution.py:320
  15.0 0.0 copy-start.2
  15.0 2.4 %collective-permute-done.low_ref = f32[1632,128]{1,0:T(8,128)S(1)} collective-permute-done((f32[1632,128]{1,0:T(8,128)}, f32[1632,128]{1,0:T(8,128)S(1)}, u32[]{:S(2)}, u32[]{:S(2)}) %collective-permute-start) | collective-permute-done | bytes 835616 | tf_op jit(solution)/shard_map/ppermute | solution.py:319
  17.3 0.0 copy-done.2
  17.4 0.0 copy-start.1
  17.4 0.9 copy-done.1
  18.3 60.2 %transport.1 = f32[4096,128]{1,0:T(8,128)} custom-call(f32[4096,128]{1,0:T(8,128)} %bitcast.39, f32[64,128]{1,0:T(8,128)} %bitcast.43, f32[64,128]{1,0:T(8,128)} %bitcast.45, f32[64,128]{1,0:T(8,128)} %bitcast.47, f32[1632,128]{1,0:T(8,128)} %copy-done.1, f32[864,128]{1,0:T(8,128)} %copy-done.2), custom_call_target="tpu_custom_call" | custom-call | tf_op jit(solution)/shard_map/transport/pallas_call | solution.py:272
  78.4 0.0 copy-start.3
  78.4 3.8 %all-to-all-start = ((f32[4,1024,128]{2,1,0:T(8,128)}), f32[4,1024,128]{2,1,0:T(8,128)S(1)}, u32[]{:S(2)}, u32[]{:S(2)}) async-start(f32[4,1024,128]{2,1,0:T(8,128)} %bitcast.41), calls=%async_computation | async-start | bytes 4194304 | tf_op jit(solution)/shard_map/all_to_all | solution.py:323
  82.3 0.0 copy-done.3
  82.3 0.1 broadcast_in_dim.7
  82.4 25.6 %all-to-all-done = f32[4,1024,128]{2,1,0:T(8,128)S(1)} async-done(((f32[4,1024,128]{2,1,0:T(8,128)}), f32[4,1024,128]{2,1,0:T(8,128)S(1)}, u32[]{:S(2)}, u32[]{:S(2)}) %all-to-all-start) | async-done | bytes 2097184 | tf_op jit(solution)/shard_map/all_to_all | solution.py:323
  107.9 0.0 copy-start
  107.9 0.7 broadcast_in_dim.8.lit_ref
  108.7 0.6 copy-done
  109.3 19.3 %chemistry.1 = f32[4096,128]{1,0:T(8,128)} custom-call(f32[4096,128]{1,0:T(8,128)} %bitcast.40, f32[16,128]{1,0:T(8,128)} %bitcast.48, f32[16,128]{1,0:T(8,128)} %bitcast.49, s32[16,128]{1,0:T(8,128)} %broadcast_in_dim.8.lit_ref, f32[768]{0:T(1024)} %rate_ref.1, f32[768]{0:T(1024)} %barrier_ref.1, f32[768]{0:T(1024)} %photo_ref.1, s32[3,768]{1,0:T(4,128)} %table_ref.1), custom_call_target="tpu_custom_call" | custom-call | tf_op jit(solution)/shard_map/chemistry/pallas_call | solution.py:288
Async XLA Ops:
  3.3 14.0 %collective-permute-start = (f32[1632,128]{1,0:T(8,128)}, f32[1632,128]{1,0:T(8,128)S(1)}, u32[]{:S(2)}, u32[]{:S(2)}) collective-permute-start(f32[1632,128]{1,0:T(8,128)} %get-tuple-element.7), channel_id=1, source_target_pairs={{0,4},{4,8},{8,12},{12,16},{16,20},{20,24},{24,28},{1,5},{5,9},{9,... | collective-permute-start | bytes 2506760 | tf_op jit(solution)/shard_map/ppermute | solution.py:319
  5.2 9.8 %collective-permute-start.1 = (f32[864,128]{1,0:T(8,128)}, f32[864,128]{1,0:T(8,128)S(1)}, u32[]{:S(2)}, u32[]{:S(2)}) collective-permute-start(f32[864,128]{1,0:T(8,128)} %get-tuple-element.8), channel_id=1, source_target_pairs={{4,0},{8,4},{12,8},{16,12},{20,16},{24,20},{28,24},{5,1},{9,5},{13... | collective-permute-start | bytes 1327112 | tf_op jit(solution)/shard_map/ppermute | solution.py:320
  15.0 2.4 %copy-start.2 = (f32[864,128]{1,0:T(8,128)}, f32[864,128]{1,0:T(8,128)S(1)}, u32[]{:S(2)}) copy-start(f32[864,128]{1,0:T(8,128)S(1)} %collective-permute-done.1.high_ref) | copy-start | bytes 1327108
  17.4 0.9 copy-start.1
  78.4 3.9 %copy-start.3 = (s32[2,4,2]{1,2,0:T(2,128)S(1)}, s32[2,4,2]{1,2,0:T(2,128)}, u32[]{:S(2)}) copy-start(s32[2,4,2]{1,2,0:T(2,128)} %param.17) | copy-start | bytes 196
  78.4 29.5 %all-to-all-start = ((f32[4,1024,128]{2,1,0:T(8,128)}), f32[4,1024,128]{2,1,0:T(8,128)S(1)}, u32[]{:S(2)}, u32[]{:S(2)}) async-start(f32[4,1024,128]{2,1,0:T(8,128)} %bitcast.41), calls=%async_computation | async-start | bytes 4194304 | tf_op jit(solution)/shard_map/all_to_all | solution.py:323
  107.9 1.3 %copy-start = (f32[4,1024,128]{2,1,0:T(8,128)}, f32[4,1024,128]{2,1,0:T(8,128)S(1)}, u32[]{:S(2)}) copy-start(f32[4,1024,128]{2,1,0:T(8,128)S(1)} %all-to-all-done) | copy-start | bytes 6291460
where the time goes:
time: 129 us
  Pallas kernels  82.7 us (64%)
  waiting for transfers between devices  34 us (26%)
  starting transfers between devices  9.4 us (7%)
  local copies, waits for them, and re-layouts  2.34 us (2%)
    pallas_call x1, Pallas kernels, transport(): pl.pallas_call(functools.partial(transport_kernel, z), out_shape=rows_of(...  60.2 us
    all_to_all x1, waiting for transfers between devices, body(): lax.all_to_all(moved, 'tracer', split_axis=0, concat_axis=0, tiled=True)  25.6 us
    pallas_call x1, Pallas kernels, chemistry(): pl.pallas_call(functools.partial(chemistry_kernel, species, blocks), out_...  19.3 us
    ppermute x1, waiting for transfers between devices, body(): high = lax.ppermute(high, 'space', [(i + 1, i) for i in range(strips - 1)])  6.12 us
    all_to_all x1, starting transfers between devices, body(): lax.all_to_all(moved, 'tracer', split_axis=0, concat_axis=0, tiled=True)  3.85 us
    ppermute x1, starting transfers between devices, body(): high = lax.ppermute(high, 'space', [(i + 1, i) for i in range(strips - 1)])  3.64 us
    pallas_call x1, Pallas kernels, pack(): pl.pallas_call(functools.partial(pack_kernel, z), out_shape=(rows_of(z.lo...  3.31 us
  transfers between devices with their start and end apart: 3, of which 3 were waited for; matrix products, arithmetic and copies ran while one was open for 0% of the time, Pallas kernels for 0%

commit v1 on v0

--- a/solution.py
+++ b/solution.py
@@ -13,6 +13,7 @@
 SUB = 8
 LOW = 2 * SECTIONS
 HIGH = SECTIONS
+TOGETHER = 2
 
 
 def flat_rows(cells):
@@ -43,13 +44,15 @@
 
 
 def pack_kernel(z, x_ref, east_ref, north_ref, up_ref, low_ref, high_ref):
-    for offset, rows, out_ref in ((z.rows - LOW, LOW, low_ref), (0, HIGH, high_ref)):
-        for row in range(rows):
+    def one_species(index, carry):
+        for offset, rows, out_ref in ((z.rows - LOW, LOW, low_ref), (0, HIGH, high_ref)):
             for col, (level, tile) in enumerate(z.pairs()):
-                for start in range(0, z.species, SUB):
-                    source = start * z.stride + z.source_row(level, row + offset, tile)
-                    target = (row * z.columns + col) * z.species + start
-                    out_ref[pl.ds(target, SUB), :] = x_ref[pl.ds(source, SUB, stride=z.stride), :]
+                source = index * z.stride + z.source_row(level, offset, tile)
+                target = (index * z.columns + col) * rows
+                out_ref[pl.ds(target, rows), :] = x_ref[pl.ds(source, rows), :]
+        return carry
+
+    lax.fori_loop(0, z.species, one_species, 0, unroll=4)
     for out_ref, base, last in ((low_ref, z.low_rows, True), (high_ref, z.high_rows, False)):
         row = z.rows - SUB if last else 0
         for kind, ref in enumerate((east_ref, north_ref, up_ref)):
@@ -72,7 +75,7 @@
     return [jnp.where(lane >= LANES + amount, rolled[(i + 1) % count], rolled[i]) for i in range(count)]
 
 
-def transport_kernel(z, x_ref, east_ref, north_ref, up_ref, low_ref, high_ref, out_ref, coef, first, second):
+def transport_kernel(z, x_ref, east_ref, north_ref, up_ref, low_ref, high_ref, out_ref, coef, *scratch):
     span = z.rows + 2 * SUB
 
     def coef_row(kind, which, col, j):
@@ -100,87 +103,71 @@
                     coef[pl.ds(coef_row(kind, 1, col, piece * SUB), SUB), :] = 0.5 * value * (1.0 - value)
 
     def weights(kind, col, j):
-        return [
-            jnp.broadcast_to(coef[pl.ds(coef_row(kind, which, col, j), 1), :], (SUB, LANES))
-            for which in range(2)
-        ]
-
-    def one_tile(index, carry):
-        start = pl.multiple_of(index * SUB, SUB)
-
-        def place(j, col):
-            return pl.ds((j * z.columns + col) * SUB, SUB)
-
-        def initial(j, col):
-            level, tile = divmod(col, z.tiles)
-            row = j - SUB
-            if row < 0:
-                base = ((row + LOW) * z.columns + col) * z.species
-                return low_ref[pl.ds(pl.multiple_of(base + start, SUB), SUB), :]
-            if row >= z.rows:
-                base = ((row - z.rows) * z.columns + col) * z.species
-                return high_ref[pl.ds(pl.multiple_of(base + start, SUB), SUB), :]
-            return x_ref[pl.ds(start * z.stride + z.source_row(level, row, tile), SUB, stride=z.stride), :]
-
-        cols = range(z.columns)
+        return [coef[pl.ds(coef_row(kind, which, col, j), SUB), :] for which in range(2)]
+
+    cols = range(z.columns)
+
+    def one_species(index, fields, fluxes):
+        for col, (level, tile) in enumerate(z.pairs()):
+            base = index * z.columns + col
+            fields[0][pl.ds(col * span + SUB - LOW, LOW), :] = low_ref[pl.ds(base * LOW, LOW), :]
+            fields[0][pl.ds(col * span + SUB + z.rows, HIGH), :] = high_ref[pl.ds(base * HIGH, HIGH), :]
+            for row in range(0, z.rows, SUB):
+                source = index * z.stride + z.source_row(level, row, tile)
+                fields[0][pl.ds(col * span + SUB + row, SUB), :] = x_ref[pl.ds(pl.multiple_of(source, SUB), SUB), :]
         for step in range(SECTIONS):
-            bottom = SUB - LOW + 2 * step
-            top = SUB + z.rows + HIGH - step
-            if step == 0:
-                read = initial
-            else:
-                source = (first, second)[(step + 1) % 2]
-                read = lambda j, col, source=source: source[place(j, col), :]
-            here = [read(bottom + 1, col) for col in cols]
-            below = [read(bottom, col) for col in cols]
-            rise = [here[col] - below[col] for col in cols]
-            into = None
-            for j in range(bottom + 1, top - 1):
-                above = [read(j + 1, col) for col in cols]
-                climb = [above[col] - here[col] for col in cols]
-                out = []
+            read, write = fields[step % 2], fields[(step + 1) % 2]
+            bottom = SUB - LOW + 2 * (step + 1)
+            top = SUB + z.rows + HIGH - (step + 1)
+            for j in range(bottom - 1, top, SUB):
                 for col in cols:
+                    below, here, above = [read[pl.ds(col * span + j + k, SUB), :] for k in (-1, 0, 1)]
                     a, b = weights(0, col, j + 1)
-                    out.append(a * here[col] + b * middle(rise[col], climb[col]))
-                if into is not None:
-                    c = [here[col] - (out[col] - into[col]) for col in cols]
+                    fluxes[pl.ds(col * span + j, SUB), :] = a * here + b * middle(here - below, above - here)
+            for j in range(bottom, top, SUB):
+                c = []
+                for col in cols:
+                    leave = fluxes[pl.ds(col * span + j, SUB), :]
+                    enter = fluxes[pl.ds(col * span + j - 1, SUB), :]
+                    c.append(read[pl.ds(col * span + j, SUB), :] - (leave - enter))
+                for level in range(z.levels):
+                    mine = slice(level * z.tiles, (level + 1) * z.tiles)
+                    row = c[mine]
+                    back = [v - w for v, w in zip(row, shift_columns(row, 1))]
+                    ahead = shift_columns(back, -1)
+                    leave = []
+                    for tile in range(z.tiles):
+                        a, b = weights(1, level * z.tiles + tile, j)
+                        leave.append(a * row[tile] + b * middle(back[tile], ahead[tile]))
+                    enter = shift_columns(leave, 1)
+                    c[mine] = [row[t] - (leave[t] - enter[t]) for t in range(z.tiles)]
+                for tile in range(z.tiles):
+                    column = [c[level * z.tiles + tile] for level in range(z.levels)]
+                    steps = [column[0]]
+                    steps += [column[k + 1] - column[k] for k in range(z.levels - 1)]
+                    steps += [-column[-1]]
+                    lift = None
                     for level in range(z.levels):
-                        mine = slice(level * z.tiles, (level + 1) * z.tiles)
-                        row = c[mine]
-                        back = [v - w for v, w in zip(row, shift_columns(row, 1))]
-                        ahead = shift_columns(back, -1)
-                        leave = []
-                        for tile in range(z.tiles):
-                            a, b = weights(1, level * z.tiles + tile, j)
-                            leave.append(a * row[tile] + b * middle(back[tile], ahead[tile]))
-                        enter = shift_columns(leave, 1)
-                        c[mine] = [row[t] - (leave[t] - enter[t]) for t in range(z.tiles)]
-                    for tile in range(z.tiles):
-                        column = [c[level * z.tiles + tile] for level in range(z.levels)]
-                        steps = [column[0]]
-                        steps += [column[k + 1] - column[k] for k in range(z.levels - 1)]
-                        steps += [-column[-1]]
-                        lift = None
-                        for level in range(z.levels):
-                            col = level * z.tiles + tile
-                            a, b = weights(2, col, j)
-                            rising = a * column[level] + b * middle(steps[level], steps[level + 1])
-                            net = rising if lift is None else rising - lift
-                            lift = rising
-                            value = column[level] - net
-                            if step < SECTIONS - 1:
-                                (first, second)[step % 2][place(j, col), :] = value
-                            else:
-                                group, part_row = divmod(j - SUB, z.part)
-                                target = (level * z.tiles + tile) * z.part + part_row
-                                base = (group * z.species + start) * z.blocks + target
-                                out_ref[pl.ds(base, SUB, stride=z.blocks), :] = value
-                into = out
-                rise = climb
-                here = above
+                        col = level * z.tiles + tile
+                        a, b = weights(2, col, j)
+                        rising = a * column[level] + b * middle(steps[level], steps[level + 1])
+                        net = rising if lift is None else rising - lift
+                        lift = rising
+                        value = column[level] - net
+                        if step < SECTIONS - 1:
+                            write[pl.ds(col * span + j, SUB), :] = value
+                            continue
+                        for start in range(0, SUB, z.part):
+                            group = (j - SUB + start) // z.part
+                            base = (group * z.species + index) * z.blocks + col * z.part
+                            out_ref[pl.ds(base, z.part), :] = value[start : start + z.part]
+
+    def some_species(index, carry):
+        for k in range(TOGETHER):
+            one_species(index * TOGETHER + k, scratch[3 * k : 3 * k + 2], scratch[3 * k + 2])
         return carry
 
-    lax.fori_loop(0, z.species // SUB, one_tile, 0)
+    lax.fori_loop(0, z.species // TOGETHER, some_species, 0)
 
 
 def chemistry_kernel(
@@ -276,9 +263,8 @@
         out_specs=VMEM,
         scratch_shapes=[
             pltpu.VMEM((6 * z.columns * span, LANES), jnp.float32),
-            pltpu.VMEM((span * z.columns * SUB, LANES), jnp.float32),
-            pltpu.VMEM((span * z.columns * SUB, LANES), jnp.float32),
-        ],
+        ]
+        + [pltpu.VMEM((span * z.columns, LANES), jnp.float32)] * (3 * TOGETHER),
         name="transport",
     )(*flat)
 

time: 129 us -> 99.8 us (0.77)
  Pallas kernels: 82.7 us -> 53.7 us
    pallas_call x1, Pallas kernels: 60.2 us -> 31.6 us  [transport(): pl.pallas_call(functools.partial(transport_kernel, z), out_shape=rows_of(...]
where the time goes in v1:
time: 99.8 us; the launch traced here: 99.5 us
  Pallas kernels  53.7 us (54%)
  waiting for transfers between devices  34 us (34%)
  starting transfers between devices  9.4 us (9%)
  local copies, waits for them, and re-layouts  2.34 us (2%)
    pallas_call x1, Pallas kernels, transport(): pl.pallas_call(functools.partial(transport_kernel, z), out_shape=rows_of(...  31.6 us
    all_to_all x1, waiting for transfers between devices, body(): lax.all_to_all(moved, 'tracer', split_axis=0, concat_axis=0, tiled=True)  25.6 us
    pallas_call x1, Pallas kernels, chemistry(): pl.pallas_call(functools.partial(chemistry_kernel, species, blocks), out_...  19.3 us
    ppermute x1, waiting for transfers between devices, body(): high = lax.ppermute(high, 'space', [(i + 1, i) for i in range(strips - 1)])  6.12 us
    all_to_all x1, starting transfers between devices, body(): lax.all_to_all(moved, 'tracer', split_axis=0, concat_axis=0, tiled=True)  3.85 us
    ppermute x1, starting transfers between devices, body(): high = lax.ppermute(high, 'space', [(i + 1, i) for i in range(strips - 1)])  3.64 us
    pallas_call x1, Pallas kernels, pack(): pl.pallas_call(functools.partial(pack_kernel, z), out_shape=(rows_of(z.lo...  2.9 us
    ppermute x1, waiting for transfers between devices, body(): low = lax.ppermute(low, 'space', [(i, i + 1) for i in range(strips - 1)])  2.35 us
  transfers between devices with their start and end apart: 3, of which 3 were waited for; matrix products, arithmetic and copies ran while one was open for 0% of the time, Pallas kernels for 0%

profile of v1, /device:TPU:16, one launch (start us, length us, event | category | flops | bytes accessed | tf_op | source)
XLA Modules:
  0.0 99.5 jit_solution(10175285625892756912)
XLA Ops:
  0.0 2.9 %pack.1 = (f32[1632,128]{1,0:T(8,128)}, f32[864,128]{1,0:T(8,128)}) custom-call(f32[4096,128]{1,0:T(8,128)} %bitcast.38, f32[64,128]{1,0:T(8,128)} %bitcast.42, f32[64,128]{1,0:T(8,128)} %bitcast.44, f32[64,128]{1,0:T(8,128)} %bitcast.46), custom_call_target="tpu_custom_call" | custom-call | tf_op jit(solution)/shard_map/pack/pallas_call | solution.py:248
  2.9 1.9 %collective-permute-start = (f32[1632,128]{1,0:T(8,128)}, f32[1632,128]{1,0:T(8,128)S(1)}, u32[]{:S(2)}, u32[]{:S(2)}) collective-permute-start(f32[1632,128]{1,0:T(8,128)} %get-tuple-element.7), channel_id=1, source_target_pairs={{0,4},{4,8},{8,12},{12,16},{16,20},{20,24},{24,28},{1,5},{5,9},{9,... | collective-permute-start | bytes 2506760 | tf_op jit(solution)/shard_map/ppermute | solution.py:305
  4.8 3.6 %collective-permute-start.1 = (f32[864,128]{1,0:T(8,128)}, f32[864,128]{1,0:T(8,128)S(1)}, u32[]{:S(2)}, u32[]{:S(2)}) collective-permute-start(f32[864,128]{1,0:T(8,128)} %get-tuple-element.8), channel_id=1, source_target_pairs={{4,0},{8,4},{12,8},{16,12},{20,16},{24,20},{28,24},{5,1},{9,5},{13... | collective-permute-start | bytes 1327112 | tf_op jit(solution)/shard_map/ppermute | solution.py:306
  8.5 6.1 %collective-permute-done.1.high_ref = f32[864,128]{1,0:T(8,128)S(1)} collective-permute-done((f32[864,128]{1,0:T(8,128)}, f32[864,128]{1,0:T(8,128)S(1)}, u32[]{:S(2)}, u32[]{:S(2)}) %collective-permute-start.1) | collective-permute-done | bytes 442400 | tf_op jit(solution)/shard_map/ppermute | solution.py:306
  14.6 0.0 copy-start.2
  14.6 2.4 %collective-permute-done.low_ref = f32[1632,128]{1,0:T(8,128)S(1)} collective-permute-done((f32[1632,128]{1,0:T(8,128)}, f32[1632,128]{1,0:T(8,128)S(1)}, u32[]{:S(2)}, u32[]{:S(2)}) %collective-permute-start) | collective-permute-done | bytes 835616 | tf_op jit(solution)/shard_map/ppermute | solution.py:305
  16.9 0.0 copy-done.2
  16.9 0.0 copy-start.1
  16.9 0.9 copy-done.1
  17.8 31.6 %transport.1 = f32[4096,128]{1,0:T(8,128)} custom-call(f32[4096,128]{1,0:T(8,128)} %bitcast.39, f32[64,128]{1,0:T(8,128)} %bitcast.43, f32[64,128]{1,0:T(8,128)} %bitcast.45, f32[64,128]{1,0:T(8,128)} %bitcast.47, f32[1632,128]{1,0:T(8,128)} %copy-done.1, f32[864,128]{1,0:T(8,128)} %copy-done.2), custom_call_target="tpu_custom_call" | custom-call | tf_op jit(solution)/shard_map/transport/pallas_call | solution.py:259
  49.4 0.0 copy-start.3
  49.4 3.8 %all-to-all-start = ((f32[4,1024,128]{2,1,0:T(8,128)}), f32[4,1024,128]{2,1,0:T(8,128)S(1)}, u32[]{:S(2)}, u32[]{:S(2)}) async-start(f32[4,1024,128]{2,1,0:T(8,128)} %bitcast.41), calls=%async_computation | async-start | bytes 4194304 | tf_op jit(solution)/shard_map/all_to_all | solution.py:309
  53.3 0.0 copy-done.3
  53.3 0.1 broadcast_in_dim.7
  53.4 25.6 %all-to-all-done = f32[4,1024,128]{2,1,0:T(8,128)S(1)} async-done(((f32[4,1024,128]{2,1,0:T(8,128)}), f32[4,1024,128]{2,1,0:T(8,128)S(1)}, u32[]{:S(2)}, u32[]{:S(2)}) %all-to-all-start) | async-done | bytes 2097184 | tf_op jit(solution)/shard_map/all_to_all | solution.py:309
  78.9 0.0 copy-start
  78.9 0.7 broadcast_in_dim.8.lit_ref
  79.7 0.6 copy-done
  80.2 19.3 %chemistry.1 = f32[4096,128]{1,0:T(8,128)} custom-call(f32[4096,128]{1,0:T(8,128)} %bitcast.40, f32[16,128]{1,0:T(8,128)} %bitcast.48, f32[16,128]{1,0:T(8,128)} %bitcast.49, s32[16,128]{1,0:T(8,128)} %broadcast_in_dim.8.lit_ref, f32[768]{0:T(1024)} %rate_ref.1, f32[768]{0:T(1024)} %barrier_ref.1, f32[768]{0:T(1024)} %photo_ref.1, s32[3,768]{1,0:T(4,128)} %table_ref.1), custom_call_target="tpu_custom_call" | custom-call | tf_op jit(solution)/shard_map/chemistry/pallas_call | solution.py:274
Async XLA Ops:
  2.9 14.0 %collective-permute-start = (f32[1632,128]{1,0:T(8,128)}, f32[1632,128]{1,0:T(8,128)S(1)}, u32[]{:S(2)}, u32[]{:S(2)}) collective-permute-start(f32[1632,128]{1,0:T(8,128)} %get-tuple-element.7), channel_id=1, source_target_pairs={{0,4},{4,8},{8,12},{12,16},{16,20},{20,24},{24,28},{1,5},{5,9},{9,... | collective-permute-start | bytes 2506760 | tf_op jit(solution)/shard_map/ppermute | solution.py:305
  4.8 9.8 %collective-permute-start.1 = (f32[864,128]{1,0:T(8,128)}, f32[864,128]{1,0:T(8,128)S(1)}, u32[]{:S(2)}, u32[]{:S(2)}) collective-permute-start(f32[864,128]{1,0:T(8,128)} %get-tuple-element.8), channel_id=1, source_target_pairs={{4,0},{8,4},{12,8},{16,12},{20,16},{24,20},{28,24},{5,1},{9,5},{13... | collective-permute-start | bytes 1327112 | tf_op jit(solution)/shard_map/ppermute | solution.py:306
  14.6 2.4 %copy-start.2 = (f32[864,128]{1,0:T(8,128)}, f32[864,128]{1,0:T(8,128)S(1)}, u32[]{:S(2)}) copy-start(f32[864,128]{1,0:T(8,128)S(1)} %collective-permute-done.1.high_ref) | copy-start | bytes 1327108
  16.9 0.9 copy-start.1
  49.4 3.9 %copy-start.3 = (s32[2,4,2]{1,2,0:T(2,128)S(1)}, s32[2,4,2]{1,2,0:T(2,128)}, u32[]{:S(2)}) copy-start(s32[2,4,2]{1,2,0:T(2,128)} %param.17) | copy-start | bytes 196
  49.4 29.5 %all-to-all-start = ((f32[4,1024,128]{2,1,0:T(8,128)}), f32[4,1024,128]{2,1,0:T(8,128)S(1)}, u32[]{:S(2)}, u32[]{:S(2)}) async-start(f32[4,1024,128]{2,1,0:T(8,128)} %bitcast.41), calls=%async_computation | async-start | bytes 4194304 | tf_op jit(solution)/shard_map/all_to_all | solution.py:309
  78.9 1.3 %copy-start = (f32[4,1024,128]{2,1,0:T(8,128)}, f32[4,1024,128]{2,1,0:T(8,128)S(1)}, u32[]{:S(2)}) copy-start(f32[4,1024,128]{2,1,0:T(8,128)S(1)} %all-to-all-done) | copy-start | bytes 6291460

commit v2 on v1

--- a/solution.py
+++ b/solution.py
@@ -14,6 +14,7 @@
 LOW = 2 * SECTIONS
 HIGH = SECTIONS
 TOGETHER = 2
+CHUNK = 8
 
 
 def flat_rows(cells):
@@ -34,6 +35,7 @@
         self.columns = self.levels * self.tiles
         self.low_rows = LOW * self.columns * self.species
         self.high_rows = HIGH * self.columns * self.species
+        self.span = self.rows + 2 * SUB
         self.edge_rows = 3 * self.columns * SUB
 
     def source_row(self, level, row, tile):
@@ -67,61 +69,95 @@
 
 
 def shift_columns(parts, amount):
-    lane = lax.broadcasted_iota(jnp.int32, parts[0].shape, 1)
-    rolled = [pltpu.roll(part, amount % LANES, 1) for part in parts]
-    count = len(parts)
     if amount > 0:
-        return [jnp.where(lane < amount, rolled[i - 1], rolled[i]) for i in range(count)]
-    return [jnp.where(lane >= LANES + amount, rolled[(i + 1) % count], rolled[i]) for i in range(count)]
-
-
-def transport_kernel(z, x_ref, east_ref, north_ref, up_ref, low_ref, high_ref, out_ref, coef, *scratch):
-    span = z.rows + 2 * SUB
+        return [pltpu.roll(parts[-1], 1, 1)] + parts[:-1]
+    return parts[1:] + [pltpu.roll(parts[0], LANES - 1, 1)]
+
+
+def spread_matrix(tiles, back):
+    natural = lax.broadcasted_iota(jnp.int32, (tiles * LANES, tiles * LANES), 1 if back else 0)
+    spread = lax.broadcasted_iota(jnp.int32, (tiles * LANES, tiles * LANES), 0 if back else 1)
+    hit = natural == (spread % LANES) * tiles + spread // LANES
+    return jnp.where(hit, 1.0, 0.0).astype(jnp.bfloat16)
+
+
+def reorder(parts, matrix):
+    x = jnp.concatenate(parts, axis=1)
+    total = None
+    for _ in range(3):
+        piece = x.astype(jnp.bfloat16)
+        x = x - piece.astype(jnp.float32)
+        term = jnp.dot(piece, matrix, preferred_element_type=jnp.float32)
+        total = term if total is None else total + term
+    return [total[:, k * LANES : (k + 1) * LANES] for k in range(len(parts))]
+
+
+def transport_kernel(
+    z, x_ref, east_ref, north_ref, up_ref, low_ref, high_ref, out_ref, coef, natural, strip, final, *scratch
+):
+    span = z.span
+    forth = spread_matrix(z.tiles, False)
 
     def coef_row(kind, which, col, j):
         return ((kind * 2 + which) * z.columns + col) * span + j
 
     for kind, ref in enumerate((east_ref, north_ref, up_ref)):
         for level in range(z.levels):
-            for piece in range(span // SUB):
-                values = []
-                for tile in range(z.tiles):
-                    col = level * z.tiles + tile
-                    edge = (kind * z.columns + col) * SUB
-                    if piece == 0:
-                        value = low_ref[pl.ds(z.low_rows + edge, SUB), :]
-                    elif piece == span // SUB - 1:
-                        value = high_ref[pl.ds(z.high_rows + edge, SUB), :]
-                    else:
-                        value = ref[pl.ds(z.source_row(level, (piece - 1) * SUB, tile), SUB), :]
-                    values.append(value)
-                if kind == 1:
-                    values = shift_columns(values, -1)
-                for tile, value in enumerate(values):
-                    col = level * z.tiles + tile
-                    coef[pl.ds(coef_row(kind, 0, col, piece * SUB), SUB), :] = value
-                    coef[pl.ds(coef_row(kind, 1, col, piece * SUB), SUB), :] = 0.5 * value * (1.0 - value)
+            parts = []
+            for tile in range(z.tiles):
+                edge = (kind * z.columns + level * z.tiles + tile) * SUB
+                pieces = [low_ref[pl.ds(z.low_rows + edge, SUB), :]]
+                for row in range(0, z.rows, SUB):
+                    pieces.append(ref[pl.ds(z.source_row(level, row, tile), SUB), :])
+                pieces.append(high_ref[pl.ds(z.high_rows + edge, SUB), :])
+                parts.append(jnp.concatenate(pieces, axis=0))
+            parts = reorder(parts, forth)
+            if kind == 1:
+                parts = shift_columns(parts, -1)
+            for tile, value in enumerate(parts):
+                col = level * z.tiles + tile
+                coef[pl.ds(coef_row(kind, 0, col, 0), span), :] = value
+                coef[pl.ds(coef_row(kind, 1, col, 0), span), :] = 0.5 * value * (1.0 - value)
 
     def weights(kind, col, j):
         return [coef[pl.ds(coef_row(kind, which, col, j), SUB), :] for which in range(2)]
 
     cols = range(z.columns)
 
+    def gather(index, carry):
+        for k in range(CHUNK):
+            for col, (level, tile) in enumerate(z.pairs()):
+                one = index * CHUNK + k
+                base = one * z.columns + col
+                at = (k * z.columns + col) * span + SUB
+                natural[pl.ds(at - LOW, LOW), :] = low_ref[pl.ds(base * LOW, LOW), :]
+                natural[pl.ds(at + z.rows, HIGH), :] = high_ref[pl.ds(base * HIGH, HIGH), :]
+                for row in range(0, z.rows, SUB):
+                    source = one * z.stride + z.source_row(level, row, tile)
+                    natural[pl.ds(at + row, SUB), :] = x_ref[pl.ds(pl.multiple_of(source, SUB), SUB), :]
+        count = CHUNK * z.levels
+        whole = natural[...].reshape(count, z.tiles, span, LANES)
+        parts = reorder([whole[:, t].reshape(count * span, LANES) for t in range(z.tiles)], forth)
+        for one in range(count):
+            for tile in range(z.tiles):
+                at = ((index * count + one) * z.tiles + tile) * span
+                strip[pl.ds(pl.multiple_of(at, SUB), span), :] = parts[tile][one * span : (one + 1) * span]
+        return carry
+
+    lax.fori_loop(0, z.species // CHUNK, gather, 0)
+
     def one_species(index, fields, fluxes):
-        for col, (level, tile) in enumerate(z.pairs()):
-            base = index * z.columns + col
-            fields[0][pl.ds(col * span + SUB - LOW, LOW), :] = low_ref[pl.ds(base * LOW, LOW), :]
-            fields[0][pl.ds(col * span + SUB + z.rows, HIGH), :] = high_ref[pl.ds(base * HIGH, HIGH), :]
-            for row in range(0, z.rows, SUB):
-                source = index * z.stride + z.source_row(level, row, tile)
-                fields[0][pl.ds(col * span + SUB + row, SUB), :] = x_ref[pl.ds(pl.multiple_of(source, SUB), SUB), :]
         for step in range(SECTIONS):
-            read, write = fields[step % 2], fields[(step + 1) % 2]
+            write = fields[step % 2]
+            if step == 0:
+                read = lambda col, j: strip[pl.ds((index * z.columns + col) * span + j, SUB), :]
+            else:
+                read = lambda col, j, ref=fields[(step + 1) % 2]: ref[pl.ds(col * span + j, SUB), :]
             bottom = SUB - LOW + 2 * (step + 1)
             top = SUB + z.rows + HIGH - (step + 1)
             for j in range(bottom - 1, top, SUB):
                 for col in cols:
-                    below, here, above = [read[pl.ds(col * span + j + k, SUB), :] for k in (-1, 0, 1)]
+                    below, here, above = [read(col, j + k) for k in (-1, 0, 1)]
                     a, b = weights(0, col, j + 1)
                     fluxes[pl.ds(col * span + j, SUB), :] = a * here + b * middle(here - below, above - here)
             for j in range(bottom, top, SUB):
@@ -129,7 +165,7 @@
                 for col in cols:
                     leave = fluxes[pl.ds(col * span + j, SUB), :]
                     enter = fluxes[pl.ds(col * span + j - 1, SUB), :]
-                    c.append(read[pl.ds(col * span + j, SUB), :] - (leave - enter))
+                    c.append(read(col, j) - (leave - enter))
                 for level in range(z.levels):
                     mine = slice(level * z.tiles, (level + 1) * z.tiles)
                     row = c[mine]
@@ -156,11 +192,9 @@
                         value = column[level] - net
                         if step < SECTIONS - 1:
                             write[pl.ds(col * span + j, SUB), :] = value
-                            continue
-                        for start in range(0, SUB, z.part):
-                            group = (j - SUB + start) // z.part
-                            base = (group * z.species + index) * z.blocks + col * z.part
-                            out_ref[pl.ds(base, z.part), :] = value[start : start + z.part]
+                        else:
+                            base = (index * z.columns + col) * z.rows + j - SUB
+                            final[pl.ds(pl.multiple_of(base, SUB), SUB), :] = value
 
     def some_species(index, carry):
         for k in range(TOGETHER):
@@ -168,6 +202,24 @@
         return carry
 
     lax.fori_loop(0, z.species // TOGETHER, some_species, 0)
+
+    back = spread_matrix(z.tiles, True)
+
+    def scatter(index, carry):
+        count = CHUNK * z.levels
+        size = count * z.tiles * z.rows
+        whole = final[pl.ds(pl.multiple_of(index * size, SUB), size), :].reshape(count, z.tiles, z.rows, LANES)
+        parts = reorder([whole[:, t].reshape(count * z.rows, LANES) for t in range(z.tiles)], back)
+        for one in range(count):
+            k, level = divmod(one, z.levels)
+            for tile in range(z.tiles):
+                for group in range(z.groups):
+                    start = one * z.rows + group * z.part
+                    at = (group * z.species + index * CHUNK + k) * z.blocks + (level * z.tiles + tile) * z.part
+                    out_ref[pl.ds(at, z.part), :] = parts[tile][start : start + z.part]
+        return carry
+
+    lax.fori_loop(0, z.species // CHUNK, scatter, 0)
 
 
 def chemistry_kernel(
@@ -250,12 +302,13 @@
         out_shape=(rows_of(z.low_rows + z.edge_rows), rows_of(z.high_rows + z.edge_rows)),
         in_specs=[VMEM] * 4,
         out_specs=(VMEM, VMEM),
+        compiler_params=pltpu.CompilerParams(vmem_limit_bytes=12 << 20),
         name="pack",
     )(*flat)
 
 
 def transport(z, *flat):
-    span = z.rows + 2 * SUB
+    span = z.span
     return pl.pallas_call(
         functools.partial(transport_kernel, z),
         out_shape=rows_of(z.groups * z.species * z.blocks),
@@ -263,8 +316,12 @@
         out_specs=VMEM,
         scratch_shapes=[
             pltpu.VMEM((6 * z.columns * span, LANES), jnp.float32),
+            pltpu.VMEM((CHUNK * z.columns * span, LANES), jnp.float32),
+            pltpu.VMEM((z.species * z.columns * span, LANES), jnp.float32),
+            pltpu.VMEM((z.species * z.columns * z.rows, LANES), jnp.float32),
         ]
         + [pltpu.VMEM((span * z.columns, LANES), jnp.float32)] * (3 * TOGETHER),
+        compiler_params=pltpu.CompilerParams(vmem_limit_bytes=32 << 20),
         name="transport",
     )(*flat)
 
@@ -277,6 +334,7 @@
         in_specs=[VMEM] * 4 + [SMEM] * 4,
         out_specs=VMEM,
         scratch_shapes=[pltpu.VMEM(size, jnp.float32)] * 6,
+        compiler_params=pltpu.CompilerParams(vmem_limit_bytes=32 << 20),
         name="chemistry",
     )(*args)
 

time: 99.8 us -> 94.3 us (0.945)
  Pallas kernels: 53.7 us -> 45.7 us
  local copies, waits for them, and re-layouts: 2.34 us -> 5.38 us
  waiting for transfers between devices: 34 us -> 33 us
    pallas_call x1, Pallas kernels: 31.6 us -> 27.1 us  [transport(): pl.pallas_call(functools.partial(transport_kernel, z), out_shape=rows_of(...]
    unnamed x8 -> x32, local copies, waits for them, and re-layouts: 1.51 us -> 5.22 us
    pallas_call x1, Pallas kernels: 2.9 us -> 0.26 us  [pack(): pl.pallas_call(functools.partial(pack_kernel, z), out_shape=(rows_of(z.lo...]
where the time goes in v2:
time: 94.3 us; the launch traced here: 93.8 us
  Pallas kernels  45.7 us (48%)
  waiting for transfers between devices  33 us (35%)
  starting transfers between devices  9.57 us (10%)
  local copies, waits for them, and re-layouts  5.38 us (6%)
    pallas_call x1, Pallas kernels, transport(): pl.pallas_call(functools.partial(transport_kernel, z), out_shape=rows_of(...  27.1 us
    all_to_all x1, waiting for transfers between devices, body(): lax.all_to_all(moved, 'tracer', split_axis=0, concat_axis=0, tiled=True)  24.8 us
    pallas_call x1, Pallas kernels, chemistry(): pl.pallas_call(functools.partial(chemistry_kernel, species, blocks), out_...  18.4 us
    ppermute x1, waiting for transfers between devices, body(): high = lax.ppermute(high, 'space', [(i + 1, i) for i in range(strips - 1)])  5.8 us
    unnamed x32, local copies, waits for them, and re-layouts  5.22 us
    all_to_all x1, starting transfers between devices, body(): lax.all_to_all(moved, 'tracer', split_axis=0, concat_axis=0, tiled=True)  3.88 us
    ppermute x1, starting transfers between devices, body(): high = lax.ppermute(high, 'space', [(i + 1, i) for i in range(strips - 1)])  3.64 us
    ppermute x1, waiting for transfers between devices, body(): low = lax.ppermute(low, 'space', [(i, i + 1) for i in range(strips - 1)])  2.46 us
  transfers between devices with their start and end apart: 3, of which 3 were waited for; matrix products, arithmetic and copies ran while one was open for 0% of the time, Pallas kernels for 0%

profile of v2, /device:TPU:16, one launch (start us, length us, event | category | flops | bytes accessed | tf_op | source)
XLA Modules:
  0.0 93.8 jit_solution(9585078582593363514)
XLA Ops:
  0.0 0.0 copy-start
  0.0 1.6 %copy-done = f32[64,2,16,256]{3,2,1,0:T(8,128)S(1)} copy-done((f32[64,2,16,256]{3,2,1,0:T(8,128)S(1)}, f32[64,2,16,256]{3,2,1,0:T(8,128)}, u32[]{:S(2)}) %copy-start) | copy-done | bytes 2097176
  1.6 0.0 copy-start.3
  1.6 0.8 copy-done.3
  2.4 0.0 copy-start.5
  2.4 0.8 copy-done.5
  3.1 0.0 copy-start.7
  3.1 0.8 copy-done.7
  3.9 0.0 copy-start.1
  3.9 0.0 copy-start.4
  3.9 0.0 copy-start.6
  3.9 0.0 copy-start.8
  3.9 0.3 pack.1
  4.1 2.1 %collective-permute-start = (f32[1632,128]{1,0:T(8,128)S(1)}, f32[1632,128]{1,0:T(8,128)S(1)}, u32[]{:S(2)}, u32[]{:S(2)}) collective-permute-start(f32[1632,128]{1,0:T(8,128)S(1)} %get-tuple-element.7), channel_id=1, source_target_pairs={{0,4},{4,8},{8,12},{12,16},{16,20},{20,24},{24,28},{1,5},{5,9},{9,... | collective-permute-start | bytes 2506760 | tf_op jit(solution)/shard_map/ppermute | solution.py:363
  6.2 3.6 %collective-permute-start.1 = (f32[864,128]{1,0:T(8,128)S(1)}, f32[864,128]{1,0:T(8,128)S(1)}, u32[]{:S(2)}, u32[]{:S(2)}) collective-permute-start(f32[864,128]{1,0:T(8,128)S(1)} %get-tuple-element.8), channel_id=1, source_target_pairs={{4,0},{8,4},{12,8},{16,12},{20,16},{24,20},{28,24},{5,1},{9,5},{13... | collective-permute-start | bytes 1327112 | tf_op jit(solution)/shard_map/ppermute | solution.py:364
  9.9 5.8 %collective-permute-done.1.high_ref = f32[864,128]{1,0:T(8,128)S(1)} collective-permute-done((f32[864,128]{1,0:T(8,128)S(1)}, f32[864,128]{1,0:T(8,128)S(1)}, u32[]{:S(2)}, u32[]{:S(2)}) %collective-permute-start.1) | collective-permute-done | bytes 442400 | tf_op jit(solution)/shard_map/ppermute | solution.py:364
  15.7 2.5 %collective-permute-done.low_ref = f32[1632,128]{1,0:T(8,128)S(1)} collective-permute-done((f32[1632,128]{1,0:T(8,128)S(1)}, f32[1632,128]{1,0:T(8,128)S(1)}, u32[]{:S(2)}, u32[]{:S(2)}) %collective-permute-start) | collective-permute-done | bytes 835616 | tf_op jit(solution)/shard_map/ppermute | solution.py:363
  18.1 0.0 copy-done.1
  18.1 0.0 copy-done.4
  18.1 0.0 copy-done.6
  18.1 0.0 copy-done.8
  18.1 27.1 %transport.1 = f32[4096,128]{1,0:T(8,128)S(1)} custom-call(f32[4096,128]{1,0:T(8,128)S(1)} %bitcast.39, f32[64,128]{1,0:T(8,128)S(1)} %bitcast.43, f32[64,128]{1,0:T(8,128)S(1)} %bitcast.45, f32[64,128]{1,0:T(8,128)S(1)} %bitcast.47, f32[1632,128]{1,0:T(8,128)S(1)} %collective-permute-done.low_ref, f32[864,128]{1,0:T(8,128)S(1)} %collective-permute-done.1.high_ref), custom_call_target="tpu_custom_call" | custom-call | tf_op jit(solution)/shard_map/transport/pallas_call | solution.py:312
  45.2 0.0 copy-start.2
  45.2 1.3 %copy-done.2 = f32[4096,128]{1,0:T(8,128)} copy-done((f32[4096,128]{1,0:T(8,128)}, f32[4096,128]{1,0:T(8,128)S(1)}, u32[]{:S(2)}) %copy-start.2) | copy-done | bytes 2097176
  46.5 0.0 copy-start.15
  46.5 0.0 copy-start.9
  46.5 0.0 copy-start.10
  46.5 0.0 copy-start.11
  46.6 0.0 copy-start.12
  46.6 0.0 copy-start.13
  46.6 0.0 copy-start.14
  46.6 3.9 %all-to-all-start = ((f32[4,1024,128]{2,1,0:T(8,128)}), f32[4,1024,128]{2,1,0:T(8,128)S(1)}, u32[]{:S(2)}, u32[]{:S(2)}) async-start(f32[4,1024,128]{2,1,0:T(8,128)} %bitcast.41), calls=%async_computation | async-start | bytes 4194304 | tf_op jit(solution)/shard_map/all_to_all | solution.py:367
  50.5 0.0 copy-done.15
  50.5 0.1 broadcast_in_dim.7
  50.6 24.8 %all-to-all-done = f32[4,1024,128]{2,1,0:T(8,128)S(1)} async-done(((f32[4,1024,128]{2,1,0:T(8,128)}), f32[4,1024,128]{2,1,0:T(8,128)S(1)}, u32[]{:S(2)}, u32[]{:S(2)}) %all-to-all-start) | async-done | bytes 2097184 | tf_op jit(solution)/shard_map/all_to_all | solution.py:367
  75.3 0.1 broadcast_in_dim.8.lit_ref
  75.4 0.0 copy-done.9
  75.4 0.0 copy-done.10
  75.4 0.0 copy-done.11
  75.4 0.0 copy-done.12
  75.4 0.0 copy-done.13
  75.4 0.0 copy-done.14
  75.5 18.4 %chemistry.1 = f32[4096,128]{1,0:T(8,128)} custom-call(f32[4096,128]{1,0:T(8,128)S(1)} %bitcast.40, f32[16,128]{1,0:T(8,128)S(1)} %bitcast.48, f32[16,128]{1,0:T(8,128)S(1)} %bitcast.49, s32[16,128]{1,0:T(8,128)S(1)} %broadcast_in_dim.8.lit_ref, f32[768]{0:T(1024)S(1)} %copy-done.12, f32[768]{0:T(1024)S(1)} %copy-done.13, f32[768]{0:T(1024)S(1)} %copy-done.14, ...), custom_call_target="tpu_custom_call" | custom-call | tf_op jit(solution)/shard_map/chemistry/pallas_call | solution.py:331
Async XLA Ops:
  0.0 1.6 %copy-start = (f32[64,2,16,256]{3,2,1,0:T(8,128)S(1)}, f32[64,2,16,256]{3,2,1,0:T(8,128)}, u32[]{:S(2)}) copy-start(f32[64,2,16,256]{3,2,1,0:T(8,128)} %param.11) | copy-start | bytes 6291460
  1.6 0.8 copy-start.3
  2.4 0.8 copy-start.5
  3.1 0.8 copy-start.7
  3.9 14.2 %copy-start.1 = (f32[64,2,16,256]{3,2,1,0:T(8,128)S(1)}, f32[64,2,16,256]{3,2,1,0:T(8,128)}, u32[]{:S(2)}) copy-start(f32[64,2,16,256]{3,2,1,0:T(8,128)} %param.11) | copy-start | bytes 6291460
  3.9 14.2 %copy-start.4 = (f32[2,16,256]{2,1,0:T(8,128)S(1)}, f32[2,16,256]{2,1,0:T(8,128)}, u32[]{:S(2)}) copy-start(f32[2,16,256]{2,1,0:T(8,128)} %param.12) | copy-start | bytes 98308
  3.9 14.2 %copy-start.6 = (f32[2,16,256]{2,1,0:T(8,128)S(1)}, f32[2,16,256]{2,1,0:T(8,128)}, u32[]{:S(2)}) copy-start(f32[2,16,256]{2,1,0:T(8,128)} %param.13) | copy-start | bytes 98308
  3.9 14.3 %copy-start.8 = (f32[2,16,256]{2,1,0:T(8,128)S(1)}, f32[2,16,256]{2,1,0:T(8,128)}, u32[]{:S(2)}) copy-start(f32[2,16,256]{2,1,0:T(8,128)} %param.14) | copy-start | bytes 98308
  4.1 14.0 %collective-permute-start = (f32[1632,128]{1,0:T(8,128)S(1)}, f32[1632,128]{1,0:T(8,128)S(1)}, u32[]{:S(2)}, u32[]{:S(2)}) collective-permute-start(f32[1632,128]{1,0:T(8,128)S(1)} %get-tuple-element.7), channel_id=1, source_target_pairs={{0,4},{4,8},{8,12},{12,16},{16,20},{20,24},{24,28},{1,5},{5,9},{9,... | collective-permute-start | bytes 2506760 | tf_op jit(solution)/shard_map/ppermute | solution.py:363
  6.2 9.4 %collective-permute-start.1 = (f32[864,128]{1,0:T(8,128)S(1)}, f32[864,128]{1,0:T(8,128)S(1)}, u32[]{:S(2)}, u32[]{:S(2)}) collective-permute-start(f32[864,128]{1,0:T(8,128)S(1)} %get-tuple-element.8), channel_id=1, source_target_pairs={{4,0},{8,4},{12,8},{16,12},{20,16},{24,20},{28,24},{5,1},{9,5},{13... | collective-permute-start | bytes 1327112 | tf_op jit(solution)/shard_map/ppermute | solution.py:364
  45.2 1.3 %copy-start.2 = (f32[4096,128]{1,0:T(8,128)}, f32[4096,128]{1,0:T(8,128)S(1)}, u32[]{:S(2)}) copy-start(f32[4096,128]{1,0:T(8,128)S(1)} %transport.1) | copy-start | bytes 6291460
  46.5 3.9 %copy-start.15 = (s32[2,4,2]{1,2,0:T(2,128)S(1)}, s32[2,4,2]{1,2,0:T(2,128)}, u32[]{:S(2)}) copy-start(s32[2,4,2]{1,2,0:T(2,128)} %param.17) | copy-start | bytes 196
  46.5 28.9 %copy-start.9 = (s32[3,768]{1,0:T(4,128)S(1)}, s32[3,768]{1,0:T(4,128)}, u32[]{:S(2)}) copy-start(s32[3,768]{1,0:T(4,128)} %table_ref.1) | copy-start | bytes 27652
  46.5 28.9 %copy-start.10 = (f32[2,4,256]{2,1,0:T(4,128)S(1)}, f32[2,4,256]{2,1,0:T(4,128)}, u32[]{:S(2)}) copy-start(f32[2,4,256]{2,1,0:T(4,128)} %param.15) | copy-start | bytes 24580
  46.5 28.9 %copy-start.11 = (f32[2,4,256]{2,1,0:T(4,128)S(1)}, f32[2,4,256]{2,1,0:T(4,128)}, u32[]{:S(2)}) copy-start(f32[2,4,256]{2,1,0:T(4,128)} %param.16) | copy-start | bytes 24580
  46.6 28.9 %copy-start.12 = (f32[768]{0:T(1024)S(1)}, f32[768]{0:T(1024)}, u32[]{:S(2)}) copy-start(f32[768]{0:T(1024)} %rate_ref.1) | copy-start | bytes 9220
  46.6 28.9 %copy-start.13 = (f32[768]{0:T(1024)S(1)}, f32[768]{0:T(1024)}, u32[]{:S(2)}) copy-start(f32[768]{0:T(1024)} %barrier_ref.1) | copy-start | bytes 9220
  46.6 28.9 %copy-start.14 = (f32[768]{0:T(1024)S(1)}, f32[768]{0:T(1024)}, u32[]{:S(2)}) copy-start(f32[768]{0:T(1024)} %photo_ref.1) | copy-start | bytes 9220
  46.6 28.8 %all-to-all-start = ((f32[4,1024,128]{2,1,0:T(8,128)}), f32[4,1024,128]{2,1,0:T(8,128)S(1)}, u32[]{:S(2)}, u32[]{:S(2)}) async-start(f32[4,1024,128]{2,1,0:T(8,128)} %bitcast.41), calls=%async_computation | async-start | bytes 4194304 | tf_op jit(solution)/shard_map/all_to_all | solution.py:367

commit v3 on v2

--- a/solution.py
+++ b/solution.py
@@ -13,8 +13,10 @@
 SUB = 8
 LOW = 2 * SECTIONS
 HIGH = SECTIONS
-TOGETHER = 2
+PARTS = 2
+TOGETHER = 8
 CHUNK = 8
+LOG2E = 1.4426950408889634
 
 
 def flat_rows(cells):
@@ -45,16 +47,13 @@
         return [(level, tile) for level in range(self.levels) for tile in range(self.tiles)]
 
 
-def pack_kernel(z, x_ref, east_ref, north_ref, up_ref, low_ref, high_ref):
-    def one_species(index, carry):
-        for offset, rows, out_ref in ((z.rows - LOW, LOW, low_ref), (0, HIGH, high_ref)):
-            for col, (level, tile) in enumerate(z.pairs()):
-                source = index * z.stride + z.source_row(level, offset, tile)
-                target = (index * z.columns + col) * rows
-                out_ref[pl.ds(target, rows), :] = x_ref[pl.ds(source, rows), :]
-        return carry
-
-    lax.fori_loop(0, z.species, one_species, 0, unroll=4)
+def pack_kernel(z, x_hbm, east_hbm, north_hbm, up_hbm, low_ref, high_ref, x_ref, east_ref, north_ref, up_ref, sems):
+    pairs = ((x_hbm, x_ref), (east_hbm, east_ref), (north_hbm, north_ref), (up_hbm, up_ref))
+    copies = [pltpu.make_async_copy(src, dst, sems.at[k]) for k, (src, dst) in enumerate(pairs)]
+    for copy in copies:
+        copy.start()
+    for copy in copies[1:]:
+        copy.wait()
     for out_ref, base, last in ((low_ref, z.low_rows, True), (high_ref, z.high_rows, False)):
         row = z.rows - SUB if last else 0
         for kind, ref in enumerate((east_ref, north_ref, up_ref)):
@@ -62,6 +61,17 @@
                 target = base + (kind * z.columns + col) * SUB
                 source = z.source_row(level, row, tile)
                 out_ref[pl.ds(target, SUB), :] = ref[pl.ds(source, SUB), :]
+    copies[0].wait()
+
+    def one_species(index, carry):
+        for offset, rows, out_ref in ((z.rows - LOW, LOW, low_ref), (0, HIGH, high_ref)):
+            for col, (level, tile) in enumerate(z.pairs()):
+                source = index * z.stride + z.source_row(level, offset, tile)
+                target = (index * z.columns + col) * rows
+                out_ref[pl.ds(target, rows), :] = x_ref[pl.ds(source, rows), :]
+        return carry
+
+    lax.fori_loop(0, z.species, one_species, 0, unroll=4)
 
 
 def middle(a, b):
@@ -93,7 +103,7 @@
 
 
 def transport_kernel(
-    z, x_ref, east_ref, north_ref, up_ref, low_ref, high_ref, out_ref, coef, natural, strip, final, *scratch
+    z, first, count, x_ref, east_ref, north_ref, up_ref, low_ref, high_ref, out_ref, coef, natural, strip, final, *scratch
 ):
     span = z.span
     forth = spread_matrix(z.tiles, False)
@@ -127,7 +137,7 @@
     def gather(index, carry):
         for k in range(CHUNK):
             for col, (level, tile) in enumerate(z.pairs()):
-                one = index * CHUNK + k
+                one = first + index * CHUNK + k
                 base = one * z.columns + col
                 at = (k * z.columns + col) * span + SUB
                 natural[pl.ds(at - LOW, LOW), :] = low_ref[pl.ds(base * LOW, LOW), :]
@@ -135,16 +145,16 @@
                 for row in range(0, z.rows, SUB):
                     source = one * z.stride + z.source_row(level, row, tile)
                     natural[pl.ds(at + row, SUB), :] = x_ref[pl.ds(pl.multiple_of(source, SUB), SUB), :]
-        count = CHUNK * z.levels
-        whole = natural[...].reshape(count, z.tiles, span, LANES)
-        parts = reorder([whole[:, t].reshape(count * span, LANES) for t in range(z.tiles)], forth)
-        for one in range(count):
+        many = CHUNK * z.levels
+        whole = natural[...].reshape(many, z.tiles, span, LANES)
+        parts = reorder([whole[:, t].reshape(many * span, LANES) for t in range(z.tiles)], forth)
+        for one in range(many):
             for tile in range(z.tiles):
-                at = ((index * count + one) * z.tiles + tile) * span
+                at = ((index * many + one) * z.tiles + tile) * span
                 strip[pl.ds(pl.multiple_of(at, SUB), span), :] = parts[tile][one * span : (one + 1) * span]
         return carry
 
-    lax.fori_loop(0, z.species // CHUNK, gather, 0)
+    lax.fori_loop(0, count // CHUNK, gather, 0)
 
     def one_species(index, fields, fluxes):
         for step in range(SECTIONS):
@@ -201,88 +211,101 @@
             one_species(index * TOGETHER + k, scratch[3 * k : 3 * k + 2], scratch[3 * k + 2])
         return carry
 
-    lax.fori_loop(0, z.species // TOGETHER, some_species, 0)
+    lax.fori_loop(0, count // TOGETHER, some_species, 0)
 
     back = spread_matrix(z.tiles, True)
 
     def scatter(index, carry):
-        count = CHUNK * z.levels
-        size = count * z.tiles * z.rows
-        whole = final[pl.ds(pl.multiple_of(index * size, SUB), size), :].reshape(count, z.tiles, z.rows, LANES)
-        parts = reorder([whole[:, t].reshape(count * z.rows, LANES) for t in range(z.tiles)], back)
-        for one in range(count):
+        many = CHUNK * z.levels
+        size = many * z.tiles * z.rows
+        whole = final[pl.ds(pl.multiple_of(index * size, SUB), size), :].reshape(many, z.tiles, z.rows, LANES)
+        parts = reorder([whole[:, t].reshape(many * z.rows, LANES) for t in range(z.tiles)], back)
+        for one in range(many):
             k, level = divmod(one, z.levels)
             for tile in range(z.tiles):
                 for group in range(z.groups):
                     start = one * z.rows + group * z.part
-                    at = (group * z.species + index * CHUNK + k) * z.blocks + (level * z.tiles + tile) * z.part
+                    at = (group * count + index * CHUNK + k) * z.blocks + (level * z.tiles + tile) * z.part
                     out_ref[pl.ds(at, z.part), :] = parts[tile][start : start + z.part]
         return carry
 
-    lax.fori_loop(0, z.species // CHUNK, scatter, 0)
-
-
-def chemistry_kernel(
-    species, blocks, c_ref, warm_ref, glow_ref, lit_ref, rate_ref, barrier_ref, photo_ref, table_ref,
-    out_ref, made_a, made_b, lost_a, lost_b, lost_c, lost_d,
-):
-    pieces = blocks // SUB
-    reactions = rate_ref.shape[0]
-    made = (made_a, made_b)
-    lost = ((lost_a, lost_b), (lost_c, lost_d))
-
-    def cell(index, piece):
-        return pl.ds(pl.multiple_of(index * blocks, SUB) + piece * SUB, SUB)
-
-    lit = [lit_ref[pl.ds(piece * SUB, SUB), :] == 1 for piece in range(pieces)]
-    warm = [warm_ref[pl.ds(piece * SUB, SUB), :] - 1.0 for piece in range(pieces)]
-    glow = [jnp.where(lit[p], glow_ref[pl.ds(p * SUB, SUB), :], 0.0) for p in range(pieces)]
+    lax.fori_loop(0, count // CHUNK, scatter, 0)
+
+
+def rates_kernel(pieces, after_ref, warm_ref, glow_ref, lit_ref, rate_ref, barrier_ref, photo_ref, out_ref):
+    warm = [(1.0 - warm_ref[pl.ds(p * SUB, SUB), :]) * LOG2E for p in range(pieces)]
+    glow = [
+        jnp.where(lit_ref[pl.ds(p * SUB, SUB), :] == 1, glow_ref[pl.ds(p * SUB, SUB), :], 0.0)
+        for p in range(pieces)
+    ]
+
+    def one(r, carry):
+        for p in range(pieces):
+            at = pl.ds(pl.multiple_of(r * pieces * SUB, SUB) + p * SUB, SUB)
+            out_ref[at, :] = rate_ref[r] * jnp.exp2(barrier_ref[r] * warm[p]) + photo_ref[r] * glow[p]
+        return carry
+
+    lax.fori_loop(0, rate_ref.shape[0], one, 0, unroll=8)
+
+
+def chemistry_kernel(z, species, *refs):
+    pieces = z.blocks // SUB
+    parts, (lit_ref, k_ref, table_ref, out_ref, state, made, lost_a, lost_b) = refs[:PARTS], refs[PARTS:]
+    reactions = k_ref.shape[0] // z.blocks
+
+    def cell(row, piece):
+        return pl.ds(pl.multiple_of(row, SUB) + piece * SUB, SUB)
+
+    lit = [lit_ref[pl.ds(p * SUB, SUB), :] == 1 for p in range(pieces)]
+    steps = [jnp.where(lit[p], float(DAY_STEPS), 1.0) for p in range(pieces)]
+    zero = jnp.zeros((SUB, LANES), jnp.float32)
+
+    def prepare(at, p, value):
+        made[at, :] = steps[p] * value
+        lost_a[at, :] = steps[p]
+        lost_b[at, :] = zero
+
+    count = z.species // PARTS
+
+    def begin(index, carry):
+        for part, ref in enumerate(parts):
+            for group in range(z.groups):
+                for p in range(pieces):
+                    value = ref[cell((group * count + index) * z.blocks, p), :]
+                    at = cell((group * z.species + part * count + index) * z.blocks, p)
+                    state[at, :] = value
+                    prepare(at, p, value)
+        return carry
+
+    lax.fori_loop(0, count, begin, 0)
+
+    def react(r, carry):
+        first, second, product = table_ref[r], table_ref[reactions + r], table_ref[2 * reactions + r]
+        for p in range(pieces):
+            k = k_ref[cell(r * z.blocks, p), :]
+            x = state[cell(first, p), :]
+            y = state[cell(second, p), :]
+            kx = k * x
+            ky = k * y
+            made[cell(product, p), :] += kx * y
+            lost_a[cell(first, p), :] += ky
+            lost_b[cell(second, p), :] += kx
+        return carry
 
     for sub in range(DAY_STEPS):
-        source = c_ref if sub == 0 else out_ref
-        steps = [jnp.where(lit[p], float(DAY_STEPS), 1.0) for p in range(pieces)]
-
-        def begin(s, carry):
-            for p in range(pieces):
-                made[0][cell(s, p), :] = steps[p] * source[cell(s, p), :]
-                made[1][cell(s, p), :] = jnp.zeros((SUB, LANES), jnp.float32)
-                for k in range(2):
-                    for side in range(2):
-                        fill = steps[p] if k == 0 and side == 0 else jnp.zeros((SUB, LANES), jnp.float32)
-                        lost[k][side][cell(s, p), :] = fill
-            return carry
-
-        lax.fori_loop(0, species, begin, 0, unroll=4)
-
-        def react(r, parity):
-            first, second, product = table_ref[0, r], table_ref[1, r], table_ref[2, r]
-            rate, barrier, photo = rate_ref[r], barrier_ref[r], photo_ref[r]
-            for p in range(pieces):
-                k = rate * jnp.exp(-barrier * warm[p]) + photo * glow[p]
-                x = source[cell(first, p), :]
-                y = source[cell(second, p), :]
-                kx = k * x
-                ky = k * y
-                made[parity][cell(product, p), :] += kx * y
-                lost[parity][0][cell(first, p), :] += ky
-                lost[parity][1][cell(second, p), :] += kx
-
-        def two(i, carry):
-            react(2 * i, 0)
-            react(2 * i + 1, 1)
-            return carry
-
-        lax.fori_loop(0, reactions // 2, two, 0, unroll=4)
+        lax.fori_loop(0, reactions, react, 0, unroll=16)
 
         def finish(s, carry):
             for p in range(pieces):
-                at = cell(s, p)
-                top = made[0][at, :] + made[1][at, :]
-                bottom = (lost[0][0][at, :] + lost[0][1][at, :]) + (lost[1][0][at, :] + lost[1][1][at, :])
-                value = top / bottom
+                at = cell(s * z.blocks, p)
+                value = made[at, :] / (lost_a[at, :] + lost_b[at, :])
+                if sub < DAY_STEPS - 1:
+                    prepare(at, p, value)
+                    if sub == 0:
+                        state[at, :] = value
                 if sub > 0:
-                    value = jnp.where(lit[p], value, source[at, :])
-                out_ref[at, :] = value
+                    value = jnp.where(lit[p], value, state[at, :])
+                    out_ref[at, :] = value
             return carry
 
         lax.fori_loop(0, species, finish, 0, unroll=4)
@@ -294,47 +317,68 @@
 
 def rows_of(count):
     return jax.ShapeDtypeStruct((count, LANES), jnp.float32)
+
+
+ANY = pl.BlockSpec(memory_space=pl.ANY)
+HBM = pl.BlockSpec(memory_space=pltpu.HBM)
 
 
 def pack(z, *flat):
     return pl.pallas_call(
         functools.partial(pack_kernel, z),
         out_shape=(rows_of(z.low_rows + z.edge_rows), rows_of(z.high_rows + z.edge_rows)),
-        in_specs=[VMEM] * 4,
+        in_specs=[HBM] * 4,
         out_specs=(VMEM, VMEM),
+        scratch_shapes=[pltpu.VMEM(a.shape, jnp.float32) for a in flat] + [pltpu.SemaphoreType.DMA((4,))],
         compiler_params=pltpu.CompilerParams(vmem_limit_bytes=12 << 20),
         name="pack",
     )(*flat)
 
 
-def transport(z, *flat):
-    span = z.span
+def transport(z, part, *flat):
+    count = z.species // PARTS
     return pl.pallas_call(
-        functools.partial(transport_kernel, z),
-        out_shape=rows_of(z.groups * z.species * z.blocks),
+        functools.partial(transport_kernel, z, part * count, count),
+        out_shape=rows_of(z.groups * count * z.blocks),
         in_specs=[VMEM] * 6,
         out_specs=VMEM,
         scratch_shapes=[
-            pltpu.VMEM((6 * z.columns * span, LANES), jnp.float32),
-            pltpu.VMEM((CHUNK * z.columns * span, LANES), jnp.float32),
-            pltpu.VMEM((z.species * z.columns * span, LANES), jnp.float32),
-            pltpu.VMEM((z.species * z.columns * z.rows, LANES), jnp.float32),
+            pltpu.VMEM((6 * z.columns * z.span, LANES), jnp.float32),
+            pltpu.VMEM((CHUNK * z.columns * z.span, LANES), jnp.float32),
+            pltpu.VMEM((count * z.columns * z.span, LANES), jnp.float32),
+            pltpu.VMEM((count * z.columns * z.rows, LANES), jnp.float32),
         ]
-        + [pltpu.VMEM((span * z.columns, LANES), jnp.float32)] * (3 * TOGETHER),
-        compiler_params=pltpu.CompilerParams(vmem_limit_bytes=32 << 20),
+        + [pltpu.VMEM((z.span * z.columns, LANES), jnp.float32)] * (3 * TOGETHER),
+        compiler_params=pltpu.CompilerParams(vmem_limit_bytes=24 << 20),
+        cost_estimate=pl.CostEstimate(flops=400 * count * z.stride * LANES, bytes_accessed=0, transcendentals=0),
         name="transport",
     )(*flat)
 
 
-def chemistry(species, blocks, *args):
-    size = (species * blocks, LANES)
+def rates(z, after, warm, glow, lit, rate, barrier, photo):
+    reactions = rate.shape[0]
     return pl.pallas_call(
-        functools.partial(chemistry_kernel, species, blocks),
-        out_shape=rows_of(species * blocks),
-        in_specs=[VMEM] * 4 + [SMEM] * 4,
+        functools.partial(rates_kernel, z.blocks // SUB),
+        out_shape=rows_of(reactions * z.blocks),
+        in_specs=[ANY] + [VMEM] * 3 + [SMEM] * 3,
         out_specs=VMEM,
-        scratch_shapes=[pltpu.VMEM(size, jnp.float32)] * 6,
-        compiler_params=pltpu.CompilerParams(vmem_limit_bytes=32 << 20),
+        compiler_params=pltpu.CompilerParams(vmem_limit_bytes=16 << 20),
+        cost_estimate=pl.CostEstimate(
+            flops=40 * reactions * z.blocks * LANES, bytes_accessed=0, transcendentals=0
+        ),
+        name="rates",
+    )(after, warm, glow, lit, rate, barrier, photo)
+
+
+def chemistry(z, species, *args):
+    size = (species * z.blocks, LANES)
+    return pl.pallas_call(
+        functools.partial(chemistry_kernel, z, species),
+        out_shape=rows_of(species * z.blocks),
+        in_specs=[VMEM] * (PARTS + 2) + [SMEM],
+        out_specs=VMEM,
+        scratch_shapes=[pltpu.VMEM(size, jnp.float32)] * 4,
+        compiler_params=pltpu.CompilerParams(vmem_limit_bytes=24 << 20),
         name="chemistry",
     )(*args)
 
@@ -362,24 +406,29 @@
     low, high = pack(z, *flat)
     low = lax.ppermute(low, "space", [(i, i + 1) for i in range(strips - 1)])
     high = lax.ppermute(high, "space", [(i + 1, i) for i in range(strips - 1)])
-    moved = transport(z, *flat, low, high)
-    moved = moved.reshape(groups, z.species * z.blocks, LANES)
-    moved = lax.all_to_all(moved, "tracer", split_axis=0, concat_axis=0, tiled=True)
     species = z.species * groups
+    count = z.species // PARTS
+    arrived = []
+    for part in range(PARTS):
+        moved = transport(z, part, *flat, low, high)
+        regrouped = lax.all_to_all(
+            moved.reshape(groups, count * z.blocks, LANES), "tracer", split_axis=0, concat_axis=0, tiled=True
+        )
+        arrived.append(regrouped.reshape(species // PARTS * z.blocks, LANES))
     lit = jnp.moveaxis(daylight_mask, 2, 1).reshape(z.blocks, 1)
     lit = jnp.broadcast_to(lit, (z.blocks, LANES))
-    out = chemistry(
-        species,
-        z.blocks,
-        moved.reshape(species * z.blocks, LANES),
+    table, lit, _ = lax.optimization_barrier((stoichiometry_table, lit, moved))
+    k = rates(
+        z,
+        moved,
         flat_rows(thermal_anomaly),
         flat_rows(radiant_flux),
         lit,
         baseline_kinetic_coefficient,
         arrhenius_barrier,
         photodissociation_factor,
-        stoichiometry_table,
     )
+    out = chemistry(z, species, *arrived, lit, k, table.reshape(-1) * z.blocks)
     out = out.reshape(species, z.levels, z.tiles, z.part, LANES)
     return jnp.moveaxis(out, 2, 3).reshape(species, z.levels, z.part, z.width)
 

time: 94.3 us -> 80 us (0.85)
  waiting for transfers between devices: 33 us -> 16.3 us
  Pallas kernels: 45.7 us -> 36.6 us
  local copies, waits for them, and re-layouts: 5.38 us -> 12.6 us
  starting transfers between devices: 9.57 us -> 13.6 us
    all_to_all x1 -> x2, waiting for transfers between devices: 24.8 us -> 8.02 us  [body(): lax.all_to_all(moved.reshape(groups, count * z.blocks, LANES), 'tracer',...]
    pallas_call x2 -> x4, Pallas kernels: 45.4 us -> 36 us  [the longest x2 18.8 us: transport(): pl.pallas_call(functools.partial(transport_kernel, z, part * count, count...]
    unnamed x32 -> x44, local copies, waits for them, and re-layouts: 5.22 us -> 12.5 us
    all_to_all x1 -> x2, starting transfers between devices: 3.88 us -> 7.95 us  [body(): lax.all_to_all(moved.reshape(groups, count * z.blocks, LANES), 'tracer',...]
  transfers between devices with their start and end apart: 3 -> 4, of which waited for: 3 -> 4; matrix products, arithmetic and copies ran while one was open for 0% -> 0% of each run, Pallas kernels for 0% -> 16%
where the time goes in v3:
time: 80 us; the launch traced here: 79.3 us
  Pallas kernels  36.6 us (46%)
  waiting for transfers between devices  16.3 us (20%)
  starting transfers between devices  13.6 us (17%)
  local copies, waits for them, and re-layouts  12.6 us (16%)
    pallas_call x2, Pallas kernels, transport(): pl.pallas_call(functools.partial(transport_kernel, z, part * count, count...  18.8 us
    pallas_call x1, Pallas kernels, chemistry(): pl.pallas_call(functools.partial(chemistry_kernel, z, species), out_shape...  13.4 us
    unnamed x44, local copies, waits for them, and re-layouts  12.5 us
    all_to_all x2, waiting for transfers between devices, body(): lax.all_to_all(moved.reshape(groups, count * z.blocks, LANES), 'tracer',...  8.02 us
    all_to_all x2, starting transfers between devices, body(): lax.all_to_all(moved.reshape(groups, count * z.blocks, LANES), 'tracer',...  7.95 us
    ppermute x1, waiting for transfers between devices, body(): high = lax.ppermute(high, 'space', [(i + 1, i) for i in range(strips - 1)])  5.8 us
    pallas_call x1, Pallas kernels, rates(): pl.pallas_call(functools.partial(rates_kernel, z.blocks // SUB), out_shap...  3.76 us
    ppermute x1, starting transfers between devices, body(): high = lax.ppermute(high, 'space', [(i + 1, i) for i in range(strips - 1)])  3.64 us
  transfers between devices with their start and end apart: 4, of which 4 were waited for; matrix products, arithmetic and copies ran while one was open for 0% of the time, Pallas kernels for 16%

profile of v3, /device:TPU:16, one launch (start us, length us, event | category | flops | bytes accessed | tf_op | source)
XLA Modules:
  0.0 79.3 jit_solution(9235892871060797968)
XLA Ops:
  0.0 0.0 copy-start.2
  0.0 1.6 %copy-done.2 = f32[64,2,16,256]{3,2,1,0:T(8,128)S(1)} copy-done((f32[64,2,16,256]{3,2,1,0:T(8,128)S(1)}, f32[64,2,16,256]{3,2,1,0:T(8,128)}, u32[]{:S(2)}) %copy-start.2) | copy-done | bytes 2097176
  1.6 0.0 copy-start.9
  1.6 0.8 copy-done.9
  2.4 0.0 copy-start.11
  2.4 0.8 copy-done.11
  3.1 0.0 copy-start.13
  3.1 0.8 copy-done.13
  3.9 0.0 copy-start.3
  3.9 0.6 pack.1
  4.5 2.1 %collective-permute-start = (f32[1632,128]{1,0:T(8,128)S(1)}, f32[1632,128]{1,0:T(8,128)S(1)}, u32[]{:S(2)}, u32[]{:S(2)}) collective-permute-start(f32[1632,128]{1,0:T(8,128)S(1)} %get-tuple-element.9), channel_id=1, source_target_pairs={{0,4},{4,8},{8,12},{12,16},{16,20},{20,24},{24,28},{1,5},{5,9},{9,... | collective-permute-start | bytes 2506760 | tf_op jit(solution)/shard_map/ppermute | solution.py:407
  6.5 3.6 %collective-permute-start.1 = (f32[864,128]{1,0:T(8,128)S(1)}, f32[864,128]{1,0:T(8,128)S(1)}, u32[]{:S(2)}, u32[]{:S(2)}) collective-permute-start(f32[864,128]{1,0:T(8,128)S(1)} %get-tuple-element.10), channel_id=1, source_target_pairs={{4,0},{8,4},{12,8},{16,12},{20,16},{24,20},{28,24},{5,1},{9,5},{13... | collective-permute-start | bytes 1327112 | tf_op jit(solution)/shard_map/ppermute | solution.py:408
  10.2 5.8 %collective-permute-done.1.high_ref = f32[864,128]{1,0:T(8,128)S(1)} collective-permute-done((f32[864,128]{1,0:T(8,128)S(1)}, f32[864,128]{1,0:T(8,128)S(1)}, u32[]{:S(2)}, u32[]{:S(2)}) %collective-permute-start.1) | collective-permute-done | bytes 442400 | tf_op jit(solution)/shard_map/ppermute | solution.py:408
  16.0 2.5 %collective-permute-done.low_ref = f32[1632,128]{1,0:T(8,128)S(1)} collective-permute-done((f32[1632,128]{1,0:T(8,128)S(1)}, f32[1632,128]{1,0:T(8,128)S(1)}, u32[]{:S(2)}, u32[]{:S(2)}) %collective-permute-start) | collective-permute-done | bytes 835616 | tf_op jit(solution)/shard_map/ppermute | solution.py:407
  18.4 0.0 copy-done.3
  18.4 0.0 copy-done.10
  18.4 0.0 copy-done.12
  18.4 0.0 copy-done.14
  18.4 0.0 copy-start.5
  18.5 9.9 %transport.3.after_ref = f32[2048,128]{1,0:T(8,128)} custom-call(f32[4096,128]{1,0:T(8,128)S(1)} %bitcast.41, f32[64,128]{1,0:T(8,128)S(1)} %bitcast.46, f32[64,128]{1,0:T(8,128)S(1)} %bitcast.49, f32[64,128]{1,0:T(8,128)S(1)} %bitcast.52, f32[1632,128]{1,0:T(8,128)S(1)} %collective-permute-done.low_ref, f32[864,128]{1,0:T(8,128)S(1)} %collective-permute-done.1.high_ref), custom_call_target="tpu_custom_call" | custom-call | flops 104857600 | tf_op jit(solution)/shard_map/transport/pallas_call | solution.py:340
  28.4 0.0 copy-done.7
  28.4 0.0 copy-done.5
  28.4 3.7 %all-to-all-start.1 = ((f32[4,512,128]{2,1,0:T(8,128)}), f32[4,512,128]{2,1,0:T(8,128)S(1)}, u32[]{:S(2)}, u32[]{:S(2)}) async-start(f32[4,512,128]{2,1,0:T(8,128)} %bitcast.22), calls=%async_computation.1 | async-start | bytes 2097152 | tf_op jit(solution)/shard_map/all_to_all | solution.py:414
  32.1 1.1 %copy-done.6 = f32[1632,128]{1,0:T(8,128)S(1)} copy-done((f32[1632,128]{1,0:T(8,128)S(1)}, f32[1632,128]{1,0:T(8,128)}, u32[]{:S(2)}) %copy-start.6) | copy-done | bytes 835608
  33.2 1.0 %copy-done.8 = f32[864,128]{1,0:T(8,128)S(1)} copy-done((f32[864,128]{1,0:T(8,128)S(1)}, f32[864,128]{1,0:T(8,128)}, u32[]{:S(2)}) %copy-start.8) | copy-done | bytes 442392
  34.3 8.9 %transport.2 = f32[2048,128]{1,0:T(8,128)S(1)} custom-call(f32[4096,128]{1,0:T(8,128)S(1)} %bitcast.42, f32[64,128]{1,0:T(8,128)S(1)} %bitcast.47, f32[64,128]{1,0:T(8,128)S(1)} %bitcast.50, f32[64,128]{1,0:T(8,128)S(1)} %bitcast.53, f32[1632,128]{1,0:T(8,128)S(1)} %copy-done.6, f32[864,128]{1,0:T(8,128)S(1)} %copy-done.8), custom_call_target="tpu_custom_call" | custom-call | flops 104857600 | tf_op jit(solution)/shard_map/transport/pallas_call | solution.py:340
  43.2 0.0 copy-start.4
  43.2 1.0 %copy-done.4 = f32[2048,128]{1,0:T(8,128)} copy-done((f32[2048,128]{1,0:T(8,128)}, f32[2048,128]{1,0:T(8,128)S(1)}, u32[]{:S(2)}) %copy-start.4) | copy-done | bytes 1048600
  44.2 0.0 copy-start.17
  44.2 0.0 copy-start.18
  44.2 0.0 copy-start.19
  44.2 1.5 %all-to-all-done.1 = f32[4,512,128]{2,1,0:T(8,128)S(1)} async-done(((f32[4,512,128]{2,1,0:T(8,128)}), f32[4,512,128]{2,1,0:T(8,128)S(1)}, u32[]{:S(2)}, u32[]{:S(2)}) %all-to-all-start.1) | async-done | bytes 1048608 | tf_op jit(solution)/shard_map/all_to_all | solution.py:414
  45.7 4.2 %all-to-all-start = ((f32[4,512,128]{2,1,0:T(8,128)}), f32[4,512,128]{2,1,0:T(8,128)}, u32[]{:S(2)}, u32[]{:S(2)}) async-start(f32[4,512,128]{2,1,0:T(8,128)} %bitcast.44), calls=%async_computation | async-start | bytes 2097152 | tf_op jit(solution)/shard_map/all_to_all | solution.py:414
  49.9 0.0 copy-done.21
  49.9 0.1 broadcast_in_dim.7
  50.0 0.1 broadcast_in_dim.8.lit_ref.refs_2_
  50.1 0.0 copy-done.20
  50.1 0.0 copy-done.15
  50.1 0.0 copy-done.16
  50.1 0.0 copy-done.17
  50.1 0.0 copy-done.18
  50.1 0.0 copy-done.19
  50.2 3.8 %rates.1.refs_3_ = f32[12288,128]{1,0:T(8,128)S(1)} custom-call(f32[2048,128]{1,0:T(8,128)} %transport.3.after_ref, f32[16,128]{1,0:T(8,128)S(1)} %bitcast.54, f32[16,128]{1,0:T(8,128)S(1)} %bitcast.55, s32[16,128]{1,0:T(8,128)S(1)} %broadcast_in_dim.8.lit_ref.refs_2_, f32[768]{0:T(1024)S(1)} %copy-done.17, f32[768]{0:T(1024)S(1)} %copy-done.18, ...), custom_call_target="tpu_custom_call" | custom-call | flops 62914560 | tf_op jit(solution)/shard_map/rates/pallas_call | solution.py:360
  53.9 0.0 copy-start
  53.9 2.6 %copy-done = f32[12288,128]{1,0:T(8,128)} copy-done((f32[12288,128]{1,0:T(8,128)}, f32[12288,128]{1,0:T(8,128)S(1)}, u32[]{:S(2)}) %copy-start) | copy-done | bytes 6291480
  56.6 6.6 %all-to-all-done = f32[4,512,128]{2,1,0:T(8,128)} async-done(((f32[4,512,128]{2,1,0:T(8,128)}), f32[4,512,128]{2,1,0:T(8,128)}, u32[]{:S(2)}, u32[]{:S(2)}) %all-to-all-start) | async-done | bytes 1048608 | tf_op jit(solution)/shard_map/all_to_all | solution.py:414
  63.1 2.8 %copy-done.1 = f32[12288,128]{1,0:T(8,128)S(1)} copy-done((f32[12288,128]{1,0:T(8,128)S(1)}, f32[12288,128]{1,0:T(8,128)}, u32[]{:S(2)}) %copy-start.1) | copy-done | bytes 6291480
  65.9 13.4 %chemistry.1 = f32[4096,128]{1,0:T(8,128)} custom-call(f32[2048,128]{1,0:T(8,128)} %bitcast.21.refs_0_, f32[2048,128]{1,0:T(8,128)S(1)} %bitcast.43, s32[16,128]{1,0:T(8,128)S(1)} %broadcast_in_dim.8.lit_ref.refs_2_, f32[12288,128]{1,0:T(8,128)S(1)} %copy-done.1, s32[2304]{0:T(1024)S(1)} %mul.10.refs_4_), custom_call_target="tpu_custom_call" | custom-call | tf_op jit(solution)/shard_map/chemistry/pallas_call | solution.py:375
  (13 shorter events, 0.0 us)
Async XLA Ops:
  0.0 1.6 %copy-start.2 = (f32[64,2,16,256]{3,2,1,0:T(8,128)S(1)}, f32[64,2,16,256]{3,2,1,0:T(8,128)}, u32[]{:S(2)}) copy-start(f32[64,2,16,256]{3,2,1,0:T(8,128)} %param.11) | copy-start | bytes 6291460
  1.6 0.8 copy-start.9
  2.4 0.8 copy-start.11
  3.1 0.8 copy-start.13
  3.9 14.6 %copy-start.3 = (f32[64,2,16,256]{3,2,1,0:T(8,128)S(1)}, f32[64,2,16,256]{3,2,1,0:T(8,128)}, u32[]{:S(2)}) copy-start(f32[64,2,16,256]{3,2,1,0:T(8,128)} %param.11) | copy-start | bytes 6291460
  3.9 14.6 %copy-start.10 = (f32[2,16,256]{2,1,0:T(8,128)S(1)}, f32[2,16,256]{2,1,0:T(8,128)}, u32[]{:S(2)}) copy-start(f32[2,16,256]{2,1,0:T(8,128)} %param.12) | copy-start | bytes 98308
  3.9 14.6 %copy-start.12 = (f32[2,16,256]{2,1,0:T(8,128)S(1)}, f32[2,16,256]{2,1,0:T(8,128)}, u32[]{:S(2)}) copy-start(f32[2,16,256]{2,1,0:T(8,128)} %param.13) | copy-start | bytes 98308
  3.9 14.6 %copy-start.14 = (f32[2,16,256]{2,1,0:T(8,128)S(1)}, f32[2,16,256]{2,1,0:T(8,128)}, u32[]{:S(2)}) copy-start(f32[2,16,256]{2,1,0:T(8,128)} %param.14) | copy-start | bytes 98308
  4.5 14.0 %collective-permute-start = (f32[1632,128]{1,0:T(8,128)S(1)}, f32[1632,128]{1,0:T(8,128)S(1)}, u32[]{:S(2)}, u32[]{:S(2)}) collective-permute-start(f32[1632,128]{1,0:T(8,128)S(1)} %get-tuple-element.9), channel_id=1, source_target_pairs={{0,4},{4,8},{8,12},{12,16},{16,20},{20,24},{24,28},{1,5},{5,9},{9,... | collective-permute-start | bytes 2506760 | tf_op jit(solution)/shard_map/ppermute | solution.py:407
  6.5 9.4 %collective-permute-start.1 = (f32[864,128]{1,0:T(8,128)S(1)}, f32[864,128]{1,0:T(8,128)S(1)}, u32[]{:S(2)}, u32[]{:S(2)}) collective-permute-start(f32[864,128]{1,0:T(8,128)S(1)} %get-tuple-element.10), channel_id=1, source_target_pairs={{4,0},{8,4},{12,8},{16,12},{20,16},{24,20},{28,24},{5,1},{9,5},{13... | collective-permute-start | bytes 1327112 | tf_op jit(solution)/shard_map/ppermute | solution.py:408
  16.0 12.4 %copy-start.7 = (f32[864,128]{1,0:T(8,128)}, f32[864,128]{1,0:T(8,128)S(1)}, u32[]{:S(2)}) copy-start(f32[864,128]{1,0:T(8,128)S(1)} %collective-permute-done.1.high_ref) | copy-start | bytes 1327108
  18.4 9.9 %copy-start.5 = (f32[1632,128]{1,0:T(8,128)}, f32[1632,128]{1,0:T(8,128)S(1)}, u32[]{:S(2)}) copy-start(f32[1632,128]{1,0:T(8,128)S(1)} %collective-permute-done.low_ref) | copy-start | bytes 2506756
  28.4 17.3 %all-to-all-start.1 = ((f32[4,512,128]{2,1,0:T(8,128)}), f32[4,512,128]{2,1,0:T(8,128)S(1)}, u32[]{:S(2)}, u32[]{:S(2)}) async-start(f32[4,512,128]{2,1,0:T(8,128)} %bitcast.22), calls=%async_computation.1 | async-start | bytes 2097152 | tf_op jit(solution)/shard_map/all_to_all | solution.py:414
  32.1 1.1 %copy-start.6 = (f32[1632,128]{1,0:T(8,128)S(1)}, f32[1632,128]{1,0:T(8,128)}, u32[]{:S(2)}) copy-start(f32[1632,128]{1,0:T(8,128)} %copy-done.5) | copy-start | bytes 2506756
  33.2 1.0 %copy-start.8 = (f32[864,128]{1,0:T(8,128)S(1)}, f32[864,128]{1,0:T(8,128)}, u32[]{:S(2)}) copy-start(f32[864,128]{1,0:T(8,128)} %copy-done.7) | copy-start | bytes 1327108
  43.2 1.0 %copy-start.4 = (f32[2048,128]{1,0:T(8,128)}, f32[2048,128]{1,0:T(8,128)S(1)}, u32[]{:S(2)}) copy-start(f32[2048,128]{1,0:T(8,128)S(1)} %transport.2) | copy-start | bytes 3145732
  44.2 5.8 %copy-start.21 = (s32[2,4,2]{1,2,0:T(2,128)S(1)}, s32[2,4,2]{1,2,0:T(2,128)}, u32[]{:S(2)}) copy-start(s32[2,4,2]{1,2,0:T(2,128)} %param.17) | copy-start | bytes 196
  44.2 5.9 %copy-start.20 = (s32[3,768]{1,0:T(4,128)S(1)}, s32[3,768]{1,0:T(4,128)}, u32[]{:S(2)}) copy-start(s32[3,768]{1,0:T(4,128)} %param.21) | copy-start | bytes 27652
  44.2 6.0 %copy-start.15 = (f32[2,4,256]{2,1,0:T(4,128)S(1)}, f32[2,4,256]{2,1,0:T(4,128)}, u32[]{:S(2)}) copy-start(f32[2,4,256]{2,1,0:T(4,128)} %param.15) | copy-start | bytes 24580
  44.2 6.0 %copy-start.16 = (f32[2,4,256]{2,1,0:T(4,128)S(1)}, f32[2,4,256]{2,1,0:T(4,128)}, u32[]{:S(2)}) copy-start(f32[2,4,256]{2,1,0:T(4,128)} %param.16) | copy-start | bytes 24580
  44.2 6.0 %copy-start.17 = (f32[768]{0:T(1024)S(1)}, f32[768]{0:T(1024)}, u32[]{:S(2)}) copy-start(f32[768]{0:T(1024)} %rate_ref.1) | copy-start | bytes 9220
  44.2 6.0 %copy-start.18 = (f32[768]{0:T(1024)S(1)}, f32[768]{0:T(1024)}, u32[]{:S(2)}) copy-start(f32[768]{0:T(1024)} %barrier_ref.1) | copy-start | bytes 9220
  44.2 6.0 %copy-start.19 = (f32[768]{0:T(1024)S(1)}, f32[768]{0:T(1024)}, u32[]{:S(2)}) copy-start(f32[768]{0:T(1024)} %photo_ref.1) | copy-start | bytes 9220
  45.7 17.5 %all-to-all-start = ((f32[4,512,128]{2,1,0:T(8,128)}), f32[4,512,128]{2,1,0:T(8,128)}, u32[]{:S(2)}, u32[]{:S(2)}) async-start(f32[4,512,128]{2,1,0:T(8,128)} %bitcast.44), calls=%async_computation | async-start | bytes 2097152 | tf_op jit(solution)/shard_map/all_to_all | solution.py:414
  53.9 2.6 %copy-start = (f32[12288,128]{1,0:T(8,128)}, f32[12288,128]{1,0:T(8,128)S(1)}, u32[]{:S(2)}) copy-start(f32[12288,128]{1,0:T(8,128)S(1)} %rates.1.refs_3_) | copy-start | bytes 18874372
  63.1 2.8 %copy-start.1 = (f32[12288,128]{1,0:T(8,128)S(1)}, f32[12288,128]{1,0:T(8,128)}, u32[]{:S(2)}) copy-start(f32[12288,128]{1,0:T(8,128)} %copy-done) | copy-start | bytes 18874372

commit v4 on v3

v4 whole, which is shorter than its diff:
```python
import functools

import jax
import jax.numpy as jnp
from jax import lax
from jax.experimental import pallas as pl
from jax.experimental.pallas import tpu as pltpu
from jax.sharding import PartitionSpec as P


SECTIONS = 3
DAY_STEPS = 2
LANES = 128
SUB = 8
LOW = 2 * SECTIONS
HIGH = SECTIONS
PARTS = 2
TOGETHER = 8
CHUNK = 8
BATCHES = 4
LOG2E = 1.4426950408889634


def flat_rows(cells):
    *lead, rows, width = cells.shape
    sub = min(rows, SUB)
    split = cells.reshape(*lead, rows // sub, sub, width // LANES, LANES)
    return jnp.moveaxis(split, -2, -3).reshape(-1, LANES)


class Sizes:
    def __init__(self, field, groups):
        self.species, self.levels, self.rows, self.width = field.shape
        self.tiles = self.width // LANES
        self.groups = groups
        self.part = self.rows // groups
        self.blocks = self.levels * self.tiles * self.part
        self.stride = self.levels * self.rows * self.tiles
        self.columns = self.levels * self.tiles
        self.count = self.species // PARTS
        self.low_rows = LOW * self.columns * self.species
        self.high_rows = HIGH * self.columns * self.species
        self.span = self.rows + 2 * SUB
        self.edge_rows = 3 * self.columns * SUB

    def source_row(self, level, row, tile):
        return ((level * (self.rows // SUB) + row // SUB) * self.tiles + tile) * SUB + row % SUB

    def pairs(self):
        return [(level, tile) for level in range(self.levels) for tile in range(self.tiles)]


def middle(a, b):
    return jnp.maximum(jnp.minimum(a, b), jnp.minimum(jnp.maximum(a, b), 0.0))


def shift_columns(parts, amount):
    if amount > 0:
        return [pltpu.roll(parts[-1], 1, 1)] + parts[:-1]
    return parts[1:] + [pltpu.roll(parts[0], LANES - 1, 1)]


def spread_matrix(tiles, back):
    natural = lax.broadcasted_iota(jnp.int32, (tiles * LANES, tiles * LANES), 1 if back else 0)
    spread = lax.broadcasted_iota(jnp.int32, (tiles * LANES, tiles * LANES), 0 if back else 1)
    hit = natural == (spread % LANES) * tiles + spread // LANES
    return jnp.where(hit, 1.0, 0.0).astype(jnp.bfloat16)


def reorder(parts, matrix):
    x = jnp.concatenate(parts, axis=1)
    total = None
    for _ in range(3):
        piece = x.astype(jnp.bfloat16)
        x = x - piece.astype(jnp.float32)
        term = jnp.dot(piece, matrix, preferred_element_type=jnp.float32)
        total = term if total is None else total + term
    return [total[:, k * LANES : (k + 1) * LANES] for k in range(len(parts))]


def pack_kernel(z, x_ref, courant_ref, low_ref, high_ref, courant_out, *fields):
    forth = spread_matrix(z.tiles, False)

    def spread(flat, strips):
        split = flat.reshape(strips, z.rows // SUB, z.tiles, SUB, LANES)
        return reorder([split[:, :, t].reshape(strips * z.rows, LANES) for t in range(z.tiles)], forth)

    parts = spread(courant_ref[...], 3 * z.levels)
    shifted = shift_columns(parts, -1)
    for strip in range(3 * z.levels):
        rows = slice(strip * z.rows, (strip + 1) * z.rows)
        for tile in range(z.tiles):
            value = (shifted if strip // z.levels == 1 else parts)[tile][rows]
            col = strip * z.tiles + tile
            courant_out[pl.ds(col * z.rows, z.rows), :] = value
            low_ref[pl.ds(z.low_rows + col * SUB, SUB), :] = value[z.rows - SUB :]
            high_ref[pl.ds(z.high_rows + col * SUB, SUB), :] = value[:SUB]

    for part, field in enumerate(fields):

        def some(index, carry):
            strips = CHUNK * z.levels
            size = strips * z.tiles * z.rows
            start = pl.multiple_of((part * (z.count // CHUNK) + index) * size, SUB)
            values = spread(x_ref[pl.ds(start, size), :], strips)
            for strip in range(strips):
                for tile in range(z.tiles):
                    at = pl.multiple_of(index * size + (strip * z.tiles + tile) * z.rows, SUB)
                    field[pl.ds(at, z.rows), :] = values[tile][strip * z.rows : (strip + 1) * z.rows]
            return carry

        lax.fori_loop(0, z.count // CHUNK, some, 0)

        def edges(index, carry):
            for col in range(z.columns):
                source = (index * z.columns + col) * z.rows
                target = (part * z.count + index) * z.columns + col
                low_ref[pl.ds(target * LOW, LOW), :] = field[pl.ds(source + z.rows - LOW, LOW), :]
                high_ref[pl.ds(target * HIGH, HIGH), :] = field[pl.ds(source, HIGH), :]
            return carry

        lax.fori_loop(0, z.count, edges, 0, unroll=4)


def transport_kernel(z, part, field_in, courant_in, low_in, high_in, out_ref, coef, final, *scratch):
    span = z.span
    cols = range(z.columns)
    slots, scratch = scratch[: 4 * TOGETHER], scratch[4 * TOGETHER :]
    if part == 0:
        field_ref, courant_ref, low_ref, high_ref = field_in, courant_in, low_in, high_in
        low_edge, high_edge = low_in.at[pl.ds(z.low_rows, z.edge_rows)], high_in.at[pl.ds(z.high_rows, z.edge_rows)]
    else:
        field_ref, courant_ref, low_ref, high_ref, low_edge, high_edge, sems = scratch
        fixed = [
            pltpu.make_async_copy(courant_in, courant_ref, sems.at[0, 0]),
            pltpu.make_async_copy(low_in.at[pl.ds(z.low_rows, z.edge_rows)], low_edge, sems.at[0, 1]),
            pltpu.make_async_copy(high_in.at[pl.ds(z.high_rows, z.edge_rows)], high_edge, sems.at[0, 2]),
        ]

        def pieces(index):
            result = []
            for k, (source, target, rows, first) in enumerate(
                (
                    (field_in, field_ref, z.rows, 0),
                    (low_in, low_ref, LOW, part * z.count),
                    (high_in, high_ref, HIGH, part * z.count),
                )
            ):
                size = TOGETHER * z.columns * rows
                here = pl.ds(pl.multiple_of(index * size, SUB), size)
                there = pl.ds(pl.multiple_of(index * size + first * z.columns * rows, SUB), size)
                result.append(pltpu.make_async_copy(source.at[there], target.at[here], sems.at[index + 1, k]))
            return result

        for copy in fixed:
            copy.start()
        for index in range(z.count // TOGETHER):
            for copy in pieces(index):
                copy.start()
        for copy in fixed:
            copy.wait()

    def coef_row(kind, which, col, j):
        return ((kind * 2 + which) * z.columns + col) * span + j

    for kind in range(3):
        for col in cols:
            one = kind * z.columns + col
            tiles = [low_edge[pl.ds(one * SUB, SUB), :]]
            tiles += [courant_ref[pl.ds(one * z.rows + row, SUB), :] for row in range(0, z.rows, SUB)]
            tiles += [high_edge[pl.ds(one * SUB, SUB), :]]
            for k, value in enumerate(tiles):
                coef[pl.ds(coef_row(kind, 0, col, k * SUB), SUB), :] = value
                coef[pl.ds(coef_row(kind, 1, col, k * SUB), SUB), :] = 0.5 * value * (1.0 - value)

    def weights(kind, col, j):
        return [coef[pl.ds(coef_row(kind, which, col, j), SUB), :] for which in range(2)]

    def one_species(index, start, fields, fluxes):
        for col in cols:
            base = index * z.columns + col
            at = col * span + SUB
            start[pl.ds(at - LOW, LOW), :] = low_ref[pl.ds(base * LOW, LOW), :]
            start[pl.ds(at + z.rows, HIGH), :] = high_ref[pl.ds(base * HIGH, HIGH), :]
            start[pl.ds(at, z.rows), :] = field_ref[pl.ds(pl.multiple_of(base * z.rows, SUB), z.rows), :]
        for step in range(SECTIONS):
            write = fields[step % 2]
            source = start if step == 0 else fields[(step + 1) % 2]
            read = lambda col, j, ref=source: ref[pl.ds(col * span + j, SUB), :]
            bottom = SUB - LOW + 2 * (step + 1)
            top = SUB + z.rows + HIGH - (step + 1)
            for j in range(bottom - 1, top, SUB):
                for col in cols:
                    below, here, above = [read(col, j + k) for k in (-1, 0, 1)]
                    a, b = weights(0, col, j + 1)
                    fluxes[pl.ds(col * span + j, SUB), :] = a * here + b * middle(here - below, above - here)
            for j in range(bottom, top, SUB):
                c = []
                for col in cols:
                    leave = fluxes[pl.ds(col * span + j, SUB), :]
                    enter = fluxes[pl.ds(col * span + j - 1, SUB), :]
                    c.append(read(col, j) - (leave - enter))
                for level in range(z.levels):
                    mine = slice(level * z.tiles, (level + 1) * z.tiles)
                    row = c[mine]
                    back = [v - w for v, w in zip(row, shift_columns(row, 1))]
                    ahead = shift_columns(back, -1)
                    leave = []
                    for tile in range(z.tiles):
                        a, b = weights(1, level * z.tiles + tile, j)
                        leave.append(a * row[tile] + b * middle(back[tile], ahead[tile]))
                    enter = shift_columns(leave, 1)
                    c[mine] = [row[t] - (leave[t] - enter[t]) for t in range(z.tiles)]
                for tile in range(z.tiles):
                    column = [c[level * z.tiles + tile] for level in range(z.levels)]
                    steps = [column[0]]
                    steps += [column[k + 1] - column[k] for k in range(z.levels - 1)]
                    steps += [-column[-1]]
                    lift = None
                    for level in range(z.levels):
                        col = level * z.tiles + tile
                        a, b = weights(2, col, j)
                        rising = a * column[level] + b * middle(steps[level], steps[level + 1])
                        net = rising if lift is None else rising - lift
                        lift = rising
                        value = column[level] - net
                        if step < SECTIONS - 1:
                            write[pl.ds(col * span + j, SUB), :] = value
                        else:
                            base = (index * z.columns + col) * z.rows + j - SUB
                            final[pl.ds(pl.multiple_of(base, SUB), SUB), :] = value

    def some_species(index, carry):
        if part > 0:
            for copy in pieces(index):
                copy.wait()
        for k in range(TOGETHER):
            one_species(index * TOGETHER + k, slots[4 * k], slots[4 * k + 1 : 4 * k + 3], slots[4 * k + 3])
        return carry

    lax.fori_loop(0, z.count // TOGETHER, some_species, 0)

    back = spread_matrix(z.tiles, True)

    def scatter(index, carry):
        many = CHUNK * z.levels
        size = many * z.tiles * z.rows
        whole = final[pl.ds(pl.multiple_of(index * size, SUB), size), :].reshape(many, z.tiles, z.rows, LANES)
        parts = reorder([whole[:, t].reshape(many * z.rows, LANES) for t in range(z.tiles)], back)
        for one in range(many):
            k, level = divmod(one, z.levels)
            for tile in range(z.tiles):
                for group in range(z.groups):
                    start = one * z.rows + group * z.part
                    at = (group * z.count + index * CHUNK + k) * z.blocks + (level * z.tiles + tile) * z.part
                    out_ref[pl.ds(at, z.part), :] = parts[tile][start : start + z.part]
        return carry

    lax.fori_loop(0, z.count // CHUNK, scatter, 0)


def rates_kernel(pieces, after_ref, warm_ref, glow_ref, lit_ref, rate_ref, barrier_ref, photo_ref, out_ref):
    step = pl.program_id(0)
    many = out_ref.shape[0] // (pieces * SUB)
    warm = [(1.0 - warm_ref[pl.ds(p * SUB, SUB), :]) * LOG2E for p in range(pieces)]
    glow = [
        jnp.where(lit_ref[pl.ds(p * SUB, SUB), :] == 1, glow_ref[pl.ds(p * SUB, SUB), :], 0.0)
        for p in range(pieces)
    ]

    def one(i, carry):
        r = step * many + i
        for p in range(pieces):
            at = pl.ds(pl.multiple_of(i * pieces * SUB, SUB) + p * SUB, SUB)
            out_ref[at, :] = rate_ref[r] * jnp.exp2(barrier_ref[r] * warm[p]) + photo_ref[r] * glow[p]
        return carry

    lax.fori_loop(0, many, one, 0, unroll=8)


def chemistry_kernel(z, species, *refs):
    pieces = z.blocks // SUB
    sources, (lit_ref, k_hbm, table_ref, out_ref) = refs[:PARTS], refs[PARTS : PARTS + 4]
    parts, (k_ref, state, made, lost_a, lost_b, sems) = refs[PARTS + 4 : 2 * PARTS + 4], refs[2 * PARTS + 4 :]
    reactions = k_ref.shape[0] // z.blocks
    batch = reactions // BATCHES
    loads = [pltpu.make_async_copy(a, b, sems.at[i]) for i, (a, b) in enumerate(zip(sources, parts))]
    for i in range(BATCHES):
        at = pl.ds(i * batch * z.blocks, batch * z.blocks)
        loads.append(pltpu.make_async_copy(k_hbm.at[at], k_ref.at[at], sems.at[PARTS + i]))
    for load in loads:
        load.start()

    def cell(row, piece):
        return pl.ds(pl.multiple_of(row, SUB) + piece * SUB, SUB)

    lit = [lit_ref[pl.ds(p * SUB, SUB), :] == 1 for p in range(pieces)]
    steps = [jnp.where(lit[p], float(DAY_STEPS), 1.0) for p in range(pieces)]
    zero = jnp.zeros((SUB, LANES), jnp.float32)

    def prepare(at, p, value):
        made[at, :] = steps[p] * value
        lost_a[at, :] = steps[p]
        lost_b[at, :] = zero

    for part, ref in enumerate(parts):
        loads[part].wait()

        def begin(index, carry):
            for group in range(z.groups):
                for p in range(pieces):
                    value = ref[cell((group * z.count + index) * z.blocks, p), :]
                    at = cell((group * z.species + part * z.count + index) * z.blocks, p)
                    state[at, :] = value
                    prepare(at, p, value)
            return carry

        lax.fori_loop(0, z.count, begin, 0)

    def react(r, carry):
        first, second, product = table_ref[r], table_ref[reactions + r], table_ref[2 * reactions + r]
        for p in range(pieces):
            k = k_ref[cell(r * z.blocks, p), :]
            x = state[cell(first, p), :]
            y = state[cell(second, p), :]
            kx = k * x
            ky = k * y
            made[cell(product, p), :] += kx * y
            lost_a[cell(first, p), :] += ky
            lost_b[cell(second, p), :] += kx
        return carry

    for sub in range(DAY_STEPS):
        if sub == 0:
            for i in range(BATCHES):
                loads[PARTS + i].wait()
                lax.fori_loop(i * batch, (i + 1) * batch, react, 0, unroll=16)
        else:
            lax.fori_loop(0, reactions, react, 0, unroll=16)

        def finish(s, carry):
            for p in range(pieces):
                at = cell(s * z.blocks, p)
                value = made[at, :] / (lost_a[at, :] + lost_b[at, :])
                if sub < DAY_STEPS - 1:
                    prepare(at, p, value)
                    if sub == 0:
                        state[at, :] = value
                if sub > 0:
                    value = jnp.where(lit[p], value, state[at, :])
                    out_ref[at, :] = value
            return carry

        lax.fori_loop(0, species, finish, 0, unroll=4)


VMEM = pl.BlockSpec(memory_space=pltpu.VMEM)
SMEM = pl.BlockSpec(memory_space=pltpu.SMEM)


def rows_of(count):
    return jax.ShapeDtypeStruct((count, LANES), jnp.float32)


ANY = pl.BlockSpec(memory_space=pl.ANY)
HBM = pl.BlockSpec(memory_space=pltpu.HBM)


def pack(z, *flat):
    part = rows_of(z.count * z.columns * z.rows)
    return pl.pallas_call(
        functools.partial(pack_kernel, z),
        out_shape=(
            rows_of(z.low_rows + z.edge_rows),
            rows_of(z.high_rows + z.edge_rows),
            rows_of(3 * z.columns * z.rows),
        )
        + (part,) * PARTS,
        in_specs=[VMEM] * 2,
        out_specs=(VMEM,) * (3 + PARTS),
        compiler_params=pltpu.CompilerParams(vmem_limit_bytes=16 << 20),
        name="pack",
    )(*flat)


def transport(z, part, *flat):
    rows = [z.count * z.columns * k for k in (z.rows, LOW, HIGH)]
    size = z.span * z.columns
    scratch = [6 * size, z.count * z.columns * z.rows] + [size] * (4 * TOGETHER)
    params = {}
    if part == 0:
        params["vmem_limit_bytes"] = 24 << 20
    else:
        scratch += [rows[0], 3 * z.columns * z.rows, rows[1], rows[2], z.edge_rows, z.edge_rows]
    scratch = [pltpu.VMEM((n, LANES), jnp.float32) for n in scratch]
    if part > 0:
        scratch += [pltpu.SemaphoreType.DMA((z.count // TOGETHER + 1, 3))]
    return pl.pallas_call(
        functools.partial(transport_kernel, z, part),
        out_shape=rows_of(z.groups * z.count * z.blocks),
        in_specs=[VMEM if part == 0 else ANY] * 4,
        out_specs=VMEM,
        scratch_shapes=scratch,
        compiler_params=pltpu.CompilerParams(**params),
        cost_estimate=pl.CostEstimate(flops=400 * z.count * z.stride * LANES, bytes_accessed=0, transcendentals=0),
        name="transport",
    )(*flat)


def rates(z, after, warm, glow, lit, rate, barrier, photo):
    reactions = rate.shape[0]
    whole = lambda i: (0, 0)
    cells = pl.BlockSpec((z.blocks, LANES), whole)
    return pl.pallas_call(
        functools.partial(rates_kernel, z.blocks // SUB),
        out_shape=rows_of(reactions * z.blocks),
        grid=(BATCHES,),
        in_specs=[ANY] + [cells] * 3 + [SMEM] * 3,
        out_specs=pl.BlockSpec((reactions // BATCHES * z.blocks, LANES), lambda i: (i, 0)),
        cost_estimate=pl.CostEstimate(
            flops=40 * reactions * z.blocks * LANES, bytes_accessed=0, transcendentals=0
        ),
        name="rates",
    )(after, warm, glow, lit, rate, barrier, photo)


def chemistry(z, species, k, *args):
    size = species * z.blocks
    scratch = [size // PARTS] * PARTS + [k.shape[0]] + [size] * 4
    scratch = [pltpu.VMEM((n, LANES), jnp.float32) for n in scratch]
    parts, (lit, table) = args[:PARTS], args[PARTS:]
    return pl.pallas_call(
        functools.partial(chemistry_kernel, z, species),
        out_shape=rows_of(size),
        in_specs=[ANY] * PARTS + [VMEM, ANY, SMEM],
        out_specs=VMEM,
        scratch_shapes=scratch + [pltpu.SemaphoreType.DMA((PARTS + BATCHES,))],
        name="chemistry",
    )(*parts, lit, k, table)


def body(
    mixing_ratio_field,
    eastward_face_cfl,
    northward_face_cfl,
    upward_face_cfl,
    thermal_anomaly,
    radiant_flux,
    daylight_mask,
    baseline_kinetic_coefficient,
    arrhenius_barrier,
    photodissociation_factor,
    stoichiometry_table,
):
    groups = lax.axis_size("tracer")
    strips = lax.axis_size("space")
    z = Sizes(mixing_ratio_field, groups)
    courant = jnp.stack([eastward_face_cfl, northward_face_cfl, upward_face_cfl])
    low, high, courant, *fields = pack(z, flat_rows(mixing_ratio_field), flat_rows(courant))
    mask, table, _ = lax.optimization_barrier((daylight_mask, stoichiometry_table, courant))
    lit = jnp.broadcast_to(jnp.moveaxis(mask, 2, 1).reshape(z.blocks, 1), (z.blocks, LANES))
    k = rates(
        z,
        courant,
        flat_rows(thermal_anomaly),
        flat_rows(radiant_flux),
        lit,
        baseline_kinetic_coefficient,
        arrhenius_barrier,
        photodissociation_factor,
    )
    table = table.reshape(-1) * z.blocks
    low = lax.ppermute(low, "space", [(i, i + 1) for i in range(strips - 1)])
    high = lax.ppermute(high, "space", [(i + 1, i) for i in range(strips - 1)])
    low, high, k, lit, table = lax.optimization_barrier((low, high, k, lit, table))
    species = z.species * groups
    arrived = []
    moved = low
    for part in range(PARTS):
        field, _ = lax.optimization_barrier((fields[part], moved))
        moved = transport(z, part, field, courant, low, high)
        regrouped = lax.all_to_all(
            moved.reshape(groups, z.count * z.blocks, LANES), "tracer", split_axis=0, concat_axis=0, tiled=True
        )
        arrived.append(regrouped.reshape(species // PARTS * z.blocks, LANES))
    out = chemistry(z, species, k, *arrived, lit, table)
    out = out.reshape(species, z.levels, z.tiles, z.part, LANES)
    return jnp.moveaxis(out, 2, 3).reshape(species, z.levels, z.part, z.width)


def solution(mesh):
    placed = (
        P("tracer", None, "space", None),
        P(None, "space", None),
        P(None, "space", None),
        P(None, "space", None),
        P(None, ("space", "tracer"), None),
        P(None, ("space", "tracer"), None),
        P(None, ("space", "tracer"), None),
        P(),
        P(),
        P(),
        P(),
    )
    return jax.shard_map(
        body,
        mesh=mesh,
        in_specs=placed,
        out_specs=P(None, None, ("space", "tracer"), None),
        check_vma=False,
    )
```

time: 80 us -> 87.5 us (1.094)
  blocking collectives: 0 us -> 35 us
  waiting for transfers between devices: 16.3 us -> 1.01 us
  starting transfers between devices: 13.6 us -> 5.55 us
  local copies, waits for them, and re-layouts: 12.6 us -> 4.58 us
  Pallas kernels: 36.6 us -> 40 us
    all_to_all x0 -> x2, blocking collectives: none -> 35 us  [body(): lax.all_to_all(moved.reshape(groups, z.count * z.blocks, LANES), 'tracer'...]
    unnamed x44 -> x16, local copies, waits for them, and re-layouts: 12.5 us -> 3.22 us
    all_to_all x2 -> x0, waiting for transfers between devices: 8.02 us -> none  [body(): lax.all_to_all(moved.reshape(groups, count * z.blocks, LANES), 'tracer',...]
    all_to_all x2 -> x0, starting transfers between devices: 7.95 us -> none  [body(): lax.all_to_all(moved.reshape(groups, count * z.blocks, LANES), 'tracer',...]
    ppermute x1, waiting for transfers between devices: 5.8 us -> 0.01 us  [body(): high = lax.ppermute(high, 'space', [(i + 1, i) for i in range(strips - 1)])]
    pallas_call x1, Pallas kernels: 0.56 us -> 3.57 us  [pack(): pl.pallas_call(functools.partial(pack_kernel, z), out_shape=(rows_of(z.lo...]
    pallas_call x2, Pallas kernels: 18.8 us -> 16.1 us  [transport(): pl.pallas_call(functools.partial(transport_kernel, z, part), out_shape=ro...]
    pallas_call x1, Pallas kernels: 3.76 us -> 5.86 us  [rates(): pl.pallas_call(functools.partial(rates_kernel, z.blocks // SUB), out_shap...]
  transfers between devices with their start and end apart: 4 -> 2, of which waited for: 4 -> 1; matrix products, arithmetic and copies ran while one was open for 0% -> 2% of each run, Pallas kernels for 16% -> 7%
where the time goes in v4:
time: 87.5 us; the launch traced here: 87.1 us
  Pallas kernels  40 us (46%)
  blocking collectives  35 us (40%)
  starting transfers between devices  5.55 us (6%)
  local copies, waits for them, and re-layouts  4.58 us (5%)
  waiting for transfers between devices  1.01 us (1%)
    all_to_all x2, blocking collectives, body(): lax.all_to_all(moved.reshape(groups, z.count * z.blocks, LANES), 'tracer'...  35 us
    pallas_call x2, Pallas kernels, transport(): pl.pallas_call(functools.partial(transport_kernel, z, part), out_shape=ro...  16.1 us
    pallas_call x1, Pallas kernels, chemistry(): pl.pallas_call(functools.partial(chemistry_kernel, z, species), out_shape...  14.5 us
    pallas_call x1, Pallas kernels, rates(): pl.pallas_call(functools.partial(rates_kernel, z.blocks // SUB), out_shap...  5.86 us
    ppermute x1, starting transfers between devices, body(): high = lax.ppermute(high, 'space', [(i + 1, i) for i in range(strips - 1)])  3.64 us
    pallas_call x1, Pallas kernels, pack(): pl.pallas_call(functools.partial(pack_kernel, z), out_shape=(rows_of(z.lo...  3.57 us
    unnamed x16, local copies, waits for them, and re-layouts  3.22 us
    ppermute x1, starting transfers between devices, body(): low = lax.ppermute(low, 'space', [(i, i + 1) for i in range(strips - 1)])  1.91 us
  transfers between devices with their start and end apart: 2, of which 1 were waited for; matrix products, arithmetic and copies ran while one was open for 2% of the time, Pallas kernels for 7%

profile of v4, /device:TPU:16, one launch (start us, length us, event | category | flops | bytes accessed | tf_op | source)
XLA Modules:
  0.0 87.1 jit_solution(451451598064423771)
XLA Ops:
  0.0 0.0 copy-start.6
  0.0 0.0 copy-start.7
  0.0 0.8 pad_maximum_fusion
  0.8 0.0 copy-start.1
  0.8 1.6 %copy-done.1 = f32[64,2,16,256]{3,2,1,0:T(8,128)S(1)} copy-done((f32[64,2,16,256]{3,2,1,0:T(8,128)S(1)}, f32[64,2,16,256]{3,2,1,0:T(8,128)}, u32[]{:S(2)}) %copy-start.1) | copy-done | bytes 2097176
  2.4 3.6 %pack.1 = (f32[1632,128]{1,0:T(8,128)S(1)}, f32[864,128]{1,0:T(8,128)}, f32[192,128]{1,0:T(8,128)S(1)}, f32[2048,128]{1,0:T(8,128)S(1)}, f32[2048,128]{1,0:T(8,128)S(1)}) custom-call(f32[4096,128]{1,0:T(8,128)S(1)} %bitcast.32, f32[192,128]{1,0:T(8,128)S(1)} %bitcast.33), custom_call_target="tpu_custom_call" | custom-call | tf_op jit(solution)/shard_map/pack/pallas_call | solution.py:371
  6.0 0.0 copy-start.3
  6.0 1.0 %copy-done.3 = f32[2048,128]{1,0:T(8,128)} copy-done((f32[2048,128]{1,0:T(8,128)}, f32[2048,128]{1,0:T(8,128)S(1)}, u32[]{:S(2)}) %copy-start.3) | copy-done | bytes 1048600
  7.0 0.0 copy-start.4
  7.0 0.6 copy-done.4
  7.6 1.9 %collective-permute-start = (f32[1632,128]{1,0:T(8,128)S(1)}, f32[1632,128]{1,0:T(8,128)S(1)}, u32[]{:S(2)}, u32[]{:S(2)}) collective-permute-start(f32[1632,128]{1,0:T(8,128)S(1)} %get-tuple-element.20), channel_id=1, source_target_pairs={{0,4},{4,8},{8,12},{12,16},{16,20},{20,24},{24,28},{1,5},{5,9},{9,... | collective-permute-start | bytes 2506760 | tf_op jit(solution)/shard_map/ppermute | solution.py:473
  9.5 3.6 %collective-permute-start.1 = (f32[864,128]{1,0:T(8,128)}, f32[864,128]{1,0:T(8,128)S(1)}, u32[]{:S(2)}, u32[]{:S(2)}) collective-permute-start(f32[864,128]{1,0:T(8,128)} %get-tuple-element.21), channel_id=1, source_target_pairs={{4,0},{8,4},{12,8},{16,12},{20,16},{24,20},{28,24},{5,1},{9,5},{13... | collective-permute-start | bytes 1327112 | tf_op jit(solution)/shard_map/ppermute | solution.py:474
  13.2 0.0 copy-done.7
  13.2 0.1 broadcast_in_dim.7
  13.3 0.0 copy-done.6
  13.3 0.6 mul.11.refs_4_
  13.9 0.7 broadcast_in_dim.8.lit_ref.refs_2_
  14.6 0.0 copy-start.5
  14.6 5.9 %rates.1.refs_3_ = f32[12288,128]{1,0:T(8,128)} custom-call(f32[192,128]{1,0:T(8,128)} %copy-done.4, f32[16,128]{1,0:T(8,128)} %bitcast.40, f32[16,128]{1,0:T(8,128)} %bitcast.41, s32[16,128]{1,0:T(8,128)} %broadcast_in_dim.8.lit_ref.refs_2_, f32[768]{0:T(1024)} %rate_ref.1, f32[768]{0:T(1024)} %barrier_ref.1, f32[768]{0:T(1024)} %photo_ref.1), custom_call_target="tpu_custom_call" | custom-call | flops 62914560 | tf_op jit(solution)/shard_map/rates/pallas_call | solution.py:414
  20.4 0.0 collective-permute-done.1.high_in
  20.4 0.0 copy-start.2
  20.4 1.0 %collective-permute-done.low_in = f32[1632,128]{1,0:T(8,128)S(1)} collective-permute-done((f32[1632,128]{1,0:T(8,128)S(1)}, f32[1632,128]{1,0:T(8,128)S(1)}, u32[]{:S(2)}, u32[]{:S(2)}) %collective-permute-start) | collective-permute-done | bytes 835616 | tf_op jit(solution)/shard_map/ppermute | solution.py:473
  21.4 0.0 copy-start
  21.4 0.0 copy-done.5
  21.4 6.9 %transport.2 = f32[2048,128]{1,0:T(8,128)S(1)} custom-call(f32[2048,128]{1,0:T(8,128)S(1)} %get-tuple-element.26.field_in, f32[192,128]{1,0:T(8,128)S(1)} %copy-done.5, f32[1632,128]{1,0:T(8,128)S(1)} %collective-permute-done.low_in, f32[864,128]{1,0:T(8,128)S(1)} %collective-permute-done.1.high_in), custom_call_target="tpu_custom_call" | custom-call | flops 104857600 | tf_op jit(solution)/shard_map/transport/pallas_call | solution.py:398
  28.4 0.0 copy-done.2
  28.4 0.0 copy-done
  28.4 9.2 %transport.3 = f32[2048,128]{1,0:T(8,128)} custom-call(f32[2048,128]{1,0:T(8,128)} %copy-done.3, f32[192,128]{1,0:T(8,128)} %copy-done.4, f32[1632,128]{1,0:T(8,128)} %copy-done, f32[864,128]{1,0:T(8,128)} %copy-done.2), custom_call_target="tpu_custom_call" | custom-call | flops 104857600 | tf_op jit(solution)/shard_map/transport/pallas_call | solution.py:398
  37.6 18.8 %all_to_all.10 = f32[4,512,128]{2,1,0:T(8,128)} all-to-all(f32[4,512,128]{2,1,0:T(8,128)} %bitcast.36), channel_id=1, replica_groups=mesh['space'=8,'tracer'=4] {'tracer'}, dimensions={0} | all-to-all | bytes 2097152 | tf_op jit(solution)/shard_map/all_to_all | solution.py:482
  56.4 16.2 %all_to_all.11 = f32[4,512,128]{2,1,0:T(8,128)} all-to-all(f32[4,512,128]{2,1,0:T(8,128)S(1)} %bitcast.31), channel_id=1, replica_groups=mesh['space'=8,'tracer'=4] {'tracer'}, dimensions={0} | all-to-all | bytes 2097152 | tf_op jit(solution)/shard_map/all_to_all | solution.py:482
  72.6 14.5 %chemistry.1 = f32[4096,128]{1,0:T(8,128)} custom-call(f32[2048,128]{1,0:T(8,128)} %bitcast.35, f32[2048,128]{1,0:T(8,128)} %bitcast.34, s32[16,128]{1,0:T(8,128)} %broadcast_in_dim.8.lit_ref.refs_2_, f32[12288,128]{1,0:T(8,128)} %rates.1.refs_3_, s32[2304]{0:T(1024)} %mul.11.refs_4_), custom_call_target="tpu_custom_call" | custom-call | tf_op jit(solution)/shard_map/chemistry/pallas_call | solution.py:432
  (1 shorter events, 0.0 us)
Async XLA Ops:
  0.0 13.3 %copy-start.6 = (s32[3,768]{1,0:T(4,128)S(1)}, s32[3,768]{1,0:T(4,128)}, u32[]{:S(2)}) copy-start(s32[3,768]{1,0:T(4,128)} %param.21) | copy-start | bytes 27652
  0.0 13.2 %copy-start.7 = (s32[2,4,2]{1,2,0:T(2,128)S(1)}, s32[2,4,2]{1,2,0:T(2,128)}, u32[]{:S(2)}) copy-start(s32[2,4,2]{1,2,0:T(2,128)} %param.17) | copy-start | bytes 196
  0.8 1.6 %copy-start.1 = (f32[64,2,16,256]{3,2,1,0:T(8,128)S(1)}, f32[64,2,16,256]{3,2,1,0:T(8,128)}, u32[]{:S(2)}) copy-start(f32[64,2,16,256]{3,2,1,0:T(8,128)} %param.11) | copy-start | bytes 6291460
  6.0 1.0 %copy-start.3 = (f32[2048,128]{1,0:T(8,128)}, f32[2048,128]{1,0:T(8,128)S(1)}, u32[]{:S(2)}) copy-start(f32[2048,128]{1,0:T(8,128)S(1)} %get-tuple-element.29.field_in) | copy-start | bytes 3145732
  7.0 0.6 copy-start.4
  7.6 13.8 %collective-permute-start = (f32[1632,128]{1,0:T(8,128)S(1)}, f32[1632,128]{1,0:T(8,128)S(1)}, u32[]{:S(2)}, u32[]{:S(2)}) collective-permute-start(f32[1632,128]{1,0:T(8,128)S(1)} %get-tuple-element.20), channel_id=1, source_target_pairs={{0,4},{4,8},{8,12},{12,16},{16,20},{20,24},{24,28},{1,5},{5,9},{9,... | collective-permute-start | bytes 2506760 | tf_op jit(solution)/shard_map/ppermute | solution.py:473
  9.5 10.9 %collective-permute-start.1 = (f32[864,128]{1,0:T(8,128)}, f32[864,128]{1,0:T(8,128)S(1)}, u32[]{:S(2)}, u32[]{:S(2)}) collective-permute-start(f32[864,128]{1,0:T(8,128)} %get-tuple-element.21), channel_id=1, source_target_pairs={{4,0},{8,4},{12,8},{16,12},{20,16},{24,20},{28,24},{5,1},{9,5},{13... | collective-permute-start | bytes 1327112 | tf_op jit(solution)/shard_map/ppermute | solution.py:474
  14.6 6.9 %copy-start.5 = (f32[192,128]{1,0:T(8,128)S(1)}, f32[192,128]{1,0:T(8,128)}, u32[]{:S(2)}) copy-start(f32[192,128]{1,0:T(8,128)} %copy-done.4) | copy-start | bytes 294916
  20.4 8.0 %copy-start.2 = (f32[864,128]{1,0:T(8,128)}, f32[864,128]{1,0:T(8,128)S(1)}, u32[]{:S(2)}) copy-start(f32[864,128]{1,0:T(8,128)S(1)} %collective-permute-done.1.high_in) | copy-start | bytes 1327108
  21.4 6.9 %copy-start = (f32[1632,128]{1,0:T(8,128)}, f32[1632,128]{1,0:T(8,128)S(1)}, u32[]{:S(2)}) copy-start(f32[1632,128]{1,0:T(8,128)S(1)} %collective-permute-done.low_in) | copy-start | bytes 2506756

commit v5 on v3

v5 whole, which is shorter than its diff:
```python
import functools

import jax
import jax.numpy as jnp
from jax import lax
from jax.experimental import pallas as pl
from jax.experimental.pallas import tpu as pltpu
from jax.sharding import PartitionSpec as P


SECTIONS = 3
DAY_STEPS = 2
LANES = 128
SUB = 8
LOW = 2 * SECTIONS
HIGH = SECTIONS
PARTS = 2
TOGETHER = 8
CHUNK = 8
LOG2E = 1.4426950408889634


def flat_rows(cells):
    *lead, rows, width = cells.shape
    sub = min(rows, SUB)
    split = cells.reshape(*lead, rows // sub, sub, width // LANES, LANES)
    return jnp.moveaxis(split, -2, -3).reshape(-1, LANES)


class Sizes:
    def __init__(self, field, groups):
        self.species, self.levels, self.rows, self.width = field.shape
        self.tiles = self.width // LANES
        self.groups = groups
        self.part = self.rows // groups
        self.blocks = self.levels * self.tiles * self.part
        self.stride = self.levels * self.rows * self.tiles
        self.columns = self.levels * self.tiles
        self.count = self.species // PARTS
        self.low_rows = LOW * self.columns * self.count
        self.high_rows = HIGH * self.columns * self.count
        self.span = self.rows + 2 * SUB
        self.edge_rows = 3 * self.columns * SUB

    def source_row(self, level, row, tile):
        return ((level * (self.rows // SUB) + row // SUB) * self.tiles + tile) * SUB + row % SUB

    def pairs(self):
        return [(level, tile) for level in range(self.levels) for tile in range(self.tiles)]


def middle(a, b):
    return jnp.maximum(jnp.minimum(a, b), jnp.minimum(jnp.maximum(a, b), 0.0))


def shift_columns(parts, amount):
    if amount > 0:
        return [pltpu.roll(parts[-1], 1, 1)] + parts[:-1]
    return parts[1:] + [pltpu.roll(parts[0], LANES - 1, 1)]


def spread_matrix(tiles, back):
    natural = lax.broadcasted_iota(jnp.int32, (tiles * LANES, tiles * LANES), 1 if back else 0)
    spread = lax.broadcasted_iota(jnp.int32, (tiles * LANES, tiles * LANES), 0 if back else 1)
    hit = natural == (spread % LANES) * tiles + spread // LANES
    return jnp.where(hit, 1.0, 0.0).astype(jnp.bfloat16)


def reorder(parts, matrix):
    x = jnp.concatenate(parts, axis=1)
    total = None
    for _ in range(3):
        piece = x.astype(jnp.bfloat16)
        x = x - piece.astype(jnp.float32)
        term = jnp.dot(piece, matrix, preferred_element_type=jnp.float32)
        total = term if total is None else total + term
    return [total[:, k * LANES : (k + 1) * LANES] for k in range(len(parts))]


def pack_kernel(z, part, x_ref, *refs):
    forth = spread_matrix(z.tiles, False)
    if part == 0:
        courant_ref, low_ref, high_ref, field, courant_out = refs
    else:
        low_ref, high_ref, field = refs

    def spread(flat, strips):
        split = flat.reshape(strips, z.rows // SUB, z.tiles, SUB, LANES)
        return reorder([split[:, :, t].reshape(strips * z.rows, LANES) for t in range(z.tiles)], forth)

    if part == 0:
        parts = spread(courant_ref[...], 3 * z.levels)
        shifted = shift_columns(parts, -1)
        for strip in range(3 * z.levels):
            rows = slice(strip * z.rows, (strip + 1) * z.rows)
            for tile in range(z.tiles):
                value = (shifted if strip // z.levels == 1 else parts)[tile][rows]
                col = strip * z.tiles + tile
                courant_out[pl.ds(col * z.rows, z.rows), :] = value
                low_ref[pl.ds(z.low_rows + col * SUB, SUB), :] = value[z.rows - SUB :]
                high_ref[pl.ds(z.high_rows + col * SUB, SUB), :] = value[:SUB]

    def some(index, carry):
        strips = CHUNK * z.levels
        size = strips * z.tiles * z.rows
        start = pl.multiple_of((part * (z.count // CHUNK) + index) * size, SUB)
        values = spread(x_ref[pl.ds(start, size), :], strips)
        for strip in range(strips):
            for tile in range(z.tiles):
                at = pl.multiple_of(index * size + (strip * z.tiles + tile) * z.rows, SUB)
                field[pl.ds(at, z.rows), :] = values[tile][strip * z.rows : (strip + 1) * z.rows]
        return carry

    lax.fori_loop(0, z.count // CHUNK, some, 0)

    def edges(index, carry):
        for col in range(z.columns):
            target = index * z.columns + col
            source = target * z.rows
            low_ref[pl.ds(target * LOW, LOW), :] = field[pl.ds(source + z.rows - LOW, LOW), :]
            high_ref[pl.ds(target * HIGH, HIGH), :] = field[pl.ds(source, HIGH), :]
        return carry

    lax.fori_loop(0, z.count, edges, 0, unroll=4)


def transport_kernel(z, field_ref, courant_ref, low_edge, high_edge, low_ref, high_ref, *refs):
    span = z.span
    cols = range(z.columns)
    outs, (coef, final, natural), slots = refs[: z.groups], refs[z.groups : z.groups + 3], refs[z.groups + 3 :]

    def coef_row(kind, which, col, j):
        return ((kind * 2 + which) * z.columns + col) * span + j

    for kind in range(3):
        for col in cols:
            one = kind * z.columns + col
            tiles = [low_edge[pl.ds(one * SUB, SUB), :]]
            tiles += [courant_ref[pl.ds(one * z.rows + row, SUB), :] for row in range(0, z.rows, SUB)]
            tiles += [high_edge[pl.ds(one * SUB, SUB), :]]
            for k, value in enumerate(tiles):
                coef[pl.ds(coef_row(kind, 0, col, k * SUB), SUB), :] = value
                coef[pl.ds(coef_row(kind, 1, col, k * SUB), SUB), :] = 0.5 * value * (1.0 - value)

    def weights(kind, col, j):
        return [coef[pl.ds(coef_row(kind, which, col, j), SUB), :] for which in range(2)]

    def one_species(index, start, fields, fluxes):
        for col in cols:
            base = index * z.columns + col
            at = col * span + SUB
            start[pl.ds(at - LOW, LOW), :] = low_ref[pl.ds(base * LOW, LOW), :]
            start[pl.ds(at + z.rows, HIGH), :] = high_ref[pl.ds(base * HIGH, HIGH), :]
            start[pl.ds(at, z.rows), :] = field_ref[pl.ds(pl.multiple_of(base * z.rows, SUB), z.rows), :]
        for step in range(SECTIONS):
            write = fields[step % 2]
            source = start if step == 0 else fields[(step + 1) % 2]
            read = lambda col, j, ref=source: ref[pl.ds(col * span + j, SUB), :]
            bottom = SUB - LOW + 2 * (step + 1)
            top = SUB + z.rows + HIGH - (step + 1)
            for j in range(bottom - 1, top, SUB):
                for col in cols:
                    below, here, above = [read(col, j + k) for k in (-1, 0, 1)]
                    a, b = weights(0, col, j + 1)
                    fluxes[pl.ds(col * span + j, SUB), :] = a * here + b * middle(here - below, above - here)
            for j in range(bottom, top, SUB):
                c = []
                for col in cols:
                    leave = fluxes[pl.ds(col * span + j, SUB), :]
                    enter = fluxes[pl.ds(col * span + j - 1, SUB), :]
                    c.append(read(col, j) - (leave - enter))
                for level in range(z.levels):
                    mine = slice(level * z.tiles, (level + 1) * z.tiles)
                    row = c[mine]
                    back = [v - w for v, w in zip(row, shift_columns(row, 1))]
                    ahead = shift_columns(back, -1)
                    leave = []
                    for tile in range(z.tiles):
                        a, b = weights(1, level * z.tiles + tile, j)
                        leave.append(a * row[tile] + b * middle(back[tile], ahead[tile]))
                    enter = shift_columns(leave, 1)
                    c[mine] = [row[t] - (leave[t] - enter[t]) for t in range(z.tiles)]
                for tile in range(z.tiles):
                    column = [c[level * z.tiles + tile] for level in range(z.levels)]
                    steps = [column[0]]
                    steps += [column[k + 1] - column[k] for k in range(z.levels - 1)]
                    steps += [-column[-1]]
                    lift = None
                    for level in range(z.levels):
                        col = level * z.tiles + tile
                        a, b = weights(2, col, j)
                        rising = a * column[level] + b * middle(steps[level], steps[level + 1])
                        net = rising if lift is None else rising - lift
                        lift = rising
                        value = column[level] - net
                        if step < SECTIONS - 1:
                            write[pl.ds(col * span + j, SUB), :] = value
                        else:
                            base = (index * z.columns + col) * z.rows + j - SUB
                            final[pl.ds(pl.multiple_of(base, SUB), SUB), :] = value

    def some_species(index, carry):
        for k in range(TOGETHER):
            one_species(index * TOGETHER + k, slots[4 * k], slots[4 * k + 1 : 4 * k + 3], slots[4 * k + 3])
        return carry

    lax.fori_loop(0, z.count // TOGETHER, some_species, 0)

    back = spread_matrix(z.tiles, True)
    me = lax.axis_index("tracer")

    def scatter(index, carry):
        many = CHUNK * z.levels
        size = many * z.tiles * z.rows
        whole = final[pl.ds(pl.multiple_of(index * size, SUB), size), :].reshape(many, z.tiles, z.rows, LANES)
        parts = reorder([whole[:, t].reshape(many * z.rows, LANES) for t in range(z.tiles)], back)
        for one in range(many):
            for tile in range(z.tiles):
                strip = one * z.tiles + tile
                natural[pl.ds(strip * z.rows, z.rows), :] = parts[tile][one * z.rows : (one + 1) * z.rows]
        for k, out_ref in enumerate(outs):
            first = (me ^ k) * z.part
            for strip in range(many * z.tiles):
                at = index * CHUNK * z.blocks + strip * z.part
                out_ref[pl.ds(at, z.part), :] = natural[pl.ds(strip * z.rows + first, z.part), :]
        return carry

    lax.fori_loop(0, z.count // CHUNK, scatter, 0)


def rates_kernel(pieces, warm_ref, glow_ref, lit_ref, rate_ref, barrier_ref, photo_ref, out_ref):
    warm = [(1.0 - warm_ref[pl.ds(p * SUB, SUB), :]) * LOG2E for p in range(pieces)]
    glow = [
        jnp.where(lit_ref[pl.ds(p * SUB, SUB), :] == 1, glow_ref[pl.ds(p * SUB, SUB), :], 0.0)
        for p in range(pieces)
    ]

    def one(r, carry):
        for p in range(pieces):
            at = pl.ds(pl.multiple_of(r * pieces * SUB, SUB) + p * SUB, SUB)
            out_ref[at, :] = rate_ref[r] * jnp.exp2(barrier_ref[r] * warm[p]) + photo_ref[r] * glow[p]
        return carry

    lax.fori_loop(0, rate_ref.shape[0], one, 0, unroll=8)


def chemistry_kernel(z, species, *refs):
    pieces = z.blocks // SUB
    sources = refs[: PARTS * z.groups]
    lit_ref, k_ref, table_ref, out_ref, state, made, lost_a, lost_b = refs[PARTS * z.groups :]
    reactions = k_ref.shape[0] // z.blocks

    def cell(row, piece):
        return pl.ds(pl.multiple_of(row, SUB) + piece * SUB, SUB)

    lit = [lit_ref[pl.ds(p * SUB, SUB), :] == 1 for p in range(pieces)]
    steps = [jnp.where(lit[p], float(DAY_STEPS), 1.0) for p in range(pieces)]
    zero = jnp.zeros((SUB, LANES), jnp.float32)
    me = lax.axis_index("tracer")

    def prepare(at, p, value):
        made[at, :] = steps[p] * value
        lost_a[at, :] = steps[p]
        lost_b[at, :] = zero

    def begin(index, carry):
        for number, ref in enumerate(sources):
            part, k = divmod(number, z.groups)
            first = (me ^ k) * z.species + part * z.count
            for p in range(pieces):
                value = ref[cell(index * z.blocks, p), :]
                at = cell((first + index) * z.blocks, p)
                state[at, :] = value
                prepare(at, p, value)
        return carry

    lax.fori_loop(0, z.count, begin, 0)

    def react(r, carry):
        first, second, product = table_ref[r], table_ref[reactions + r], table_ref[2 * reactions + r]
        for p in range(pieces):
            k = k_ref[cell(r * z.blocks, p), :]
            x = state[cell(first, p), :]
            y = state[cell(second, p), :]
            kx = k * x
            ky = k * y
            made[cell(product, p), :] += kx * y
            lost_a[cell(first, p), :] += ky
            lost_b[cell(second, p), :] += kx
        return carry

    for sub in range(DAY_STEPS):
        lax.fori_loop(0, reactions, react, 0, unroll=16)

        def finish(s, carry):
            for p in range(pieces):
                at = cell(s * z.blocks, p)
                value = made[at, :] / (lost_a[at, :] + lost_b[at, :])
                if sub < DAY_STEPS - 1:
                    prepare(at, p, value)
                    if sub == 0:
                        state[at, :] = value
                if sub > 0:
                    value = jnp.where(lit[p], value, state[at, :])
                    out_ref[at, :] = value
            return carry

        lax.fori_loop(0, species, finish, 0, unroll=4)


VMEM = pl.BlockSpec(memory_space=pltpu.VMEM)
SMEM = pl.BlockSpec(memory_space=pltpu.SMEM)


def rows_of(count):
    return jax.ShapeDtypeStruct((count, LANES), jnp.float32)


ANY = pl.BlockSpec(memory_space=pl.ANY)
HBM = pl.BlockSpec(memory_space=pltpu.HBM)


def pack(z, part, *flat):
    extra = z.edge_rows if part == 0 else 0
    rows = [z.low_rows + extra, z.high_rows + extra, z.count * z.columns * z.rows]
    if part == 0:
        rows.append(3 * z.columns * z.rows)
    return pl.pallas_call(
        functools.partial(pack_kernel, z, part),
        out_shape=tuple(rows_of(n) for n in rows),
        in_specs=[VMEM] * len(flat),
        out_specs=(VMEM,) * len(rows),
        compiler_params=pltpu.CompilerParams(vmem_limit_bytes=16 << 20),
        cost_estimate=pl.CostEstimate(flops=100 * z.count * z.stride * LANES, bytes_accessed=0, transcendentals=0),
        name="pack",
    )(*flat)


def transport(z, *flat):
    size = z.span * z.columns
    scratch = [6 * size, z.count * z.columns * z.rows, CHUNK * z.columns * z.rows] + [size] * (4 * TOGETHER)
    return pl.pallas_call(
        functools.partial(transport_kernel, z),
        out_shape=(rows_of(z.count * z.blocks),) * z.groups,
        in_specs=[VMEM] * len(flat),
        out_specs=(VMEM,) * z.groups,
        scratch_shapes=[pltpu.VMEM((n, LANES), jnp.float32) for n in scratch],
        compiler_params=pltpu.CompilerParams(vmem_limit_bytes=20 << 20),
        cost_estimate=pl.CostEstimate(flops=400 * z.count * z.stride * LANES, bytes_accessed=0, transcendentals=0),
        name="transport",
    )(*flat)


def rates(z, warm, glow, lit, rate, barrier, photo):
    reactions = rate.shape[0]
    return pl.pallas_call(
        functools.partial(rates_kernel, z.blocks // SUB),
        out_shape=rows_of(reactions * z.blocks),
        in_specs=[VMEM] * 3 + [SMEM] * 3,
        out_specs=VMEM,
        compiler_params=pltpu.CompilerParams(vmem_limit_bytes=16 << 20),
        cost_estimate=pl.CostEstimate(
            flops=40 * reactions * z.blocks * LANES, bytes_accessed=0, transcendentals=0
        ),
        name="rates",
    )(warm, glow, lit, rate, barrier, photo)


def chemistry(z, species, arrived, lit, k, table):
    size = species * z.blocks
    return pl.pallas_call(
        functools.partial(chemistry_kernel, z, species),
        out_shape=rows_of(size),
        in_specs=[VMEM] * (len(arrived) + 2) + [SMEM],
        out_specs=VMEM,
        scratch_shapes=[pltpu.VMEM((size, LANES), jnp.float32)] * 4,
        compiler_params=pltpu.CompilerParams(vmem_limit_bytes=20 << 20),
        name="chemistry",
    )(*arrived, lit, k, table)


def body(
    mixing_ratio_field,
    eastward_face_cfl,
    northward_face_cfl,
    upward_face_cfl,
    thermal_anomaly,
    radiant_flux,
    daylight_mask,
    baseline_kinetic_coefficient,
    arrhenius_barrier,
    photodissociation_factor,
    stoichiometry_table,
):
    groups = lax.axis_size("tracer")
    strips = lax.axis_size("space")
    z = Sizes(mixing_ratio_field, groups)
    courant = flat_rows(jnp.stack([eastward_face_cfl, northward_face_cfl, upward_face_cfl]))
    field = flat_rows(mixing_ratio_field)
    upward = [(i, i + 1) for i in range(strips - 1)]
    downward = [(i + 1, i) for i in range(strips - 1)]
    fields, halos = [], []
    for part in range(PARTS):
        if part == 0:
            low, high, ready, courant = pack(z, part, field, courant)
        else:
            field, _ = lax.optimization_barrier((field, ready))
            low, high, ready = pack(z, part, field)
        low = lax.ppermute(low, "space", upward)
        high = lax.ppermute(high, "space", downward)
        fields.append(ready)
        halos.append((low, high))
    low_edge = halos[0][0][z.low_rows :]
    high_edge = halos[0][1][z.high_rows :]
    arrived = []
    for part in range(PARTS):
        ready = fields[part]
        if part > 0:
            ready, _ = lax.optimization_barrier((ready, moved[0]))
        moved = transport(z, ready, courant, low_edge, high_edge, *halos[part])
        arrived.append(moved[0])
        for k in range(1, groups):
            arrived.append(lax.ppermute(moved[k], "tracer", [(i, i ^ k) for i in range(groups)]))
    mask, table, _ = lax.optimization_barrier((daylight_mask, stoichiometry_table, moved[0]))
    lit = jnp.broadcast_to(jnp.moveaxis(mask, 2, 1).reshape(z.blocks, 1), (z.blocks, LANES))
    k = rates(
        z,
        flat_rows(thermal_anomaly),
        flat_rows(radiant_flux),
        lit,
        baseline_kinetic_coefficient,
        arrhenius_barrier,
        photodissociation_factor,
    )
    species = z.species * groups
    out = chemistry(z, species, arrived, lit, k, table.reshape(-1) * z.blocks)
    out = out.reshape(species, z.levels, z.tiles, z.part, LANES)
    return jnp.moveaxis(out, 2, 3).reshape(species, z.levels, z.part, z.width)


def solution(mesh):
    placed = (
        P("tracer", None, "space", None),
        P(None, "space", None),
        P(None, "space", None),
        P(None, "space", None),
        P(None, ("space", "tracer"), None),
        P(None, ("space", "tracer"), None),
        P(None, ("space", "tracer"), None),
        P(),
        P(),
        P(),
        P(),
    )
    return jax.shard_map(
        body,
        mesh=mesh,
        in_specs=placed,
        out_specs=P(None, None, ("space", "tracer"), None),
        check_vma=False,
    )
```

time: 80 us -> 65.1 us (0.81)
  the two profiles are of different devices: /device:TPU:16 before, /device:TPU:17 now
where the time goes in v5:
time: 65.1 us; the launch traced here: 64.8 us
  Pallas kernels  33.8 us (52%)
  starting transfers between devices  16.9 us (26%)
  waiting for transfers between devices  11.3 us (17%)
  local copies, waits for them, and re-layouts  1.81 us (3%)
  other arithmetic  0.8 us (1%)
    pallas_call x2, Pallas kernels, transport(): pl.pallas_call(functools.partial(transport_kernel, z), out_shape=(rows_of...  14.3 us
    pallas_call x1, Pallas kernels, chemistry(): pl.pallas_call(functools.partial(chemistry_kernel, z, species), out_shape...  12.9 us
    ppermute x2, starting transfers between devices, body(): low = lax.ppermute(low, 'space', upward)  7.53 us
    ppermute x6, waiting for transfers between devices, body(): lax.ppermute(moved[k], 'tracer', [(i, i ^ k) for i in range(groups)])  7 us
    ppermute x6, starting transfers between devices, body(): lax.ppermute(moved[k], 'tracer', [(i, i ^ k) for i in range(groups)])  5.53 us
    ppermute x2, waiting for transfers between devices, body(): high = lax.ppermute(high, 'space', downward)  4.29 us
    ppermute x2, starting transfers between devices, body(): high = lax.ppermute(high, 'space', downward)  3.83 us
    pallas_call x1, Pallas kernels, rates(): pl.pallas_call(functools.partial(rates_kernel, z.blocks // SUB), out_shap...  3.76 us
  transfers between devices with their start and end apart: 10, of which 5 were waited for; matrix products, arithmetic and copies ran while one was open for 0% of the time, Pallas kernels for 30%

profile of v5, /device:TPU:17, one launch (start us, length us, event | category | flops | bytes accessed | tf_op | source)
XLA Modules:
  0.0 64.8 jit_solution(18047482157116818153)
XLA Ops:
  0.0 0.8 %pad_maximum_fusion = f32[3,2,2,8,2,128]{5,3,4,2,1,0:T(8,128)S(1)} fusion(f32[1,2,2,8,2,128]{5,3,4,2,1,0:T(8,128)} %bitcast.32, f32[1,2,2,8,2,128]{5,3,4,2,1,0:T(8,128)} %bitcast.33, f32[1,2,2,8,2,128]{5,3,4,2,1,0:T(8,128)} %bitcast.34), kind=kLoop, calls=%fused_computation | loop fusion | flops 49152 | bytes 196608 | tf_op jit(solution)/shard_map/stack | solution.py:398
  0.8 0.0 copy-start
  0.8 1.6 %copy-done = f32[64,2,16,256]{3,2,1,0:T(8,128)S(1)} copy-done((f32[64,2,16,256]{3,2,1,0:T(8,128)S(1)}, f32[64,2,16,256]{3,2,1,0:T(8,128)}, u32[]{:S(2)}) %copy-start) | copy-done | bytes 2097176
  2.4 1.5 %pack.2 = (f32[864,128]{1,0:T(8,128)S(1)}, f32[480,128]{1,0:T(8,128)S(1)}, f32[2048,128]{1,0:T(8,128)S(1)}, f32[192,128]{1,0:T(8,128)S(1)}) custom-call(f32[4096,128]{1,0:T(8,128)S(1)} %bitcast.27, f32[192,128]{1,0:T(8,128)S(1)} %bitcast.29), custom_call_target="tpu_custom_call" | custom-call | flops 26214400 | tf_op jit(solution)/shard_map/pack/pallas_call | solution.py:328
  3.9 3.8 %collective-permute-start = (f32[864,128]{1,0:T(8,128)S(1)}, f32[864,128]{1,0:T(8,128)S(1)}, u32[]{:S(2)}, u32[]{:S(2)}) collective-permute-start(f32[864,128]{1,0:T(8,128)S(1)} %get-tuple-element.26), channel_id=1, source_target_pairs={{0,4},{4,8},{8,12},{12,16},{16,20},{20,24},{24,28},{1,5},{5,9},{9,... | collective-permute-start | bytes 1327112 | tf_op jit(solution)/shard_map/ppermute | solution.py:409
  7.7 1.9 %collective-permute-start.1 = (f32[480,128]{1,0:T(8,128)S(1)}, f32[480,128]{1,0:T(8,128)S(1)}, u32[]{:S(2)}, u32[]{:S(2)}) collective-permute-start(f32[480,128]{1,0:T(8,128)S(1)} %get-tuple-element.27), channel_id=1, source_target_pairs={{4,0},{8,4},{12,8},{16,12},{20,16},{24,20},{28,24},{5,1},{9,5},{13... | collective-permute-start | bytes 737288 | tf_op jit(solution)/shard_map/ppermute | solution.py:410
  9.6 1.3 %pack.3 = (f32[768,128]{1,0:T(8,128)S(1)}, f32[384,128]{1,0:T(8,128)S(1)}, f32[2048,128]{1,0:T(8,128)S(1)}) custom-call(f32[4096,128]{1,0:T(8,128)S(1)} %bitcast.28), custom_call_target="tpu_custom_call" | custom-call | flops 26214400 | tf_op jit(solution)/shard_map/pack/pallas_call | solution.py:328
  10.9 0.0 copy-start.7
  10.9 0.0 copy-start.6
  10.9 0.0 copy-start.1
  11.0 0.0 copy-start.2
  11.0 0.0 copy-start.3
  11.0 0.0 copy-start.4
  11.0 0.0 copy-start.5
  11.0 3.8 %collective-permute-start.5 = (f32[768,128]{1,0:T(8,128)S(1)}, f32[768,128]{1,0:T(8,128)S(1)}, u32[]{:S(2)}, u32[]{:S(2)}) collective-permute-start(f32[768,128]{1,0:T(8,128)S(1)} %get-tuple-element.35), channel_id=1, source_target_pairs={{0,4},{4,8},{8,12},{12,16},{16,20},{20,24},{24,28},{1,5},{5,9},{9,... | collective-permute-start | bytes 1179656 | tf_op jit(solution)/shard_map/ppermute | solution.py:409
  14.8 0.4 collective-permute-done.1.high_ref
  15.2 0.0 collective-permute-done.low_ref
  15.2 7.2 %transport.2 = (f32[512,128]{1,0:T(8,128)S(1)}, f32[512,128]{1,0:T(8,128)S(1)}, f32[512,128]{1,0:T(8,128)S(1)}, f32[512,128]{1,0:T(8,128)S(1)}) custom-call(f32[2048,128]{1,0:T(8,128)S(1)} %get-tuple-element.24.field_ref, f32[192,128]{1,0:T(8,128)S(1)} %get-tuple-element.25.courant_ref, f32[96,128]{1,0:T(8,128)S(1)} %slice.8.low_edge, ...), custom_call_target="tpu_custom_call" | custom-call | flops 104857600 | tf_op jit(solution)/shard_map/transport/pallas_call | solution.py:342
  22.4 1.3 %collective-permute-start.2 = (f32[512,128]{1,0:T(8,128)S(1)}, f32[512,128]{1,0:T(8,128)S(1)}, u32[]{:S(2)}, u32[]{:S(2)}) collective-permute-start(f32[512,128]{1,0:T(8,128)S(1)} %get-tuple-element.29), channel_id=1, source_target_pairs={{0,1},{1,0},{2,3},{3,2},{4,5},{5,4},{6,7},{7,6},{8,9},{9,8},{10,11... | collective-permute-start | bytes 786440 | tf_op jit(solution)/shard_map/ppermute | solution.py:423
  23.7 1.9 %collective-permute-start.6 = (f32[384,128]{1,0:T(8,128)S(1)}, f32[384,128]{1,0:T(8,128)S(1)}, u32[]{:S(2)}, u32[]{:S(2)}) collective-permute-start(f32[384,128]{1,0:T(8,128)S(1)} %get-tuple-element.36), channel_id=1, source_target_pairs={{4,0},{8,4},{12,8},{16,12},{20,16},{24,20},{28,24},{5,1},{9,5},{13... | collective-permute-start | bytes 589832 | tf_op jit(solution)/shard_map/ppermute | solution.py:410
  25.6 1.4 %collective-permute-start.3 = (f32[512,128]{1,0:T(8,128)S(1)}, f32[512,128]{1,0:T(8,128)S(1)}, u32[]{:S(2)}, u32[]{:S(2)}) collective-permute-start(f32[512,128]{1,0:T(8,128)S(1)} %get-tuple-element.30), channel_id=1, source_target_pairs={{0,2},{1,3},{2,0},{3,1},{4,6},{5,7},{6,4},{7,5},{8,10},{9,11},{10,... | collective-permute-start | bytes 786440 | tf_op jit(solution)/shard_map/ppermute | solution.py:423
  27.1 0.1 collective-permute-start.4
  27.1 3.9 %collective-permute-done.6.high_ref = f32[384,128]{1,0:T(8,128)S(1)} collective-permute-done((f32[384,128]{1,0:T(8,128)S(1)}, f32[384,128]{1,0:T(8,128)S(1)}, u32[]{:S(2)}, u32[]{:S(2)}) %collective-permute-start.6) | collective-permute-done | bytes 196640 | tf_op jit(solution)/shard_map/ppermute | solution.py:410
  31.0 0.0 collective-permute-done.5.low_ref
  31.0 7.2 %transport.3 = (f32[512,128]{1,0:T(8,128)S(1)}, f32[512,128]{1,0:T(8,128)S(1)}, f32[512,128]{1,0:T(8,128)S(1)}, f32[512,128]{1,0:T(8,128)S(1)}) custom-call(f32[2048,128]{1,0:T(8,128)S(1)} %get-tuple-element.34.field_ref, f32[192,128]{1,0:T(8,128)S(1)} %get-tuple-element.25.courant_ref, f32[96,128]{1,0:T(8,128)S(1)} %slice.8.low_edge, ...), custom_call_target="tpu_custom_call" | custom-call | flops 104857600 | tf_op jit(solution)/shard_map/transport/pallas_call | solution.py:342
  38.2 0.3 collective-permute-start.7
  38.5 1.5 %collective-permute-start.8 = (f32[512,128]{1,0:T(8,128)S(1)}, f32[512,128]{1,0:T(8,128)S(1)}, u32[]{:S(2)}, u32[]{:S(2)}) collective-permute-start(f32[512,128]{1,0:T(8,128)S(1)} %get-tuple-element.39), channel_id=1, source_target_pairs={{0,2},{1,3},{2,0},{3,1},{4,6},{5,7},{6,4},{7,5},{8,10},{9,11},{10,... | collective-permute-start | bytes 786440 | tf_op jit(solution)/shard_map/ppermute | solution.py:423
  40.0 0.0 collective-permute-done.2.refs_1_
  40.0 0.9 %collective-permute-start.9 = (f32[512,128]{1,0:T(8,128)S(1)}, f32[512,128]{1,0:T(8,128)S(1)}, u32[]{:S(2)}, u32[]{:S(2)}) collective-permute-start(f32[512,128]{1,0:T(8,128)S(1)} %get-tuple-element.40), channel_id=1, source_target_pairs={{0,3},{1,2},{2,1},{3,0},{4,7},{5,6},{6,5},{7,4},{8,11},{9,10},{10,... | collective-permute-start | bytes 786440 | tf_op jit(solution)/shard_map/ppermute | solution.py:423
  40.9 0.0 copy-done.7
  40.9 0.1 broadcast_in_dim.7
  41.0 0.0 copy-done.6
  41.0 0.1 broadcast_in_dim.8.lit_ref.refs_8_
  41.1 0.0 copy-done.1
  41.1 0.0 copy-done.2
  41.1 0.0 copy-done.3
  41.1 0.0 copy-done.4
  41.1 0.0 copy-done.5
  41.1 3.8 %rates.1.refs_9_ = f32[12288,128]{1,0:T(8,128)S(1)} custom-call(f32[16,128]{1,0:T(8,128)S(1)} %bitcast.30, f32[16,128]{1,0:T(8,128)S(1)} %bitcast.31, s32[16,128]{1,0:T(8,128)S(1)} %broadcast_in_dim.8.lit_ref.refs_8_, f32[768]{0:T(1024)S(1)} %copy-done.3, f32[768]{0:T(1024)S(1)} %copy-done.4, f32[768]{0:T(1024)S(1)} %copy-done.5), custom_call_target="tpu_custom_call" | custom-call | flops 62914560 | tf_op jit(solution)/shard_map/rates/pallas_call | solution.py:356
  44.9 0.0 collective-permute-done.3.refs_2_
  44.9 0.0 collective-permute-done.4.refs_3_
  44.9 1.6 %collective-permute-done.7.refs_5_ = f32[512,128]{1,0:T(8,128)S(1)} collective-permute-done((f32[512,128]{1,0:T(8,128)S(1)}, f32[512,128]{1,0:T(8,128)S(1)}, u32[]{:S(2)}, u32[]{:S(2)}) %collective-permute-start.7) | collective-permute-done | bytes 262176 | tf_op jit(solution)/shard_map/ppermute | solution.py:423
  46.5 4.3 %collective-permute-done.8.refs_6_ = f32[512,128]{1,0:T(8,128)S(1)} collective-permute-done((f32[512,128]{1,0:T(8,128)S(1)}, f32[512,128]{1,0:T(8,128)S(1)}, u32[]{:S(2)}, u32[]{:S(2)}) %collective-permute-start.8) | collective-permute-done | bytes 262176 | tf_op jit(solution)/shard_map/ppermute | solution.py:423
  50.8 1.1 %collective-permute-done.9.refs_7_ = f32[512,128]{1,0:T(8,128)S(1)} collective-permute-done((f32[512,128]{1,0:T(8,128)S(1)}, f32[512,128]{1,0:T(8,128)S(1)}, u32[]{:S(2)}, u32[]{:S(2)}) %collective-permute-start.9) | collective-permute-done | bytes 262176 | tf_op jit(solution)/shard_map/ppermute | solution.py:423
  51.9 12.9 %chemistry.1 = f32[4096,128]{1,0:T(8,128)} custom-call(f32[512,128]{1,0:T(8,128)S(1)} %get-tuple-element.28.refs_0_, f32[512,128]{1,0:T(8,128)S(1)} %collective-permute-done.2.refs_1_, f32[512,128]{1,0:T(8,128)S(1)} %collective-permute-done.3.refs_2_, f32[512,128]{1,0:T(8,128)S(1)} %collective-permute-done.4.refs_3_, ...), custom_call_target="tpu_custom_call" | custom-call | tf_op jit(solution)/shard_map/chemistry/pallas_call | solution.py:371
  (4 shorter events, 0.0 us)
Async XLA Ops:
  0.8 1.6 %copy-start = (f32[64,2,16,256]{3,2,1,0:T(8,128)S(1)}, f32[64,2,16,256]{3,2,1,0:T(8,128)}, u32[]{:S(2)}) copy-start(f32[64,2,16,256]{3,2,1,0:T(8,128)} %param.11) | copy-start | bytes 6291460
  3.9 11.3 %collective-permute-start = (f32[864,128]{1,0:T(8,128)S(1)}, f32[864,128]{1,0:T(8,128)S(1)}, u32[]{:S(2)}, u32[]{:S(2)}) collective-permute-start(f32[864,128]{1,0:T(8,128)S(1)} %get-tuple-element.26), channel_id=1, source_target_pairs={{0,4},{4,8},{8,12},{12,16},{16,20},{20,24},{24,28},{1,5},{5,9},{9,... | collective-permute-start | bytes 1327112 | tf_op jit(solution)/shard_map/ppermute | solution.py:409
  7.7 7.5 %collective-permute-start.1 = (f32[480,128]{1,0:T(8,128)S(1)}, f32[480,128]{1,0:T(8,128)S(1)}, u32[]{:S(2)}, u32[]{:S(2)}) collective-permute-start(f32[480,128]{1,0:T(8,128)S(1)} %get-tuple-element.27), channel_id=1, source_target_pairs={{4,0},{8,4},{12,8},{16,12},{20,16},{24,20},{28,24},{5,1},{9,5},{13... | collective-permute-start | bytes 737288 | tf_op jit(solution)/shard_map/ppermute | solution.py:410
  10.9 30.0 %copy-start.7 = (s32[2,4,2]{1,2,0:T(2,128)S(1)}, s32[2,4,2]{1,2,0:T(2,128)}, u32[]{:S(2)}) copy-start(s32[2,4,2]{1,2,0:T(2,128)} %param.17) | copy-start | bytes 196
  10.9 30.1 %copy-start.6 = (s32[3,768]{1,0:T(4,128)S(1)}, s32[3,768]{1,0:T(4,128)}, u32[]{:S(2)}) copy-start(s32[3,768]{1,0:T(4,128)} %param.21) | copy-start | bytes 27652
  10.9 30.1 %copy-start.1 = (f32[2,4,256]{2,1,0:T(4,128)S(1)}, f32[2,4,256]{2,1,0:T(4,128)}, u32[]{:S(2)}) copy-start(f32[2,4,256]{2,1,0:T(4,128)} %param.15) | copy-start | bytes 24580
  11.0 30.1 %copy-start.2 = (f32[2,4,256]{2,1,0:T(4,128)S(1)}, f32[2,4,256]{2,1,0:T(4,128)}, u32[]{:S(2)}) copy-start(f32[2,4,256]{2,1,0:T(4,128)} %param.16) | copy-start | bytes 24580
  11.0 30.1 %copy-start.3 = (f32[768]{0:T(1024)S(1)}, f32[768]{0:T(1024)}, u32[]{:S(2)}) copy-start(f32[768]{0:T(1024)} %rate_ref.1) | copy-start | bytes 9220
  11.0 30.1 %copy-start.4 = (f32[768]{0:T(1024)S(1)}, f32[768]{0:T(1024)}, u32[]{:S(2)}) copy-start(f32[768]{0:T(1024)} %barrier_ref.1) | copy-start | bytes 9220
  11.0 30.1 %copy-start.5 = (f32[768]{0:T(1024)S(1)}, f32[768]{0:T(1024)}, u32[]{:S(2)}) copy-start(f32[768]{0:T(1024)} %photo_ref.1) | copy-start | bytes 9220
  11.0 20.0 %collective-permute-start.5 = (f32[768,128]{1,0:T(8,128)S(1)}, f32[768,128]{1,0:T(8,128)S(1)}, u32[]{:S(2)}, u32[]{:S(2)}) collective-permute-start(f32[768,128]{1,0:T(8,128)S(1)} %get-tuple-element.35), channel_id=1, source_target_pairs={{0,4},{4,8},{8,12},{12,16},{16,20},{20,24},{24,28},{1,5},{5,9},{9,... | collective-permute-start | bytes 1179656 | tf_op jit(solution)/shard_map/ppermute | solution.py:409
  22.4 17.5 %collective-permute-start.2 = (f32[512,128]{1,0:T(8,128)S(1)}, f32[512,128]{1,0:T(8,128)S(1)}, u32[]{:S(2)}, u32[]{:S(2)}) collective-permute-start(f32[512,128]{1,0:T(8,128)S(1)} %get-tuple-element.29), channel_id=1, source_target_pairs={{0,1},{1,0},{2,3},{3,2},{4,5},{5,4},{6,7},{7,6},{8,9},{9,8},{10,11... | collective-permute-start | bytes 786440 | tf_op jit(solution)/shard_map/ppermute | solution.py:423
  23.7 7.3 %collective-permute-start.6 = (f32[384,128]{1,0:T(8,128)S(1)}, f32[384,128]{1,0:T(8,128)S(1)}, u32[]{:S(2)}, u32[]{:S(2)}) collective-permute-start(f32[384,128]{1,0:T(8,128)S(1)} %get-tuple-element.36), channel_id=1, source_target_pairs={{4,0},{8,4},{12,8},{16,12},{20,16},{24,20},{28,24},{5,1},{9,5},{13... | collective-permute-start | bytes 589832 | tf_op jit(solution)/shard_map/ppermute | solution.py:410
  25.6 19.3 %collective-permute-start.3 = (f32[512,128]{1,0:T(8,128)S(1)}, f32[512,128]{1,0:T(8,128)S(1)}, u32[]{:S(2)}, u32[]{:S(2)}) collective-permute-start(f32[512,128]{1,0:T(8,128)S(1)} %get-tuple-element.30), channel_id=1, source_target_pairs={{0,2},{1,3},{2,0},{3,1},{4,6},{5,7},{6,4},{7,5},{8,10},{9,11},{10,... | collective-permute-start | bytes 786440 | tf_op jit(solution)/shard_map/ppermute | solution.py:423
  27.1 17.9 %collective-permute-start.4 = (f32[512,128]{1,0:T(8,128)S(1)}, f32[512,128]{1,0:T(8,128)S(1)}, u32[]{:S(2)}, u32[]{:S(2)}) collective-permute-start(f32[512,128]{1,0:T(8,128)S(1)} %get-tuple-element.31), channel_id=1, source_target_pairs={{0,3},{1,2},{2,1},{3,0},{4,7},{5,6},{6,5},{7,4},{8,11},{9,10},{10,... | collective-permute-start | bytes 786440 | tf_op jit(solution)/shard_map/ppermute | solution.py:423
  38.2 8.4 %collective-permute-start.7 = (f32[512,128]{1,0:T(8,128)S(1)}, f32[512,128]{1,0:T(8,128)S(1)}, u32[]{:S(2)}, u32[]{:S(2)}) collective-permute-start(f32[512,128]{1,0:T(8,128)S(1)} %get-tuple-element.38), channel_id=1, source_target_pairs={{0,1},{1,0},{2,3},{3,2},{4,5},{5,4},{6,7},{7,6},{8,9},{9,8},{10,11... | collective-permute-start | bytes 786440 | tf_op jit(solution)/shard_map/ppermute | solution.py:423
  38.5 12.3 %collective-permute-start.8 = (f32[512,128]{1,0:T(8,128)S(1)}, f32[512,128]{1,0:T(8,128)S(1)}, u32[]{:S(2)}, u32[]{:S(2)}) collective-permute-start(f32[512,128]{1,0:T(8,128)S(1)} %get-tuple-element.39), channel_id=1, source_target_pairs={{0,2},{1,3},{2,0},{3,1},{4,6},{5,7},{6,4},{7,5},{8,10},{9,11},{10,... | collective-permute-start | bytes 786440 | tf_op jit(solution)/shard_map/ppermute | solution.py:423
  40.0 11.9 %collective-permute-start.9 = (f32[512,128]{1,0:T(8,128)S(1)}, f32[512,128]{1,0:T(8,128)S(1)}, u32[]{:S(2)}, u32[]{:S(2)}) collective-permute-start(f32[512,128]{1,0:T(8,128)S(1)} %get-tuple-element.40), channel_id=1, source_target_pairs={{0,3},{1,2},{2,1},{3,0},{4,7},{5,6},{6,5},{7,4},{8,11},{9,10},{10,... | collective-permute-start | bytes 786440 | tf_op jit(solution)/shard_map/ppermute | solution.py:423

commit v6 on v5

--- a/solution.py
+++ b/solution.py
@@ -37,8 +37,7 @@
         self.stride = self.levels * self.rows * self.tiles
         self.columns = self.levels * self.tiles
         self.count = self.species // PARTS
-        self.low_rows = LOW * self.columns * self.count
-        self.high_rows = HIGH * self.columns * self.count
+        self.halo_rows = LOW * self.columns * self.count
         self.span = self.rows + 2 * SUB
         self.edge_rows = 3 * self.columns * SUB
 
@@ -80,9 +79,11 @@
 def pack_kernel(z, part, x_ref, *refs):
     forth = spread_matrix(z.tiles, False)
     if part == 0:
-        courant_ref, low_ref, high_ref, field, courant_out = refs
+        courant_ref, near_ref, far_ref, field, courant_out = refs
     else:
-        low_ref, high_ref, field = refs
+        near_ref, far_ref, field = refs
+    odd = lax.rem(lax.axis_index("space"), 2)
+    sides = ((near_ref, odd), (far_ref, 1 - odd))
 
     def spread(flat, strips):
         split = flat.reshape(strips, z.rows // SUB, z.tiles, SUB, LANES)
@@ -97,8 +98,6 @@
                 value = (shifted if strip // z.levels == 1 else parts)[tile][rows]
                 col = strip * z.tiles + tile
                 courant_out[pl.ds(col * z.rows, z.rows), :] = value
-                low_ref[pl.ds(z.low_rows + col * SUB, SUB), :] = value[z.rows - SUB :]
-                high_ref[pl.ds(z.high_rows + col * SUB, SUB), :] = value[:SUB]
 
     def some(index, carry):
         strips = CHUNK * z.levels
@@ -113,21 +112,40 @@
 
     lax.fori_loop(0, z.count // CHUNK, some, 0)
 
+    if part == 0:
+        for ref, below in sides:
+            for col in range(3 * z.columns):
+                source = col * z.rows + (1 - below) * (z.rows - SUB)
+                ref[pl.ds(z.halo_rows + col * SUB, SUB), :] = courant_out[pl.ds(pl.multiple_of(source, SUB), SUB), :]
+
     def edges(index, carry):
-        for col in range(z.columns):
-            target = index * z.columns + col
-            source = target * z.rows
-            low_ref[pl.ds(target * LOW, LOW), :] = field[pl.ds(source + z.rows - LOW, LOW), :]
-            high_ref[pl.ds(target * HIGH, HIGH), :] = field[pl.ds(source, HIGH), :]
+        for ref, below in sides:
+            for col in range(z.columns):
+                target = index * z.columns + col
+                source = target * z.rows + (1 - below) * (z.rows - LOW)
+                ref[pl.ds(target * LOW, LOW), :] = field[pl.ds(source, LOW), :]
         return carry
 
     lax.fori_loop(0, z.count, edges, 0, unroll=4)
 
 
-def transport_kernel(z, field_ref, courant_ref, low_edge, high_edge, low_ref, high_ref, *refs):
+def transport_kernel(z, field_ref, courant_ref, near_edge, far_edge, near_ref, far_ref, *refs):
     span = z.span
     cols = range(z.columns)
-    outs, (coef, final, natural), slots = refs[: z.groups], refs[z.groups : z.groups + 3], refs[z.groups + 3 :]
+    outs, (coef, final, natural, halo, edge), slots = refs[: z.groups], refs[z.groups : z.groups + 5], refs[z.groups + 5 :]
+    odd = lax.rem(lax.axis_index("space"), 2)
+    for source, above in ((near_ref, 1 - odd), (far_ref, odd)):
+
+        def place_halo(i, carry):
+            target = pl.multiple_of(above * z.halo_rows + i * SUB, SUB)
+            halo[pl.ds(target, SUB), :] = source[pl.ds(pl.multiple_of(i * SUB, SUB), SUB), :]
+            return carry
+
+        lax.fori_loop(0, z.halo_rows // SUB, place_halo, 0, unroll=12)
+    for source, above in ((near_edge, 1 - odd), (far_edge, odd)):
+        for row in range(0, z.edge_rows, SUB):
+            target = pl.multiple_of(above * z.edge_rows + row, SUB)
+            edge[pl.ds(target, SUB), :] = source[pl.ds(row, SUB), :]
 
     def coef_row(kind, which, col, j):
         return ((kind * 2 + which) * z.columns + col) * span + j
@@ -135,9 +153,9 @@
     for kind in range(3):
         for col in cols:
             one = kind * z.columns + col
-            tiles = [low_edge[pl.ds(one * SUB, SUB), :]]
+            tiles = [edge[pl.ds(one * SUB, SUB), :]]
             tiles += [courant_ref[pl.ds(one * z.rows + row, SUB), :] for row in range(0, z.rows, SUB)]
-            tiles += [high_edge[pl.ds(one * SUB, SUB), :]]
+            tiles += [edge[pl.ds(z.edge_rows + one * SUB, SUB), :]]
             for k, value in enumerate(tiles):
                 coef[pl.ds(coef_row(kind, 0, col, k * SUB), SUB), :] = value
                 coef[pl.ds(coef_row(kind, 1, col, k * SUB), SUB), :] = 0.5 * value * (1.0 - value)
@@ -149,8 +167,8 @@
         for col in cols:
             base = index * z.columns + col
             at = col * span + SUB
-            start[pl.ds(at - LOW, LOW), :] = low_ref[pl.ds(base * LOW, LOW), :]
-            start[pl.ds(at + z.rows, HIGH), :] = high_ref[pl.ds(base * HIGH, HIGH), :]
+            start[pl.ds(at - LOW, LOW), :] = halo[pl.ds(base * LOW, LOW), :]
+            start[pl.ds(at + z.rows, HIGH), :] = halo[pl.ds(z.halo_rows + base * LOW, HIGH), :]
             start[pl.ds(at, z.rows), :] = field_ref[pl.ds(pl.multiple_of(base * z.rows, SUB), z.rows), :]
         for step in range(SECTIONS):
             write = fields[step % 2]
@@ -322,7 +340,7 @@
 
 def pack(z, part, *flat):
     extra = z.edge_rows if part == 0 else 0
-    rows = [z.low_rows + extra, z.high_rows + extra, z.count * z.columns * z.rows]
+    rows = [z.halo_rows + extra, z.halo_rows + extra, z.count * z.columns * z.rows]
     if part == 0:
         rows.append(3 * z.columns * z.rows)
     return pl.pallas_call(
@@ -338,7 +356,8 @@
 
 def transport(z, *flat):
     size = z.span * z.columns
-    scratch = [6 * size, z.count * z.columns * z.rows, CHUNK * z.columns * z.rows] + [size] * (4 * TOGETHER)
+    scratch = [6 * size, z.count * z.columns * z.rows, CHUNK * z.columns * z.rows]
+    scratch += [2 * z.halo_rows, 2 * z.edge_rows] + [size] * (4 * TOGETHER)
     return pl.pallas_call(
         functools.partial(transport_kernel, z),
         out_shape=(rows_of(z.count * z.blocks),) * z.groups,
@@ -397,27 +416,26 @@
     z = Sizes(mixing_ratio_field, groups)
     courant = flat_rows(jnp.stack([eastward_face_cfl, northward_face_cfl, upward_face_cfl]))
     field = flat_rows(mixing_ratio_field)
-    upward = [(i, i + 1) for i in range(strips - 1)]
-    downward = [(i + 1, i) for i in range(strips - 1)]
+    near_pairs = [(i, i ^ 1) for i in range(strips) if i ^ 1 < strips]
+    far_pairs = [(i, ((i + 1) ^ 1) - 1) for i in range(strips) if 0 <= ((i + 1) ^ 1) - 1 < strips]
     fields, halos = [], []
     for part in range(PARTS):
         if part == 0:
-            low, high, ready, courant = pack(z, part, field, courant)
+            near, far, ready, courant = pack(z, part, field, courant)
         else:
             field, _ = lax.optimization_barrier((field, ready))
-            low, high, ready = pack(z, part, field)
-        low = lax.ppermute(low, "space", upward)
-        high = lax.ppermute(high, "space", downward)
+            near, far, ready = pack(z, part, field)
+        far = lax.ppermute(far, "space", far_pairs)
+        near = lax.ppermute(near, "space", near_pairs)
         fields.append(ready)
-        halos.append((low, high))
-    low_edge = halos[0][0][z.low_rows :]
-    high_edge = halos[0][1][z.high_rows :]
+        halos.append((near, far))
+    edges = [halo[z.halo_rows :] for halo in halos[0]]
     arrived = []
     for part in range(PARTS):
         ready = fields[part]
         if part > 0:
             ready, _ = lax.optimization_barrier((ready, moved[0]))
-        moved = transport(z, ready, courant, low_edge, high_edge, *halos[part])
+        moved = transport(z, ready, courant, *edges, *halos[part])
         arrived.append(moved[0])
         for k in range(1, groups):
             arrived.append(lax.ppermute(moved[k], "tracer", [(i, i ^ k) for i in range(groups)]))

time: 65.1 us -> 61.4 us (0.943)
  the two profiles are of different devices: /device:TPU:17 before, /device:TPU:16 now
where the time goes in v6:
time: 61.4 us; the launch traced here: 61 us
  Pallas kernels  34.1 us (56%)
  starting transfers between devices  12.8 us (21%)
  waiting for transfers between devices  11.4 us (19%)
  local copies, waits for them, and re-layouts  1.8 us (3%)
  other arithmetic  0.8 us (1%)
    pallas_call x2, Pallas kernels, transport(): pl.pallas_call(functools.partial(transport_kernel, z), out_shape=(rows_of...  14.6 us
    pallas_call x1, Pallas kernels, chemistry(): pl.pallas_call(functools.partial(chemistry_kernel, z, species), out_shape...  12.9 us
    ppermute x6, waiting for transfers between devices, body(): lax.ppermute(moved[k], 'tracer', [(i, i ^ k) for i in range(groups)])  8.73 us
    ppermute x6, starting transfers between devices, body(): lax.ppermute(moved[k], 'tracer', [(i, i ^ k) for i in range(groups)])  7.11 us
    ppermute x2, starting transfers between devices, body(): far = lax.ppermute(far, 'space', far_pairs)  4.43 us
    pallas_call x1, Pallas kernels, rates(): pl.pallas_call(functools.partial(rates_kernel, z.blocks // SUB), out_shap...  3.76 us
    pallas_call x2, Pallas kernels, pack(): pl.pallas_call(functools.partial(pack_kernel, z, part), out_shape=tuple((...  2.83 us
    ppermute x2, waiting for transfers between devices, body(): far = lax.ppermute(far, 'space', far_pairs)  2.65 us
  transfers between devices with their start and end apart: 10, of which 4 were waited for; matrix products, arithmetic and copies ran while one was open for 0% of the time, Pallas kernels for 32%

profile of v6, /device:TPU:16, one launch (start us, length us, event | category | flops | bytes accessed | tf_op | source)
XLA Modules:
  0.0 61.0 jit_solution(10593212041186582504)
XLA Ops:
  0.0 0.8 %pad_maximum_fusion = f32[3,2,2,8,2,128]{5,3,4,2,1,0:T(8,128)S(1)} fusion(f32[1,2,2,8,2,128]{5,3,4,2,1,0:T(8,128)} %bitcast.32, f32[1,2,2,8,2,128]{5,3,4,2,1,0:T(8,128)} %bitcast.33, f32[1,2,2,8,2,128]{5,3,4,2,1,0:T(8,128)} %bitcast.34), kind=kLoop, calls=%fused_computation | loop fusion | flops 49152 | bytes 196608 | tf_op jit(solution)/shard_map/stack | solution.py:417
  0.8 0.0 copy-start
  0.8 1.6 %copy-done = f32[64,2,16,256]{3,2,1,0:T(8,128)S(1)} copy-done((f32[64,2,16,256]{3,2,1,0:T(8,128)S(1)}, f32[64,2,16,256]{3,2,1,0:T(8,128)}, u32[]{:S(2)}) %copy-start) | copy-done | bytes 2097176
  2.4 1.5 %pack.2 = (f32[864,128]{1,0:T(8,128)S(1)}, f32[864,128]{1,0:T(8,128)S(1)}, f32[2048,128]{1,0:T(8,128)S(1)}, f32[192,128]{1,0:T(8,128)S(1)}) custom-call(f32[4096,128]{1,0:T(8,128)S(1)} %bitcast.27, f32[192,128]{1,0:T(8,128)S(1)} %bitcast.29), custom_call_target="tpu_custom_call" | custom-call | flops 26214400 | tf_op jit(solution)/shard_map/pack/pallas_call | solution.py:346
  3.9 0.1 collective-permute-start
  4.0 2.4 %collective-permute-start.1 = (f32[864,128]{1,0:T(8,128)S(1)}, f32[864,128]{1,0:T(8,128)S(1)}, u32[]{:S(2)}, u32[]{:S(2)}) collective-permute-start(f32[864,128]{1,0:T(8,128)S(1)} %get-tuple-element.27), channel_id=1, source_target_pairs={{4,8},{8,4},{12,16},{16,12},{20,24},{24,20},{5,9},{9,5},{13,17},{1... | collective-permute-start | bytes 1327112 | tf_op jit(solution)/shard_map/ppermute | solution.py:428
  6.5 1.3 %pack.3 = (f32[768,128]{1,0:T(8,128)S(1)}, f32[768,128]{1,0:T(8,128)S(1)}, f32[2048,128]{1,0:T(8,128)S(1)}) custom-call(f32[4096,128]{1,0:T(8,128)S(1)} %bitcast.28), custom_call_target="tpu_custom_call" | custom-call | flops 26214400 | tf_op jit(solution)/shard_map/pack/pallas_call | solution.py:346
  7.8 1.2 %collective-permute-start.5 = (f32[768,128]{1,0:T(8,128)S(1)}, f32[768,128]{1,0:T(8,128)S(1)}, u32[]{:S(2)}, u32[]{:S(2)}) collective-permute-start(f32[768,128]{1,0:T(8,128)S(1)} %get-tuple-element.35), channel_id=1, source_target_pairs={{0,4},{4,0},{8,12},{12,8},{16,20},{20,16},{24,28},{28,24},{1,5},{5... | collective-permute-start | bytes 1179656 | tf_op jit(solution)/shard_map/ppermute | solution.py:429
  9.0 2.0 %collective-permute-start.6 = (f32[768,128]{1,0:T(8,128)S(1)}, f32[768,128]{1,0:T(8,128)S(1)}, u32[]{:S(2)}, u32[]{:S(2)}) collective-permute-start(f32[768,128]{1,0:T(8,128)S(1)} %get-tuple-element.36), channel_id=1, source_target_pairs={{4,8},{8,4},{12,16},{16,12},{20,24},{24,20},{5,9},{9,5},{13,17},{1... | collective-permute-start | bytes 1179656 | tf_op jit(solution)/shard_map/ppermute | solution.py:428
  11.0 0.0 collective-permute-done.near_ref
  11.0 2.6 %collective-permute-done.1.far_ref = f32[864,128]{1,0:T(8,128)S(1)} collective-permute-done((f32[864,128]{1,0:T(8,128)S(1)}, f32[864,128]{1,0:T(8,128)S(1)}, u32[]{:S(2)}, u32[]{:S(2)}) %collective-permute-start.1) | collective-permute-done | bytes 442400 | tf_op jit(solution)/shard_map/ppermute | solution.py:428
  13.6 0.0 copy-start.7
  13.7 0.0 copy-start.6
  13.7 0.0 copy-start.1
  13.7 0.0 copy-start.2
  13.7 0.0 copy-start.3
  13.7 0.0 copy-start.4
  13.7 0.0 copy-start.5
  13.7 7.3 %transport.2 = (f32[512,128]{1,0:T(8,128)S(1)}, f32[512,128]{1,0:T(8,128)S(1)}, f32[512,128]{1,0:T(8,128)S(1)}, f32[512,128]{1,0:T(8,128)S(1)}) custom-call(f32[2048,128]{1,0:T(8,128)S(1)} %get-tuple-element.24.field_ref, f32[192,128]{1,0:T(8,128)S(1)} %get-tuple-element.25.courant_ref, f32[96,128]{1,0:T(8,128)S(1)} %slice.8.near_edge, ...), custom_call_target="tpu_custom_call" | custom-call | flops 104857600 | tf_op jit(solution)/shard_map/transport/pallas_call | solution.py:361
  21.0 1.6 %collective-permute-start.2 = (f32[512,128]{1,0:T(8,128)S(1)}, f32[512,128]{1,0:T(8,128)S(1)}, u32[]{:S(2)}, u32[]{:S(2)}) collective-permute-start(f32[512,128]{1,0:T(8,128)S(1)} %get-tuple-element.29), channel_id=1, source_target_pairs={{0,1},{1,0},{2,3},{3,2},{4,5},{5,4},{6,7},{7,6},{8,9},{9,8},{10,11... | collective-permute-start | bytes 786440 | tf_op jit(solution)/shard_map/ppermute | solution.py:441
  22.6 1.6 %collective-permute-start.3 = (f32[512,128]{1,0:T(8,128)S(1)}, f32[512,128]{1,0:T(8,128)S(1)}, u32[]{:S(2)}, u32[]{:S(2)}) collective-permute-start(f32[512,128]{1,0:T(8,128)S(1)} %get-tuple-element.30), channel_id=1, source_target_pairs={{0,2},{1,3},{2,0},{3,1},{4,6},{5,7},{6,4},{7,5},{8,10},{9,11},{10,... | collective-permute-start | bytes 786440 | tf_op jit(solution)/shard_map/ppermute | solution.py:441
  24.2 0.3 collective-permute-start.4
  24.6 0.0 collective-permute-done.5.near_ref
  24.6 0.0 collective-permute-done.6.far_ref
  24.6 7.3 %transport.3 = (f32[512,128]{1,0:T(8,128)S(1)}, f32[512,128]{1,0:T(8,128)S(1)}, f32[512,128]{1,0:T(8,128)S(1)}, f32[512,128]{1,0:T(8,128)S(1)}) custom-call(f32[2048,128]{1,0:T(8,128)S(1)} %get-tuple-element.34.field_ref, f32[192,128]{1,0:T(8,128)S(1)} %get-tuple-element.25.courant_ref, f32[96,128]{1,0:T(8,128)S(1)} %slice.8.near_edge, ...), custom_call_target="tpu_custom_call" | custom-call | flops 104857600 | tf_op jit(solution)/shard_map/transport/pallas_call | solution.py:361
  31.9 1.6 %collective-permute-start.7 = (f32[512,128]{1,0:T(8,128)S(1)}, f32[512,128]{1,0:T(8,128)S(1)}, u32[]{:S(2)}, u32[]{:S(2)}) collective-permute-start(f32[512,128]{1,0:T(8,128)S(1)} %get-tuple-element.38), channel_id=1, source_target_pairs={{0,1},{1,0},{2,3},{3,2},{4,5},{5,4},{6,7},{7,6},{8,9},{9,8},{10,11... | collective-permute-start | bytes 786440 | tf_op jit(solution)/shard_map/ppermute | solution.py:441
  33.4 1.8 %collective-permute-start.8 = (f32[512,128]{1,0:T(8,128)S(1)}, f32[512,128]{1,0:T(8,128)S(1)}, u32[]{:S(2)}, u32[]{:S(2)}) collective-permute-start(f32[512,128]{1,0:T(8,128)S(1)} %get-tuple-element.39), channel_id=1, source_target_pairs={{0,2},{1,3},{2,0},{3,1},{4,6},{5,7},{6,4},{7,5},{8,10},{9,11},{10,... | collective-permute-start | bytes 786440 | tf_op jit(solution)/shard_map/ppermute | solution.py:441
  35.2 0.0 collective-permute-done.2.refs_1_
  35.2 0.2 collective-permute-start.9
  35.4 0.0 copy-done.7
  35.4 0.1 broadcast_in_dim.7
  35.5 0.0 copy-done.6
  35.5 0.1 broadcast_in_dim.8.lit_ref.refs_8_
  35.6 0.0 copy-done.1
  35.6 0.0 copy-done.2
  35.6 0.0 copy-done.3
  35.6 0.0 copy-done.4
  35.6 0.0 copy-done.5
  35.6 3.8 %rates.1.refs_9_ = f32[12288,128]{1,0:T(8,128)S(1)} custom-call(f32[16,128]{1,0:T(8,128)S(1)} %bitcast.30, f32[16,128]{1,0:T(8,128)S(1)} %bitcast.31, s32[16,128]{1,0:T(8,128)S(1)} %broadcast_in_dim.8.lit_ref.refs_8_, f32[768]{0:T(1024)S(1)} %copy-done.3, f32[768]{0:T(1024)S(1)} %copy-done.4, f32[768]{0:T(1024)S(1)} %copy-done.5), custom_call_target="tpu_custom_call" | custom-call | flops 62914560 | tf_op jit(solution)/shard_map/rates/pallas_call | solution.py:375
  39.4 0.0 collective-permute-done.3.refs_2_
  39.4 0.0 collective-permute-done.4.refs_3_
  39.4 2.1 %collective-permute-done.7.refs_5_ = f32[512,128]{1,0:T(8,128)S(1)} collective-permute-done((f32[512,128]{1,0:T(8,128)S(1)}, f32[512,128]{1,0:T(8,128)S(1)}, u32[]{:S(2)}, u32[]{:S(2)}) %collective-permute-start.7) | collective-permute-done | bytes 262176 | tf_op jit(solution)/shard_map/ppermute | solution.py:441
  41.6 5.8 %collective-permute-done.8.refs_6_ = f32[512,128]{1,0:T(8,128)S(1)} collective-permute-done((f32[512,128]{1,0:T(8,128)S(1)}, f32[512,128]{1,0:T(8,128)S(1)}, u32[]{:S(2)}, u32[]{:S(2)}) %collective-permute-start.8) | collective-permute-done | bytes 262176 | tf_op jit(solution)/shard_map/ppermute | solution.py:441
  47.3 0.8 %collective-permute-done.9.refs_7_ = f32[512,128]{1,0:T(8,128)S(1)} collective-permute-done((f32[512,128]{1,0:T(8,128)S(1)}, f32[512,128]{1,0:T(8,128)S(1)}, u32[]{:S(2)}, u32[]{:S(2)}) %collective-permute-start.9) | collective-permute-done | bytes 262176 | tf_op jit(solution)/shard_map/ppermute | solution.py:441
  48.2 12.9 %chemistry.1 = f32[4096,128]{1,0:T(8,128)} custom-call(f32[512,128]{1,0:T(8,128)S(1)} %get-tuple-element.28.refs_0_, f32[512,128]{1,0:T(8,128)S(1)} %collective-permute-done.2.refs_1_, f32[512,128]{1,0:T(8,128)S(1)} %collective-permute-done.3.refs_2_, f32[512,128]{1,0:T(8,128)S(1)} %collective-permute-done.4.refs_3_, ...), custom_call_target="tpu_custom_call" | custom-call | tf_op jit(solution)/shard_map/chemistry/pallas_call | solution.py:390
  (4 shorter events, 0.0 us)
Async XLA Ops:
  0.8 1.6 %copy-start = (f32[64,2,16,256]{3,2,1,0:T(8,128)S(1)}, f32[64,2,16,256]{3,2,1,0:T(8,128)}, u32[]{:S(2)}) copy-start(f32[64,2,16,256]{3,2,1,0:T(8,128)} %param.11) | copy-start | bytes 6291460
  3.9 7.0 %collective-permute-start = (f32[864,128]{1,0:T(8,128)S(1)}, f32[864,128]{1,0:T(8,128)S(1)}, u32[]{:S(2)}, u32[]{:S(2)}) collective-permute-start(f32[864,128]{1,0:T(8,128)S(1)} %get-tuple-element.26), channel_id=1, source_target_pairs={{0,4},{4,0},{8,12},{12,8},{16,20},{20,16},{24,28},{28,24},{1,5},{5... | collective-permute-start | bytes 1327112 | tf_op jit(solution)/shard_map/ppermute | solution.py:429
  4.0 9.6 %collective-permute-start.1 = (f32[864,128]{1,0:T(8,128)S(1)}, f32[864,128]{1,0:T(8,128)S(1)}, u32[]{:S(2)}, u32[]{:S(2)}) collective-permute-start(f32[864,128]{1,0:T(8,128)S(1)} %get-tuple-element.27), channel_id=1, source_target_pairs={{4,8},{8,4},{12,16},{16,12},{20,24},{24,20},{5,9},{9,5},{13,17},{1... | collective-permute-start | bytes 1327112 | tf_op jit(solution)/shard_map/ppermute | solution.py:428
  7.8 16.8 %collective-permute-start.5 = (f32[768,128]{1,0:T(8,128)S(1)}, f32[768,128]{1,0:T(8,128)S(1)}, u32[]{:S(2)}, u32[]{:S(2)}) collective-permute-start(f32[768,128]{1,0:T(8,128)S(1)} %get-tuple-element.35), channel_id=1, source_target_pairs={{0,4},{4,0},{8,12},{12,8},{16,20},{20,16},{24,28},{28,24},{1,5},{5... | collective-permute-start | bytes 1179656 | tf_op jit(solution)/shard_map/ppermute | solution.py:429
  9.0 15.6 %collective-permute-start.6 = (f32[768,128]{1,0:T(8,128)S(1)}, f32[768,128]{1,0:T(8,128)S(1)}, u32[]{:S(2)}, u32[]{:S(2)}) collective-permute-start(f32[768,128]{1,0:T(8,128)S(1)} %get-tuple-element.36), channel_id=1, source_target_pairs={{4,8},{8,4},{12,16},{16,12},{20,24},{24,20},{5,9},{9,5},{13,17},{1... | collective-permute-start | bytes 1179656 | tf_op jit(solution)/shard_map/ppermute | solution.py:428
  13.6 21.8 %copy-start.7 = (s32[2,4,2]{1,2,0:T(2,128)S(1)}, s32[2,4,2]{1,2,0:T(2,128)}, u32[]{:S(2)}) copy-start(s32[2,4,2]{1,2,0:T(2,128)} %param.17) | copy-start | bytes 196
  13.7 21.9 %copy-start.6 = (s32[3,768]{1,0:T(4,128)S(1)}, s32[3,768]{1,0:T(4,128)}, u32[]{:S(2)}) copy-start(s32[3,768]{1,0:T(4,128)} %param.21) | copy-start | bytes 27652
  13.7 22.0 %copy-start.1 = (f32[2,4,256]{2,1,0:T(4,128)S(1)}, f32[2,4,256]{2,1,0:T(4,128)}, u32[]{:S(2)}) copy-start(f32[2,4,256]{2,1,0:T(4,128)} %param.15) | copy-start | bytes 24580
  13.7 21.9 %copy-start.2 = (f32[2,4,256]{2,1,0:T(4,128)S(1)}, f32[2,4,256]{2,1,0:T(4,128)}, u32[]{:S(2)}) copy-start(f32[2,4,256]{2,1,0:T(4,128)} %param.16) | copy-start | bytes 24580
  13.7 21.9 %copy-start.3 = (f32[768]{0:T(1024)S(1)}, f32[768]{0:T(1024)}, u32[]{:S(2)}) copy-start(f32[768]{0:T(1024)} %rate_ref.1) | copy-start | bytes 9220
  13.7 21.9 %copy-start.4 = (f32[768]{0:T(1024)S(1)}, f32[768]{0:T(1024)}, u32[]{:S(2)}) copy-start(f32[768]{0:T(1024)} %barrier_ref.1) | copy-start | bytes 9220
  13.7 21.9 %copy-start.5 = (f32[768]{0:T(1024)S(1)}, f32[768]{0:T(1024)}, u32[]{:S(2)}) copy-start(f32[768]{0:T(1024)} %photo_ref.1) | copy-start | bytes 9220
  21.0 14.2 %collective-permute-start.2 = (f32[512,128]{1,0:T(8,128)S(1)}, f32[512,128]{1,0:T(8,128)S(1)}, u32[]{:S(2)}, u32[]{:S(2)}) collective-permute-start(f32[512,128]{1,0:T(8,128)S(1)} %get-tuple-element.29), channel_id=1, source_target_pairs={{0,1},{1,0},{2,3},{3,2},{4,5},{5,4},{6,7},{7,6},{8,9},{9,8},{10,11... | collective-permute-start | bytes 786440 | tf_op jit(solution)/shard_map/ppermute | solution.py:441
  22.6 16.8 %collective-permute-start.3 = (f32[512,128]{1,0:T(8,128)S(1)}, f32[512,128]{1,0:T(8,128)S(1)}, u32[]{:S(2)}, u32[]{:S(2)}) collective-permute-start(f32[512,128]{1,0:T(8,128)S(1)} %get-tuple-element.30), channel_id=1, source_target_pairs={{0,2},{1,3},{2,0},{3,1},{4,6},{5,7},{6,4},{7,5},{8,10},{9,11},{10,... | collective-permute-start | bytes 786440 | tf_op jit(solution)/shard_map/ppermute | solution.py:441
  24.2 15.2 %collective-permute-start.4 = (f32[512,128]{1,0:T(8,128)S(1)}, f32[512,128]{1,0:T(8,128)S(1)}, u32[]{:S(2)}, u32[]{:S(2)}) collective-permute-start(f32[512,128]{1,0:T(8,128)S(1)} %get-tuple-element.31), channel_id=1, source_target_pairs={{0,3},{1,2},{2,1},{3,0},{4,7},{5,6},{6,5},{7,4},{8,11},{9,10},{10,... | collective-permute-start | bytes 786440 | tf_op jit(solution)/shard_map/ppermute | solution.py:441
  31.9 9.7 %collective-permute-start.7 = (f32[512,128]{1,0:T(8,128)S(1)}, f32[512,128]{1,0:T(8,128)S(1)}, u32[]{:S(2)}, u32[]{:S(2)}) collective-permute-start(f32[512,128]{1,0:T(8,128)S(1)} %get-tuple-element.38), channel_id=1, source_target_pairs={{0,1},{1,0},{2,3},{3,2},{4,5},{5,4},{6,7},{7,6},{8,9},{9,8},{10,11... | collective-permute-start | bytes 786440 | tf_op jit(solution)/shard_map/ppermute | solution.py:441
  33.4 13.9 %collective-permute-start.8 = (f32[512,128]{1,0:T(8,128)S(1)}, f32[512,128]{1,0:T(8,128)S(1)}, u32[]{:S(2)}, u32[]{:S(2)}) collective-permute-start(f32[512,128]{1,0:T(8,128)S(1)} %get-tuple-element.39), channel_id=1, source_target_pairs={{0,2},{1,3},{2,0},{3,1},{4,6},{5,7},{6,4},{7,5},{8,10},{9,11},{10,... | collective-permute-start | bytes 786440 | tf_op jit(solution)/shard_map/ppermute | solution.py:441
  35.2 12.9 %collective-permute-start.9 = (f32[512,128]{1,0:T(8,128)S(1)}, f32[512,128]{1,0:T(8,128)S(1)}, u32[]{:S(2)}, u32[]{:S(2)}) collective-permute-start(f32[512,128]{1,0:T(8,128)S(1)} %get-tuple-element.40), channel_id=1, source_target_pairs={{0,3},{1,2},{2,1},{3,0},{4,7},{5,6},{6,5},{7,4},{8,11},{9,10},{10,... | collective-permute-start | bytes 786440 | tf_op jit(solution)/shard_map/ppermute | solution.py:441

commit v7 on v6

--- a/solution.py
+++ b/solution.py
@@ -17,6 +17,7 @@
 PARTS = 2
 TOGETHER = 8
 CHUNK = 8
+BATCHES = 4
 LOG2E = 1.4426950408889634
 
 
@@ -37,6 +38,9 @@
         self.stride = self.levels * self.rows * self.tiles
         self.columns = self.levels * self.tiles
         self.count = self.species // PARTS
+        self.area = self.tiles * self.part
+        self.slices = self.levels if self.area % SUB == 0 else 1
+        self.slab = self.blocks // self.slices
         self.halo_rows = LOW * self.columns * self.count
         self.span = self.rows + 2 * SUB
         self.edge_rows = 3 * self.columns * SUB
@@ -129,10 +133,11 @@
     lax.fori_loop(0, z.count, edges, 0, unroll=4)
 
 
-def transport_kernel(z, field_ref, courant_ref, near_edge, far_edge, near_ref, far_ref, *refs):
+def transport_kernel(z, slices, field_ref, courant_ref, near_edge, far_edge, near_ref, far_ref, *refs):
     span = z.span
     cols = range(z.columns)
-    outs, (coef, final, natural, halo, edge), slots = refs[: z.groups], refs[z.groups : z.groups + 5], refs[z.groups + 5 :]
+    total = z.groups * slices
+    outs, (coef, final, natural, halo, edge), slots = refs[:total], refs[total : total + 5], refs[total + 5 :]
     odd = lax.rem(lax.axis_index("space"), 2)
     for source, above in ((near_ref, 1 - odd), (far_ref, odd)):
 
@@ -236,10 +241,13 @@
             for tile in range(z.tiles):
                 strip = one * z.tiles + tile
                 natural[pl.ds(strip * z.rows, z.rows), :] = parts[tile][one * z.rows : (one + 1) * z.rows]
-        for k, out_ref in enumerate(outs):
+        share = z.columns // slices
+        for k in range(z.groups):
             first = (me ^ k) * z.part
             for strip in range(many * z.tiles):
-                at = index * CHUNK * z.blocks + strip * z.part
+                one, col = divmod(strip, z.columns)
+                out_ref = outs[k * slices + col // share]
+                at = ((index * CHUNK + one) * share + col % share) * z.part
                 out_ref[pl.ds(at, z.part), :] = natural[pl.ds(strip * z.rows + first, z.part), :]
         return carry
 
@@ -262,16 +270,18 @@
     lax.fori_loop(0, rate_ref.shape[0], one, 0, unroll=8)
 
 
-def chemistry_kernel(z, species, *refs):
-    pieces = z.blocks // SUB
-    sources = refs[: PARTS * z.groups]
-    lit_ref, k_ref, table_ref, out_ref, state, made, lost_a, lost_b = refs[PARTS * z.groups :]
+def chemistry_kernel(z, species, number, *refs):
+    pieces = z.slab // SUB
+    total = PARTS * z.groups
+    sources, (lit_ref, k_ref, table_ref) = refs[:total], refs[total : total + 3]
+    out_hbm, result, state, made, lost_a, lost_b, sems = refs[-7:]
     reactions = k_ref.shape[0] // z.blocks
+    base = number * z.slab
 
     def cell(row, piece):
         return pl.ds(pl.multiple_of(row, SUB) + piece * SUB, SUB)
 
-    lit = [lit_ref[pl.ds(p * SUB, SUB), :] == 1 for p in range(pieces)]
+    lit = [lit_ref[pl.ds(base + p * SUB, SUB), :] == 1 for p in range(pieces)]
     steps = [jnp.where(lit[p], float(DAY_STEPS), 1.0) for p in range(pieces)]
     zero = jnp.zeros((SUB, LANES), jnp.float32)
     me = lax.axis_index("tracer")
@@ -282,12 +292,15 @@
         lost_b[at, :] = zero
 
     def begin(index, carry):
-        for number, ref in enumerate(sources):
-            part, k = divmod(number, z.groups)
+        for i, ref in enumerate(sources):
+            part, k = divmod(i, z.groups)
             first = (me ^ k) * z.species + part * z.count
             for p in range(pieces):
-                value = ref[cell(index * z.blocks, p), :]
-                at = cell((first + index) * z.blocks, p)
+                if part < PARTS - 1:
+                    value = ref[cell(index * z.blocks + base, p), :]
+                else:
+                    value = ref[cell(index * z.slab, p), :]
+                at = cell((first + index) * z.slab, p)
                 state[at, :] = value
                 prepare(at, p, value)
         return carry
@@ -297,7 +310,7 @@
     def react(r, carry):
         first, second, product = table_ref[r], table_ref[reactions + r], table_ref[2 * reactions + r]
         for p in range(pieces):
-            k = k_ref[cell(r * z.blocks, p), :]
+            k = k_ref[cell(r * z.blocks + base, p), :]
             x = state[cell(first, p), :]
             y = state[cell(second, p), :]
             kx = k * x
@@ -307,12 +320,18 @@
             lost_b[cell(second, p), :] += kx
         return carry
 
+    batch = species // BATCHES
+
+    def export(i):
+        rows = pl.ds(i * batch, batch)
+        return pltpu.make_async_copy(result.at[rows], out_hbm.at[rows, pl.ds(base, z.slab)], sems.at[i])
+
     for sub in range(DAY_STEPS):
         lax.fori_loop(0, reactions, react, 0, unroll=16)
 
         def finish(s, carry):
             for p in range(pieces):
-                at = cell(s * z.blocks, p)
+                at = cell(s * z.slab, p)
                 value = made[at, :] / (lost_a[at, :] + lost_b[at, :])
                 if sub < DAY_STEPS - 1:
                     prepare(at, p, value)
@@ -320,10 +339,16 @@
                         state[at, :] = value
                 if sub > 0:
                     value = jnp.where(lit[p], value, state[at, :])
-                    out_ref[at, :] = value
+                    result[s, pl.ds(p * SUB, SUB), :] = value
             return carry
 
-        lax.fori_loop(0, species, finish, 0, unroll=4)
+        if sub < DAY_STEPS - 1:
+            lax.fori_loop(0, species, finish, 0, unroll=8)
+    for i in range(BATCHES):
+        lax.fori_loop(i * batch, (i + 1) * batch, finish, 0, unroll=8)
+        export(i).start()
+    for i in range(BATCHES):
+        export(i).wait()
 
 
 VMEM = pl.BlockSpec(memory_space=pltpu.VMEM)
@@ -354,15 +379,15 @@
     )(*flat)
 
 
-def transport(z, *flat):
+def transport(z, slices, *flat):
     size = z.span * z.columns
     scratch = [6 * size, z.count * z.columns * z.rows, CHUNK * z.columns * z.rows]
     scratch += [2 * z.halo_rows, 2 * z.edge_rows] + [size] * (4 * TOGETHER)
     return pl.pallas_call(
-        functools.partial(transport_kernel, z),
-        out_shape=(rows_of(z.count * z.blocks),) * z.groups,
+        functools.partial(transport_kernel, z, slices),
+        out_shape=(rows_of(z.count * z.blocks // slices),) * (z.groups * slices),
         in_specs=[VMEM] * len(flat),
-        out_specs=(VMEM,) * z.groups,
+        out_specs=(VMEM,) * (z.groups * slices),
         scratch_shapes=[pltpu.VMEM((n, LANES), jnp.float32) for n in scratch],
         compiler_params=pltpu.CompilerParams(vmem_limit_bytes=20 << 20),
         cost_estimate=pl.CostEstimate(flops=400 * z.count * z.stride * LANES, bytes_accessed=0, transcendentals=0),
@@ -385,17 +410,23 @@
     )(warm, glow, lit, rate, barrier, photo)
 
 
-def chemistry(z, species, arrived, lit, k, table):
-    size = species * z.blocks
+def chemistry(z, species, number, arrived, lit, k, table, out):
+    size = species * z.slab
+    more = () if out is None else (out,)
+    args = (*arrived, lit, k, table, *more)
+    scratch = [pltpu.VMEM((species, z.slab, LANES), jnp.float32)]
+    scratch += [pltpu.VMEM((size, LANES), jnp.float32)] * 4 + [pltpu.SemaphoreType.DMA((BATCHES,))]
     return pl.pallas_call(
-        functools.partial(chemistry_kernel, z, species),
-        out_shape=rows_of(size),
-        in_specs=[VMEM] * (len(arrived) + 2) + [SMEM],
-        out_specs=VMEM,
-        scratch_shapes=[pltpu.VMEM((size, LANES), jnp.float32)] * 4,
+        functools.partial(chemistry_kernel, z, species, number),
+        out_shape=jax.ShapeDtypeStruct((species, z.blocks, LANES), jnp.float32),
+        in_specs=[VMEM] * (len(arrived) + 2) + [SMEM] + [ANY] * len(more),
+        out_specs=ANY,
+        scratch_shapes=scratch,
+        input_output_aliases={len(args) - 1: 0} if more else {},
         compiler_params=pltpu.CompilerParams(vmem_limit_bytes=20 << 20),
+        cost_estimate=pl.CostEstimate(flops=400 * size * LANES, bytes_accessed=0, transcendentals=0),
         name="chemistry",
-    )(*arrived, lit, k, table)
+    )(*args)
 
 
 def body(
@@ -430,15 +461,21 @@
         fields.append(ready)
         halos.append((near, far))
     edges = [halo[z.halo_rows :] for halo in halos[0]]
-    arrived = []
+    arrived = [[] for _ in range(z.slices)]
     for part in range(PARTS):
         ready = fields[part]
+        slices = z.slices if part == PARTS - 1 else 1
         if part > 0:
             ready, _ = lax.optimization_barrier((ready, moved[0]))
-        moved = transport(z, ready, courant, *edges, *halos[part])
-        arrived.append(moved[0])
-        for k in range(1, groups):
-            arrived.append(lax.ppermute(moved[k], "tracer", [(i, i ^ k) for i in range(groups)]))
+        moved = transport(z, slices, ready, courant, *edges, *halos[part])
+        for piece in range(slices):
+            for k in range(groups):
+                block = moved[k * slices + piece]
+                if k > 0:
+                    block = lax.ppermute(block, "tracer", [(i, i ^ k) for i in range(groups)])
+                for number in range(z.slices):
+                    if slices == 1 or number == piece:
+                        arrived[number].append(block)
     mask, table, _ = lax.optimization_barrier((daylight_mask, stoichiometry_table, moved[0]))
     lit = jnp.broadcast_to(jnp.moveaxis(mask, 2, 1).reshape(z.blocks, 1), (z.blocks, LANES))
     k = rates(
@@ -451,7 +488,10 @@
         photodissociation_factor,
     )
     species = z.species * groups
-    out = chemistry(z, species, arrived, lit, k, table.reshape(-1) * z.blocks)
+    table = table.reshape(-1) * z.slab
+    out = None
+    for number in range(z.slices):
+        out = chemistry(z, species, number, arrived[number], lit, k, table, out)
     out = out.reshape(species, z.levels, z.tiles, z.part, LANES)
     return jnp.moveaxis(out, 2, 3).reshape(species, z.levels, z.part, z.width)
 

time: 61.4 us -> 75.9 us (1.24); the launches traced: 61 us -> 74.5 us
  Pallas kernels: 34.1 us -> 42.8 us
  starting transfers between devices: 12.8 us -> 20 us
  waiting for transfers between devices: 11.4 us -> 8.91 us
    pallas_call x3 -> x4, Pallas kernels: 27.5 us -> 36.3 us  [the longest x2 21.7 us: chemistry(): pl.pallas_call(functools.partial(chemistry_kernel, z, species, number), o...]
    ppermute x6 -> x9, starting transfers between devices: 7.11 us -> 14.2 us  [body(): block = lax.ppermute(block, 'tracer', [(i, i ^ k) for i in range(groups)])]
    ppermute x6 -> x9, waiting for transfers between devices: 8.73 us -> 6.26 us  [body(): block = lax.ppermute(block, 'tracer', [(i, i ^ k) for i in range(groups)])]
  transfers between devices with their start and end apart: 10 -> 13, of which waited for: 4 -> 4; matrix products, arithmetic and copies ran while one was open for 0% -> 0% of each run, Pallas kernels for 32% -> 41%
where the time goes in v7:
time: 75.9 us; the launch traced here: 74.5 us
  Pallas kernels  42.8 us (56%)
  starting transfers between devices  20 us (26%)
  waiting for transfers between devices  8.91 us (12%)
  local copies, waits for them, and re-layouts  1.8 us (2%)
  other arithmetic  0.8 us (1%)
    pallas_call x2, Pallas kernels, chemistry(): pl.pallas_call(functools.partial(chemistry_kernel, z, species, number), o...  21.7 us
    pallas_call x2, Pallas kernels, transport(): pl.pallas_call(functools.partial(transport_kernel, z, slices), out_shape=...  14.6 us
    ppermute x9, starting transfers between devices, body(): block = lax.ppermute(block, 'tracer', [(i, i ^ k) for i in range(groups)])  14.2 us
    ppermute x9, waiting for transfers between devices, body(): block = lax.ppermute(block, 'tracer', [(i, i ^ k) for i in range(groups)])  6.26 us
    ppermute x2, starting transfers between devices, body(): far = lax.ppermute(far, 'space', far_pairs)  4.43 us
    pallas_call x1, Pallas kernels, rates(): pl.pallas_call(functools.partial(rates_kernel, z.blocks // SUB), out_shap...  3.76 us
    pallas_call x2, Pallas kernels, pack(): pl.pallas_call(functools.partial(pack_kernel, z, part), out_shape=tuple((...  2.83 us
    ppermute x2, waiting for transfers between devices, body(): far = lax.ppermute(far, 'space', far_pairs)  2.65 us
  transfers between devices with their start and end apart: 13, of which 4 were waited for; matrix products, arithmetic and copies ran while one was open for 0% of the time, Pallas kernels for 41%

profile of v7, /device:TPU:16, one launch (start us, length us, event | category | flops | bytes accessed | tf_op | source)
XLA Modules:
  0.0 74.5 jit_solution(10840470364001288650)
XLA Ops:
  0.0 0.8 %pad_maximum_fusion = f32[3,2,2,8,2,128]{5,3,4,2,1,0:T(8,128)S(1)} fusion(f32[1,2,2,8,2,128]{5,3,4,2,1,0:T(8,128)} %bitcast.32, f32[1,2,2,8,2,128]{5,3,4,2,1,0:T(8,128)} %bitcast.33, f32[1,2,2,8,2,128]{5,3,4,2,1,0:T(8,128)} %bitcast.34), kind=kLoop, calls=%fused_computation | loop fusion | flops 49152 | bytes 196608 | tf_op jit(solution)/shard_map/stack | solution.py:448
  0.8 1.6 %copy-done = f32[64,2,16,256]{3,2,1,0:T(8,128)S(1)} copy-done((f32[64,2,16,256]{3,2,1,0:T(8,128)S(1)}, f32[64,2,16,256]{3,2,1,0:T(8,128)}, u32[]{:S(2)}) %copy-start) | copy-done | bytes 2097176
  2.4 1.5 %pack.2 = (f32[864,128]{1,0:T(8,128)S(1)}, f32[864,128]{1,0:T(8,128)S(1)}, f32[2048,128]{1,0:T(8,128)S(1)}, f32[192,128]{1,0:T(8,128)S(1)}) custom-call(f32[4096,128]{1,0:T(8,128)S(1)} %bitcast.27, f32[192,128]{1,0:T(8,128)S(1)} %bitcast.29), custom_call_target="tpu_custom_call" | custom-call | flops 26214400 | tf_op jit(solution)/shard_map/pack/pallas_call | solution.py:371
  3.9 0.1 collective-permute-start
  4.0 2.4 %collective-permute-start.1 = (f32[864,128]{1,0:T(8,128)S(1)}, f32[864,128]{1,0:T(8,128)S(1)}, u32[]{:S(2)}, u32[]{:S(2)}) collective-permute-start(f32[864,128]{1,0:T(8,128)S(1)} %get-tuple-element.31), channel_id=1, source_target_pairs={{4,8},{8,4},{12,16},{16,12},{20,24},{24,20},{5,9},{9,5},{13,17},{1... | collective-permute-start | bytes 1327112 | tf_op jit(solution)/shard_map/ppermute | solution.py:459
  6.5 1.3 %pack.3 = (f32[768,128]{1,0:T(8,128)S(1)}, f32[768,128]{1,0:T(8,128)S(1)}, f32[2048,128]{1,0:T(8,128)S(1)}) custom-call(f32[4096,128]{1,0:T(8,128)S(1)} %bitcast.28), custom_call_target="tpu_custom_call" | custom-call | flops 26214400 | tf_op jit(solution)/shard_map/pack/pallas_call | solution.py:371
  7.8 1.2 %collective-permute-start.5 = (f32[768,128]{1,0:T(8,128)S(1)}, f32[768,128]{1,0:T(8,128)S(1)}, u32[]{:S(2)}, u32[]{:S(2)}) collective-permute-start(f32[768,128]{1,0:T(8,128)S(1)} %get-tuple-element.39), channel_id=1, source_target_pairs={{0,4},{4,0},{8,12},{12,8},{16,20},{20,16},{24,28},{28,24},{1,5},{5... | collective-permute-start | bytes 1179656 | tf_op jit(solution)/shard_map/ppermute | solution.py:460
  9.0 2.0 %collective-permute-start.6 = (f32[768,128]{1,0:T(8,128)S(1)}, f32[768,128]{1,0:T(8,128)S(1)}, u32[]{:S(2)}, u32[]{:S(2)}) collective-permute-start(f32[768,128]{1,0:T(8,128)S(1)} %get-tuple-element.40), channel_id=1, source_target_pairs={{4,8},{8,4},{12,16},{16,12},{20,24},{24,20},{5,9},{9,5},{13,17},{1... | collective-permute-start | bytes 1179656 | tf_op jit(solution)/shard_map/ppermute | solution.py:459
  11.0 0.0 collective-permute-done.near_ref
  11.0 2.6 %collective-permute-done.1.far_ref = f32[864,128]{1,0:T(8,128)S(1)} collective-permute-done((f32[864,128]{1,0:T(8,128)S(1)}, f32[864,128]{1,0:T(8,128)S(1)}, u32[]{:S(2)}, u32[]{:S(2)}) %collective-permute-start.1) | collective-permute-done | bytes 442400 | tf_op jit(solution)/shard_map/ppermute | solution.py:459
  13.7 0.0 copy-start.1
  13.7 0.0 copy-start.2
  13.7 0.0 copy-start.3
  13.7 0.0 copy-start.4
  13.7 0.0 copy-start.5
  13.7 7.3 %transport.2 = (f32[512,128]{1,0:T(8,128)S(1)}, f32[512,128]{1,0:T(8,128)S(1)}, f32[512,128]{1,0:T(8,128)S(1)}, f32[512,128]{1,0:T(8,128)S(1)}) custom-call(f32[2048,128]{1,0:T(8,128)S(1)} %get-tuple-element.28.field_ref, f32[192,128]{1,0:T(8,128)S(1)} %get-tuple-element.29.courant_ref, f32[96,128]{1,0:T(8,128)S(1)} %slice.8.near_edge, ...), custom_call_target="tpu_custom_call" | custom-call | flops 104857600 | tf_op jit(solution)/shard_map/transport/pallas_call | solution.py:386
  21.0 1.6 %collective-permute-start.2 = (f32[512,128]{1,0:T(8,128)S(1)}, f32[512,128]{1,0:T(8,128)S(1)}, u32[]{:S(2)}, u32[]{:S(2)}) collective-permute-start(f32[512,128]{1,0:T(8,128)S(1)} %get-tuple-element.33), channel_id=1, source_target_pairs={{0,1},{1,0},{2,3},{3,2},{4,5},{5,4},{6,7},{7,6},{8,9},{9,8},{10,11... | collective-permute-start | bytes 786440 | tf_op jit(solution)/shard_map/ppermute | solution.py:475
  22.6 0.0 collective-permute-done.5.near_ref
  22.6 0.0 collective-permute-done.6.far_ref
  22.6 7.3 %transport.3 = (f32[256,128]{1,0:T(8,128)S(1)}, f32[256,128]{1,0:T(8,128)S(1)}, f32[256,128]{1,0:T(8,128)S(1)}, f32[256,128]{1,0:T(8,128)S(1)}, f32[256,128]{1,0...) custom-call(f32[2048,128]{1,0:T(8,128)S(1)} %get-tuple-element.38.field_ref, ...), custom_call_target="tpu_custom_call" | custom-call | flops 104857600 | tf_op jit(solution)/shard_map/transport/pallas_call | solution.py:386
  29.9 0.6 collective-permute-start.10
  30.5 1.8 %collective-permute-start.11 = (f32[256,128]{1,0:T(8,128)S(1)}, f32[256,128]{1,0:T(8,128)S(1)}, u32[]{:S(2)}, u32[]{:S(2)}) collective-permute-start(f32[256,128]{1,0:T(8,128)S(1)} %get-tuple-element.49), channel_id=1, source_target_pairs={{0,2},{1,3},{2,0},{3,1},{4,6},{5,7},{6,4},{7,5},{8,10},{9,11},{10,... | collective-permute-start | bytes 393224 | tf_op jit(solution)/shard_map/ppermute | solution.py:475
  32.2 1.2 %collective-permute-start.12 = (f32[256,128]{1,0:T(8,128)S(1)}, f32[256,128]{1,0:T(8,128)S(1)}, u32[]{:S(2)}, u32[]{:S(2)}) collective-permute-start(f32[256,128]{1,0:T(8,128)S(1)} %get-tuple-element.50), channel_id=1, source_target_pairs={{0,3},{1,2},{2,1},{3,0},{4,7},{5,6},{6,5},{7,4},{8,11},{9,10},{10,... | collective-permute-start | bytes 393224 | tf_op jit(solution)/shard_map/ppermute | solution.py:475
  33.4 1.8 %collective-permute-start.3 = (f32[512,128]{1,0:T(8,128)S(1)}, f32[512,128]{1,0:T(8,128)S(1)}, u32[]{:S(2)}, u32[]{:S(2)}) collective-permute-start(f32[512,128]{1,0:T(8,128)S(1)} %get-tuple-element.34), channel_id=1, source_target_pairs={{0,2},{1,3},{2,0},{3,1},{4,6},{5,7},{6,4},{7,5},{8,10},{9,11},{10,... | collective-permute-start | bytes 786440 | tf_op jit(solution)/shard_map/ppermute | solution.py:475
  35.2 1.1 %collective-permute-done.10.refs_5_ = f32[256,128]{1,0:T(8,128)S(1)} collective-permute-done((f32[256,128]{1,0:T(8,128)S(1)}, f32[256,128]{1,0:T(8,128)S(1)}, u32[]{:S(2)}, u32[]{:S(2)}) %collective-permute-start.10) | collective-permute-done | bytes 131104 | tf_op jit(solution)/shard_map/ppermute | solution.py:475
  36.3 1.7 %collective-permute-start.4 = (f32[512,128]{1,0:T(8,128)S(1)}, f32[512,128]{1,0:T(8,128)S(1)}, u32[]{:S(2)}, u32[]{:S(2)}) collective-permute-start(f32[512,128]{1,0:T(8,128)S(1)} %get-tuple-element.35), channel_id=1, source_target_pairs={{0,3},{1,2},{2,1},{3,0},{4,7},{5,6},{6,5},{7,4},{8,11},{9,10},{10,... | collective-permute-start | bytes 786440 | tf_op jit(solution)/shard_map/ppermute | solution.py:475
  38.0 0.0 copy-done.7
  38.0 0.1 broadcast_in_dim.7
  38.1 4.8 %collective-permute-done.11.refs_6_ = f32[256,128]{1,0:T(8,128)S(1)} collective-permute-done((f32[256,128]{1,0:T(8,128)S(1)}, f32[256,128]{1,0:T(8,128)S(1)}, u32[]{:S(2)}, u32[]{:S(2)}) %collective-permute-start.11) | collective-permute-done | bytes 131104 | tf_op jit(solution)/shard_map/ppermute | solution.py:475
  42.9 3.9 %collective-permute-start.7 = (f32[256,128]{1,0:T(8,128)S(1)}, f32[256,128]{1,0:T(8,128)S(1)}, u32[]{:S(2)}, u32[]{:S(2)}) collective-permute-start(f32[256,128]{1,0:T(8,128)S(1)} %get-tuple-element.42), channel_id=1, source_target_pairs={{0,1},{1,0},{2,3},{3,2},{4,5},{5,4},{6,7},{7,6},{8,9},{9,8},{10,11... | collective-permute-start | bytes 393224 | tf_op jit(solution)/shard_map/ppermute | solution.py:475
  46.8 0.0 collective-permute-done.12.refs_7_
  46.8 1.8 %collective-permute-start.8 = (f32[256,128]{1,0:T(8,128)S(1)}, f32[256,128]{1,0:T(8,128)S(1)}, u32[]{:S(2)}, u32[]{:S(2)}) collective-permute-start(f32[256,128]{1,0:T(8,128)S(1)} %get-tuple-element.43), channel_id=1, source_target_pairs={{0,2},{1,3},{2,0},{3,1},{4,6},{5,7},{6,4},{7,5},{8,10},{9,11},{10,... | collective-permute-start | bytes 393224 | tf_op jit(solution)/shard_map/ppermute | solution.py:475
  48.5 0.0 collective-permute-done.2.refs_1_
  48.5 0.0 collective-permute-start.9
  48.6 0.0 copy-done.6
  48.6 0.1 broadcast_in_dim.8.lit_ref.refs_8_
  48.7 0.0 copy-done.1
  48.7 0.0 copy-done.2
  48.7 0.0 copy-done.4
  48.7 0.0 copy-done.5
  48.7 3.8 %rates.1.refs_9_ = f32[12288,128]{1,0:T(8,128)S(1)} custom-call(f32[16,128]{1,0:T(8,128)S(1)} %bitcast.30, f32[16,128]{1,0:T(8,128)S(1)} %bitcast.31, s32[16,128]{1,0:T(8,128)S(1)} %broadcast_in_dim.8.lit_ref.refs_8_, f32[768]{0:T(1024)S(1)} %copy-done.3, f32[768]{0:T(1024)S(1)} %copy-done.4, f32[768]{0:T(1024)S(1)} %copy-done.5), custom_call_target="tpu_custom_call" | custom-call | flops 62914560 | tf_op jit(solution)/shard_map/rates/pallas_call | solution.py:400
  52.5 0.3 collective-permute-done.3.refs_2_
  52.8 0.0 collective-permute-done.4.refs_3_
  52.8 10.8 %chemistry.2.refs_11_ = f32[256,16,128]{2,1,0:T(8,128)} custom-call(f32[512,128]{1,0:T(8,128)S(1)} %get-tuple-element.32.refs_0_, f32[512,128]{1,0:T(8,128)S(1)} %collective-permute-done.2.refs_1_, f32[512,128]{1,0:T(8,128)S(1)} %collective-permute-done.3.refs_2_, f32[512,128]{1,0:T(8,128)S(1)} %collective-permute-done.4.refs_3_, ...), custom_call_target="tpu_custom_call" | custom-call | flops 104857600 | tf_op jit(solution)/shard_map/chemistry/pallas_call | solution.py:419
  63.7 0.0 collective-permute-done.7.refs_5_
  63.7 0.0 collective-permute-done.8.refs_6_
  63.7 0.0 collective-permute-done.9.refs_7_
  63.7 10.8 %chemistry.3 = f32[256,16,128]{2,1,0:T(8,128)} custom-call(f32[512,128]{1,0:T(8,128)S(1)} %get-tuple-element.32.refs_0_, f32[512,128]{1,0:T(8,128)S(1)} %collective-permute-done.2.refs_1_, f32[512,128]{1,0:T(8,128)S(1)} %collective-permute-done.3.refs_2_, f32[512,128]{1,0:T(8,128)S(1)} %collective-permute-done.4.refs_3_, ...), custom_call_target="tpu_custom_call", output_to_operand_aliasing={{}: (11, {})} | custom-call | flops 104857600 | tf_op jit(solution)/shard_map/chemistry/pallas_call | solution.py:419
  (8 shorter events, 0.0 us)
Async XLA Ops:
  0.8 1.6 %copy-start = (f32[64,2,16,256]{3,2,1,0:T(8,128)S(1)}, f32[64,2,16,256]{3,2,1,0:T(8,128)}, u32[]{:S(2)}) copy-start(f32[64,2,16,256]{3,2,1,0:T(8,128)} %param.11) | copy-start | bytes 6291460
  3.9 7.0 %collective-permute-start = (f32[864,128]{1,0:T(8,128)S(1)}, f32[864,128]{1,0:T(8,128)S(1)}, u32[]{:S(2)}, u32[]{:S(2)}) collective-permute-start(f32[864,128]{1,0:T(8,128)S(1)} %get-tuple-element.30), channel_id=1, source_target_pairs={{0,4},{4,0},{8,12},{12,8},{16,20},{20,16},{24,28},{28,24},{1,5},{5... | collective-permute-start | bytes 1327112 | tf_op jit(solution)/shard_map/ppermute | solution.py:460
  4.0 9.6 %collective-permute-start.1 = (f32[864,128]{1,0:T(8,128)S(1)}, f32[864,128]{1,0:T(8,128)S(1)}, u32[]{:S(2)}, u32[]{:S(2)}) collective-permute-start(f32[864,128]{1,0:T(8,128)S(1)} %get-tuple-element.31), channel_id=1, source_target_pairs={{4,8},{8,4},{12,16},{16,12},{20,24},{24,20},{5,9},{9,5},{13,17},{1... | collective-permute-start | bytes 1327112 | tf_op jit(solution)/shard_map/ppermute | solution.py:459
  7.8 14.8 %collective-permute-start.5 = (f32[768,128]{1,0:T(8,128)S(1)}, f32[768,128]{1,0:T(8,128)S(1)}, u32[]{:S(2)}, u32[]{:S(2)}) collective-permute-start(f32[768,128]{1,0:T(8,128)S(1)} %get-tuple-element.39), channel_id=1, source_target_pairs={{0,4},{4,0},{8,12},{12,8},{16,20},{20,16},{24,28},{28,24},{1,5},{5... | collective-permute-start | bytes 1179656 | tf_op jit(solution)/shard_map/ppermute | solution.py:460
  9.0 13.6 %collective-permute-start.6 = (f32[768,128]{1,0:T(8,128)S(1)}, f32[768,128]{1,0:T(8,128)S(1)}, u32[]{:S(2)}, u32[]{:S(2)}) collective-permute-start(f32[768,128]{1,0:T(8,128)S(1)} %get-tuple-element.40), channel_id=1, source_target_pairs={{4,8},{8,4},{12,16},{16,12},{20,24},{24,20},{5,9},{9,5},{13,17},{1... | collective-permute-start | bytes 1179656 | tf_op jit(solution)/shard_map/ppermute | solution.py:459
  13.6 24.3 %copy-start.7 = (s32[2,4,2]{1,2,0:T(2,128)S(1)}, s32[2,4,2]{1,2,0:T(2,128)}, u32[]{:S(2)}) copy-start(s32[2,4,2]{1,2,0:T(2,128)} %param.17) | copy-start | bytes 196
  13.7 34.9 %copy-start.6 = (s32[3,768]{1,0:T(4,128)S(1)}, s32[3,768]{1,0:T(4,128)}, u32[]{:S(2)}) copy-start(s32[3,768]{1,0:T(4,128)} %param.21) | copy-start | bytes 27652
  13.7 35.0 %copy-start.1 = (f32[2,4,256]{2,1,0:T(4,128)S(1)}, f32[2,4,256]{2,1,0:T(4,128)}, u32[]{:S(2)}) copy-start(f32[2,4,256]{2,1,0:T(4,128)} %param.15) | copy-start | bytes 24580
  13.7 35.0 %copy-start.2 = (f32[2,4,256]{2,1,0:T(4,128)S(1)}, f32[2,4,256]{2,1,0:T(4,128)}, u32[]{:S(2)}) copy-start(f32[2,4,256]{2,1,0:T(4,128)} %param.16) | copy-start | bytes 24580
  13.7 35.0 %copy-start.3 = (f32[768]{0:T(1024)S(1)}, f32[768]{0:T(1024)}, u32[]{:S(2)}) copy-start(f32[768]{0:T(1024)} %rate_ref.1) | copy-start | bytes 9220
  13.7 35.0 %copy-start.4 = (f32[768]{0:T(1024)S(1)}, f32[768]{0:T(1024)}, u32[]{:S(2)}) copy-start(f32[768]{0:T(1024)} %barrier_ref.1) | copy-start | bytes 9220
  13.7 35.0 %copy-start.5 = (f32[768]{0:T(1024)S(1)}, f32[768]{0:T(1024)}, u32[]{:S(2)}) copy-start(f32[768]{0:T(1024)} %photo_ref.1) | copy-start | bytes 9220
  21.0 27.5 %collective-permute-start.2 = (f32[512,128]{1,0:T(8,128)S(1)}, f32[512,128]{1,0:T(8,128)S(1)}, u32[]{:S(2)}, u32[]{:S(2)}) collective-permute-start(f32[512,128]{1,0:T(8,128)S(1)} %get-tuple-element.33), channel_id=1, source_target_pairs={{0,1},{1,0},{2,3},{3,2},{4,5},{5,4},{6,7},{7,6},{8,9},{9,8},{10,11... | collective-permute-start | bytes 786440 | tf_op jit(solution)/shard_map/ppermute | solution.py:475
  29.9 6.4 %collective-permute-start.10 = (f32[256,128]{1,0:T(8,128)S(1)}, f32[256,128]{1,0:T(8,128)S(1)}, u32[]{:S(2)}, u32[]{:S(2)}) collective-permute-start(f32[256,128]{1,0:T(8,128)S(1)} %get-tuple-element.48), channel_id=1, source_target_pairs={{0,1},{1,0},{2,3},{3,2},{4,5},{5,4},{6,7},{7,6},{8,9},{9,8},{10,11... | collective-permute-start | bytes 393224 | tf_op jit(solution)/shard_map/ppermute | solution.py:475
  30.5 12.4 %collective-permute-start.11 = (f32[256,128]{1,0:T(8,128)S(1)}, f32[256,128]{1,0:T(8,128)S(1)}, u32[]{:S(2)}, u32[]{:S(2)}) collective-permute-start(f32[256,128]{1,0:T(8,128)S(1)} %get-tuple-element.49), channel_id=1, source_target_pairs={{0,2},{1,3},{2,0},{3,1},{4,6},{5,7},{6,4},{7,5},{8,10},{9,11},{10,... | collective-permute-start | bytes 393224 | tf_op jit(solution)/shard_map/ppermute | solution.py:475
  32.2 14.5 %collective-permute-start.12 = (f32[256,128]{1,0:T(8,128)S(1)}, f32[256,128]{1,0:T(8,128)S(1)}, u32[]{:S(2)}, u32[]{:S(2)}) collective-permute-start(f32[256,128]{1,0:T(8,128)S(1)} %get-tuple-element.50), channel_id=1, source_target_pairs={{0,3},{1,2},{2,1},{3,0},{4,7},{5,6},{6,5},{7,4},{8,11},{9,10},{10,... | collective-permute-start | bytes 393224 | tf_op jit(solution)/shard_map/ppermute | solution.py:475
  33.4 19.4 %collective-permute-start.3 = (f32[512,128]{1,0:T(8,128)S(1)}, f32[512,128]{1,0:T(8,128)S(1)}, u32[]{:S(2)}, u32[]{:S(2)}) collective-permute-start(f32[512,128]{1,0:T(8,128)S(1)} %get-tuple-element.34), channel_id=1, source_target_pairs={{0,2},{1,3},{2,0},{3,1},{4,6},{5,7},{6,4},{7,5},{8,10},{9,11},{10,... | collective-permute-start | bytes 786440 | tf_op jit(solution)/shard_map/ppermute | solution.py:475
  36.3 16.5 %collective-permute-start.4 = (f32[512,128]{1,0:T(8,128)S(1)}, f32[512,128]{1,0:T(8,128)S(1)}, u32[]{:S(2)}, u32[]{:S(2)}) collective-permute-start(f32[512,128]{1,0:T(8,128)S(1)} %get-tuple-element.35), channel_id=1, source_target_pairs={{0,3},{1,2},{2,1},{3,0},{4,7},{5,6},{6,5},{7,4},{8,11},{9,10},{10,... | collective-permute-start | bytes 786440 | tf_op jit(solution)/shard_map/ppermute | solution.py:475
  42.9 20.8 %collective-permute-start.7 = (f32[256,128]{1,0:T(8,128)S(1)}, f32[256,128]{1,0:T(8,128)S(1)}, u32[]{:S(2)}, u32[]{:S(2)}) collective-permute-start(f32[256,128]{1,0:T(8,128)S(1)} %get-tuple-element.42), channel_id=1, source_target_pairs={{0,1},{1,0},{2,3},{3,2},{4,5},{5,4},{6,7},{7,6},{8,9},{9,8},{10,11... | collective-permute-start | bytes 393224 | tf_op jit(solution)/shard_map/ppermute | solution.py:475
  46.8 16.9 %collective-permute-start.8 = (f32[256,128]{1,0:T(8,128)S(1)}, f32[256,128]{1,0:T(8,128)S(1)}, u32[]{:S(2)}, u32[]{:S(2)}) collective-permute-start(f32[256,128]{1,0:T(8,128)S(1)} %get-tuple-element.43), channel_id=1, source_target_pairs={{0,2},{1,3},{2,0},{3,1},{4,6},{5,7},{6,4},{7,5},{8,10},{9,11},{10,... | collective-permute-start | bytes 393224 | tf_op jit(solution)/shard_map/ppermute | solution.py:475
  48.5 15.1 %collective-permute-start.9 = (f32[256,128]{1,0:T(8,128)S(1)}, f32[256,128]{1,0:T(8,128)S(1)}, u32[]{:S(2)}, u32[]{:S(2)}) collective-permute-start(f32[256,128]{1,0:T(8,128)S(1)} %get-tuple-element.44), channel_id=1, source_target_pairs={{0,3},{1,2},{2,1},{3,0},{4,7},{5,6},{6,5},{7,4},{8,11},{9,10},{10,... | collective-permute-start | bytes 393224 | tf_op jit(solution)/shard_map/ppermute | solution.py:475

commit v8 on v7

--- a/solution.py
+++ b/solution.py
@@ -15,6 +15,8 @@
 LOW = 2 * SECTIONS
 HIGH = SECTIONS
 PARTS = 2
+SPLIT_LEVELS = False
+WAYS = 2
 TOGETHER = 8
 CHUNK = 8
 BATCHES = 4
@@ -39,7 +41,7 @@
         self.columns = self.levels * self.tiles
         self.count = self.species // PARTS
         self.area = self.tiles * self.part
-        self.slices = self.levels if self.area % SUB == 0 else 1
+        self.slices = self.levels if SPLIT_LEVELS and self.area % SUB == 0 else 1
         self.slab = self.blocks // self.slices
         self.halo_rows = LOW * self.columns * self.count
         self.span = self.rows + 2 * SUB
@@ -274,7 +276,9 @@
     pieces = z.slab // SUB
     total = PARTS * z.groups
     sources, (lit_ref, k_ref, table_ref) = refs[:total], refs[total : total + 3]
-    out_hbm, result, state, made, lost_a, lost_b, sems = refs[-7:]
+    out_hbm, result, state = refs[total + 3 + (number > 0) :][:3]
+    made, lost_a, lost_b = [refs[-1 - (3 - i) * WAYS :][:WAYS] for i in range(3)]
+    sems = refs[-1]
     reactions = k_ref.shape[0] // z.blocks
     base = number * z.slab
 
@@ -287,9 +291,10 @@
     me = lax.axis_index("tracer")
 
     def prepare(at, p, value):
-        made[at, :] = steps[p] * value
-        lost_a[at, :] = steps[p]
-        lost_b[at, :] = zero
+        for way in range(WAYS):
+            made[way][at, :] = zero if way else steps[p] * value
+            lost_a[way][at, :] = zero if way else steps[p]
+            lost_b[way][at, :] = zero
 
     def begin(index, carry):
         for i, ref in enumerate(sources):
@@ -307,7 +312,7 @@
 
     lax.fori_loop(0, z.count, begin, 0)
 
-    def react(r, carry):
+    def react(r, way):
         first, second, product = table_ref[r], table_ref[reactions + r], table_ref[2 * reactions + r]
         for p in range(pieces):
             k = k_ref[cell(r * z.blocks + base, p), :]
@@ -315,9 +320,13 @@
             y = state[cell(second, p), :]
             kx = k * x
             ky = k * y
-            made[cell(product, p), :] += kx * y
-            lost_a[cell(first, p), :] += ky
-            lost_b[cell(second, p), :] += kx
+            made[way][cell(product, p), :] += kx * y
+            lost_a[way][cell(first, p), :] += ky
+            lost_b[way][cell(second, p), :] += kx
+
+    def several(i, carry):
+        for way in range(WAYS):
+            react(i * WAYS + way, way)
         return carry
 
     batch = species // BATCHES
@@ -327,12 +336,13 @@
         return pltpu.make_async_copy(result.at[rows], out_hbm.at[rows, pl.ds(base, z.slab)], sems.at[i])
 
     for sub in range(DAY_STEPS):
-        lax.fori_loop(0, reactions, react, 0, unroll=16)
+        lax.fori_loop(0, reactions // WAYS, several, 0, unroll=16 // WAYS)
 
         def finish(s, carry):
             for p in range(pieces):
                 at = cell(s * z.slab, p)
-                value = made[at, :] / (lost_a[at, :] + lost_b[at, :])
+                top = sum(ref[at, :] for ref in made)
+                value = top / sum(ref[at, :] for ref in (*lost_a, *lost_b))
                 if sub < DAY_STEPS - 1:
                     prepare(at, p, value)
                     if sub == 0:
@@ -415,7 +425,7 @@
     more = () if out is None else (out,)
     args = (*arrived, lit, k, table, *more)
     scratch = [pltpu.VMEM((species, z.slab, LANES), jnp.float32)]
-    scratch += [pltpu.VMEM((size, LANES), jnp.float32)] * 4 + [pltpu.SemaphoreType.DMA((BATCHES,))]
+    scratch += [pltpu.VMEM((size, LANES), jnp.float32)] * (1 + 3 * WAYS) + [pltpu.SemaphoreType.DMA((BATCHES,))]
     return pl.pallas_call(
         functools.partial(chemistry_kernel, z, species, number),
         out_shape=jax.ShapeDtypeStruct((species, z.blocks, LANES), jnp.float32),
@@ -423,7 +433,7 @@
         out_specs=ANY,
         scratch_shapes=scratch,
         input_output_aliases={len(args) - 1: 0} if more else {},
-        compiler_params=pltpu.CompilerParams(vmem_limit_bytes=20 << 20),
+        compiler_params=pltpu.CompilerParams(vmem_limit_bytes=28 << 20),
         cost_estimate=pl.CostEstimate(flops=400 * size * LANES, bytes_accessed=0, transcendentals=0),
         name="chemistry",
     )(*args)

time: 75.9 us -> 58.4 us (0.77); the launches traced: 74.5 us -> 58 us
  Pallas kernels: 42.8 us -> 31 us
  starting transfers between devices: 20 us -> 12.8 us
  waiting for transfers between devices: 8.91 us -> 11.4 us
    pallas_call x2 -> x1, Pallas kernels: 21.7 us -> 9.84 us  [chemistry(): pl.pallas_call(functools.partial(chemistry_kernel, z, species, number), o...]
    ppermute x9 -> x6, starting transfers between devices: 14.2 us -> 7.11 us  [body(): block = lax.ppermute(block, 'tracer', [(i, i ^ k) for i in range(groups)])]
    ppermute x9 -> x6, waiting for transfers between devices: 6.26 us -> 8.73 us  [body(): block = lax.ppermute(block, 'tracer', [(i, i ^ k) for i in range(groups)])]
  transfers between devices with their start and end apart: 13 -> 10, of which waited for: 4 -> 4; matrix products, arithmetic and copies ran while one was open for 0% -> 0% of each run, Pallas kernels for 41% -> 34%
where the time goes in v8:
time: 58.4 us; the launch traced here: 58 us
  Pallas kernels  31 us (53%)
  starting transfers between devices  12.8 us (22%)
  waiting for transfers between devices  11.4 us (20%)
  local copies, waits for them, and re-layouts  1.8 us (3%)
  other arithmetic  0.8 us (1%)
    pallas_call x2, Pallas kernels, transport(): pl.pallas_call(functools.partial(transport_kernel, z, slices), out_shape=...  14.6 us
    pallas_call x1, Pallas kernels, chemistry(): pl.pallas_call(functools.partial(chemistry_kernel, z, species, number), o...  9.84 us
    ppermute x6, waiting for transfers between devices, body(): block = lax.ppermute(block, 'tracer', [(i, i ^ k) for i in range(groups)])  8.73 us
    ppermute x6, starting transfers between devices, body(): block = lax.ppermute(block, 'tracer', [(i, i ^ k) for i in range(groups)])  7.11 us
    ppermute x2, starting transfers between devices, body(): far = lax.ppermute(far, 'space', far_pairs)  4.43 us
    pallas_call x1, Pallas kernels, rates(): pl.pallas_call(functools.partial(rates_kernel, z.blocks // SUB), out_shap...  3.76 us
    pallas_call x2, Pallas kernels, pack(): pl.pallas_call(functools.partial(pack_kernel, z, part), out_shape=tuple((...  2.83 us
    ppermute x2, waiting for transfers between devices, body(): far = lax.ppermute(far, 'space', far_pairs)  2.65 us
  transfers between devices with their start and end apart: 10, of which 4 were waited for; matrix products, arithmetic and copies ran while one was open for 0% of the time, Pallas kernels for 34%

profile of v8, /device:TPU:16, one launch (start us, length us, event | category | flops | bytes accessed | tf_op | source)
XLA Modules:
  0.0 58.0 jit_solution(18285430354407635962)
XLA Ops:
  0.0 0.8 %pad_maximum_fusion = f32[3,2,2,8,2,128]{5,3,4,2,1,0:T(8,128)S(1)} fusion(f32[1,2,2,8,2,128]{5,3,4,2,1,0:T(8,128)} %bitcast.32, f32[1,2,2,8,2,128]{5,3,4,2,1,0:T(8,128)} %bitcast.33, f32[1,2,2,8,2,128]{5,3,4,2,1,0:T(8,128)} %bitcast.34), kind=kLoop, calls=%fused_computation | loop fusion | flops 49152 | bytes 196608 | tf_op jit(solution)/shard_map/stack | solution.py:458
  0.8 0.0 copy-start
  0.8 1.6 %copy-done = f32[64,2,16,256]{3,2,1,0:T(8,128)S(1)} copy-done((f32[64,2,16,256]{3,2,1,0:T(8,128)S(1)}, f32[64,2,16,256]{3,2,1,0:T(8,128)}, u32[]{:S(2)}) %copy-start) | copy-done | bytes 2097176
  2.4 1.5 %pack.2 = (f32[864,128]{1,0:T(8,128)S(1)}, f32[864,128]{1,0:T(8,128)S(1)}, f32[2048,128]{1,0:T(8,128)S(1)}, f32[192,128]{1,0:T(8,128)S(1)}) custom-call(f32[4096,128]{1,0:T(8,128)S(1)} %bitcast.27, f32[192,128]{1,0:T(8,128)S(1)} %bitcast.29), custom_call_target="tpu_custom_call" | custom-call | flops 26214400 | tf_op jit(solution)/shard_map/pack/pallas_call | solution.py:381
  3.9 0.1 collective-permute-start
  4.0 2.4 %collective-permute-start.1 = (f32[864,128]{1,0:T(8,128)S(1)}, f32[864,128]{1,0:T(8,128)S(1)}, u32[]{:S(2)}, u32[]{:S(2)}) collective-permute-start(f32[864,128]{1,0:T(8,128)S(1)} %get-tuple-element.27), channel_id=1, source_target_pairs={{4,8},{8,4},{12,16},{16,12},{20,24},{24,20},{5,9},{9,5},{13,17},{1... | collective-permute-start | bytes 1327112 | tf_op jit(solution)/shard_map/ppermute | solution.py:469
  6.5 1.3 %pack.3 = (f32[768,128]{1,0:T(8,128)S(1)}, f32[768,128]{1,0:T(8,128)S(1)}, f32[2048,128]{1,0:T(8,128)S(1)}) custom-call(f32[4096,128]{1,0:T(8,128)S(1)} %bitcast.28), custom_call_target="tpu_custom_call" | custom-call | flops 26214400 | tf_op jit(solution)/shard_map/pack/pallas_call | solution.py:381
  7.8 1.2 %collective-permute-start.5 = (f32[768,128]{1,0:T(8,128)S(1)}, f32[768,128]{1,0:T(8,128)S(1)}, u32[]{:S(2)}, u32[]{:S(2)}) collective-permute-start(f32[768,128]{1,0:T(8,128)S(1)} %get-tuple-element.35), channel_id=1, source_target_pairs={{0,4},{4,0},{8,12},{12,8},{16,20},{20,16},{24,28},{28,24},{1,5},{5... | collective-permute-start | bytes 1179656 | tf_op jit(solution)/shard_map/ppermute | solution.py:470
  9.0 2.0 %collective-permute-start.6 = (f32[768,128]{1,0:T(8,128)S(1)}, f32[768,128]{1,0:T(8,128)S(1)}, u32[]{:S(2)}, u32[]{:S(2)}) collective-permute-start(f32[768,128]{1,0:T(8,128)S(1)} %get-tuple-element.36), channel_id=1, source_target_pairs={{4,8},{8,4},{12,16},{16,12},{20,24},{24,20},{5,9},{9,5},{13,17},{1... | collective-permute-start | bytes 1179656 | tf_op jit(solution)/shard_map/ppermute | solution.py:469
  11.0 0.0 collective-permute-done.near_ref
  11.0 2.6 %collective-permute-done.1.far_ref = f32[864,128]{1,0:T(8,128)S(1)} collective-permute-done((f32[864,128]{1,0:T(8,128)S(1)}, f32[864,128]{1,0:T(8,128)S(1)}, u32[]{:S(2)}, u32[]{:S(2)}) %collective-permute-start.1) | collective-permute-done | bytes 442400 | tf_op jit(solution)/shard_map/ppermute | solution.py:469
  13.6 0.0 copy-start.7
  13.7 0.0 copy-start.6
  13.7 0.0 copy-start.1
  13.7 0.0 copy-start.2
  13.7 0.0 copy-start.3
  13.7 0.0 copy-start.4
  13.7 0.0 copy-start.5
  13.7 7.3 %transport.2 = (f32[512,128]{1,0:T(8,128)S(1)}, f32[512,128]{1,0:T(8,128)S(1)}, f32[512,128]{1,0:T(8,128)S(1)}, f32[512,128]{1,0:T(8,128)S(1)}) custom-call(f32[2048,128]{1,0:T(8,128)S(1)} %get-tuple-element.24.field_ref, f32[192,128]{1,0:T(8,128)S(1)} %get-tuple-element.25.courant_ref, f32[96,128]{1,0:T(8,128)S(1)} %slice.8.near_edge, ...), custom_call_target="tpu_custom_call" | custom-call | flops 104857600 | tf_op jit(solution)/shard_map/transport/pallas_call | solution.py:396
  21.0 1.6 %collective-permute-start.2 = (f32[512,128]{1,0:T(8,128)S(1)}, f32[512,128]{1,0:T(8,128)S(1)}, u32[]{:S(2)}, u32[]{:S(2)}) collective-permute-start(f32[512,128]{1,0:T(8,128)S(1)} %get-tuple-element.29), channel_id=1, source_target_pairs={{0,1},{1,0},{2,3},{3,2},{4,5},{5,4},{6,7},{7,6},{8,9},{9,8},{10,11... | collective-permute-start | bytes 786440 | tf_op jit(solution)/shard_map/ppermute | solution.py:485
  22.6 1.6 %collective-permute-start.3 = (f32[512,128]{1,0:T(8,128)S(1)}, f32[512,128]{1,0:T(8,128)S(1)}, u32[]{:S(2)}, u32[]{:S(2)}) collective-permute-start(f32[512,128]{1,0:T(8,128)S(1)} %get-tuple-element.30), channel_id=1, source_target_pairs={{0,2},{1,3},{2,0},{3,1},{4,6},{5,7},{6,4},{7,5},{8,10},{9,11},{10,... | collective-permute-start | bytes 786440 | tf_op jit(solution)/shard_map/ppermute | solution.py:485
  24.2 0.3 collective-permute-start.4
  24.6 0.0 collective-permute-done.5.near_ref
  24.6 0.0 collective-permute-done.6.far_ref
  24.6 7.3 %transport.3 = (f32[512,128]{1,0:T(8,128)S(1)}, f32[512,128]{1,0:T(8,128)S(1)}, f32[512,128]{1,0:T(8,128)S(1)}, f32[512,128]{1,0:T(8,128)S(1)}) custom-call(f32[2048,128]{1,0:T(8,128)S(1)} %get-tuple-element.34.field_ref, f32[192,128]{1,0:T(8,128)S(1)} %get-tuple-element.25.courant_ref, f32[96,128]{1,0:T(8,128)S(1)} %slice.8.near_edge, ...), custom_call_target="tpu_custom_call" | custom-call | flops 104857600 | tf_op jit(solution)/shard_map/transport/pallas_call | solution.py:396
  31.9 1.6 %collective-permute-start.7 = (f32[512,128]{1,0:T(8,128)S(1)}, f32[512,128]{1,0:T(8,128)S(1)}, u32[]{:S(2)}, u32[]{:S(2)}) collective-permute-start(f32[512,128]{1,0:T(8,128)S(1)} %get-tuple-element.38), channel_id=1, source_target_pairs={{0,1},{1,0},{2,3},{3,2},{4,5},{5,4},{6,7},{7,6},{8,9},{9,8},{10,11... | collective-permute-start | bytes 786440 | tf_op jit(solution)/shard_map/ppermute | solution.py:485
  33.4 1.8 %collective-permute-start.8 = (f32[512,128]{1,0:T(8,128)S(1)}, f32[512,128]{1,0:T(8,128)S(1)}, u32[]{:S(2)}, u32[]{:S(2)}) collective-permute-start(f32[512,128]{1,0:T(8,128)S(1)} %get-tuple-element.39), channel_id=1, source_target_pairs={{0,2},{1,3},{2,0},{3,1},{4,6},{5,7},{6,4},{7,5},{8,10},{9,11},{10,... | collective-permute-start | bytes 786440 | tf_op jit(solution)/shard_map/ppermute | solution.py:485
  35.2 0.0 collective-permute-done.2.refs_1_
  35.2 0.2 collective-permute-start.9
  35.4 0.0 copy-done.7
  35.4 0.1 broadcast_in_dim.7
  35.5 0.0 copy-done.6
  35.5 0.1 broadcast_in_dim.8.lit_ref.refs_8_
  35.6 0.0 copy-done.1
  35.6 0.0 copy-done.2
  35.6 0.0 copy-done.3
  35.6 0.0 copy-done.4
  35.6 0.0 copy-done.5
  35.6 3.8 %rates.1.refs_9_ = f32[12288,128]{1,0:T(8,128)S(1)} custom-call(f32[16,128]{1,0:T(8,128)S(1)} %bitcast.30, f32[16,128]{1,0:T(8,128)S(1)} %bitcast.31, s32[16,128]{1,0:T(8,128)S(1)} %broadcast_in_dim.8.lit_ref.refs_8_, f32[768]{0:T(1024)S(1)} %copy-done.3, f32[768]{0:T(1024)S(1)} %copy-done.4, f32[768]{0:T(1024)S(1)} %copy-done.5), custom_call_target="tpu_custom_call" | custom-call | flops 62914560 | tf_op jit(solution)/shard_map/rates/pallas_call | solution.py:410
  39.4 0.0 collective-permute-done.3.refs_2_
  39.4 0.0 collective-permute-done.4.refs_3_
  39.4 2.1 %collective-permute-done.7.refs_5_ = f32[512,128]{1,0:T(8,128)S(1)} collective-permute-done((f32[512,128]{1,0:T(8,128)S(1)}, f32[512,128]{1,0:T(8,128)S(1)}, u32[]{:S(2)}, u32[]{:S(2)}) %collective-permute-start.7) | collective-permute-done | bytes 262176 | tf_op jit(solution)/shard_map/ppermute | solution.py:485
  41.6 5.8 %collective-permute-done.8.refs_6_ = f32[512,128]{1,0:T(8,128)S(1)} collective-permute-done((f32[512,128]{1,0:T(8,128)S(1)}, f32[512,128]{1,0:T(8,128)S(1)}, u32[]{:S(2)}, u32[]{:S(2)}) %collective-permute-start.8) | collective-permute-done | bytes 262176 | tf_op jit(solution)/shard_map/ppermute | solution.py:485
  47.3 0.8 %collective-permute-done.9.refs_7_ = f32[512,128]{1,0:T(8,128)S(1)} collective-permute-done((f32[512,128]{1,0:T(8,128)S(1)}, f32[512,128]{1,0:T(8,128)S(1)}, u32[]{:S(2)}, u32[]{:S(2)}) %collective-permute-start.9) | collective-permute-done | bytes 262176 | tf_op jit(solution)/shard_map/ppermute | solution.py:485
  48.2 9.8 %chemistry.1 = f32[256,16,128]{2,1,0:T(8,128)} custom-call(f32[512,128]{1,0:T(8,128)S(1)} %get-tuple-element.28.refs_0_, f32[512,128]{1,0:T(8,128)S(1)} %collective-permute-done.2.refs_1_, f32[512,128]{1,0:T(8,128)S(1)} %collective-permute-done.3.refs_2_, f32[512,128]{1,0:T(8,128)S(1)} %collective-permute-done.4.refs_3_, ...), custom_call_target="tpu_custom_call" | custom-call | flops 209715200 | tf_op jit(solution)/shard_map/chemistry/pallas_call | solution.py:429
  (4 shorter events, 0.0 us)
Async XLA Ops:
  0.8 1.6 %copy-start = (f32[64,2,16,256]{3,2,1,0:T(8,128)S(1)}, f32[64,2,16,256]{3,2,1,0:T(8,128)}, u32[]{:S(2)}) copy-start(f32[64,2,16,256]{3,2,1,0:T(8,128)} %param.11) | copy-start | bytes 6291460
  3.9 7.0 %collective-permute-start = (f32[864,128]{1,0:T(8,128)S(1)}, f32[864,128]{1,0:T(8,128)S(1)}, u32[]{:S(2)}, u32[]{:S(2)}) collective-permute-start(f32[864,128]{1,0:T(8,128)S(1)} %get-tuple-element.26), channel_id=1, source_target_pairs={{0,4},{4,0},{8,12},{12,8},{16,20},{20,16},{24,28},{28,24},{1,5},{5... | collective-permute-start | bytes 1327112 | tf_op jit(solution)/shard_map/ppermute | solution.py:470
  4.0 9.6 %collective-permute-start.1 = (f32[864,128]{1,0:T(8,128)S(1)}, f32[864,128]{1,0:T(8,128)S(1)}, u32[]{:S(2)}, u32[]{:S(2)}) collective-permute-start(f32[864,128]{1,0:T(8,128)S(1)} %get-tuple-element.27), channel_id=1, source_target_pairs={{4,8},{8,4},{12,16},{16,12},{20,24},{24,20},{5,9},{9,5},{13,17},{1... | collective-permute-start | bytes 1327112 | tf_op jit(solution)/shard_map/ppermute | solution.py:469
  7.8 16.8 %collective-permute-start.5 = (f32[768,128]{1,0:T(8,128)S(1)}, f32[768,128]{1,0:T(8,128)S(1)}, u32[]{:S(2)}, u32[]{:S(2)}) collective-permute-start(f32[768,128]{1,0:T(8,128)S(1)} %get-tuple-element.35), channel_id=1, source_target_pairs={{0,4},{4,0},{8,12},{12,8},{16,20},{20,16},{24,28},{28,24},{1,5},{5... | collective-permute-start | bytes 1179656 | tf_op jit(solution)/shard_map/ppermute | solution.py:470
  9.0 15.6 %collective-permute-start.6 = (f32[768,128]{1,0:T(8,128)S(1)}, f32[768,128]{1,0:T(8,128)S(1)}, u32[]{:S(2)}, u32[]{:S(2)}) collective-permute-start(f32[768,128]{1,0:T(8,128)S(1)} %get-tuple-element.36), channel_id=1, source_target_pairs={{4,8},{8,4},{12,16},{16,12},{20,24},{24,20},{5,9},{9,5},{13,17},{1... | collective-permute-start | bytes 1179656 | tf_op jit(solution)/shard_map/ppermute | solution.py:469
  13.6 21.8 %copy-start.7 = (s32[2,4,2]{1,2,0:T(2,128)S(1)}, s32[2,4,2]{1,2,0:T(2,128)}, u32[]{:S(2)}) copy-start(s32[2,4,2]{1,2,0:T(2,128)} %param.17) | copy-start | bytes 196
  13.7 21.9 %copy-start.6 = (s32[3,768]{1,0:T(4,128)S(1)}, s32[3,768]{1,0:T(4,128)}, u32[]{:S(2)}) copy-start(s32[3,768]{1,0:T(4,128)} %param.21) | copy-start | bytes 27652
  13.7 22.0 %copy-start.1 = (f32[2,4,256]{2,1,0:T(4,128)S(1)}, f32[2,4,256]{2,1,0:T(4,128)}, u32[]{:S(2)}) copy-start(f32[2,4,256]{2,1,0:T(4,128)} %param.15) | copy-start | bytes 24580
  13.7 21.9 %copy-start.2 = (f32[2,4,256]{2,1,0:T(4,128)S(1)}, f32[2,4,256]{2,1,0:T(4,128)}, u32[]{:S(2)}) copy-start(f32[2,4,256]{2,1,0:T(4,128)} %param.16) | copy-start | bytes 24580
  13.7 21.9 %copy-start.3 = (f32[768]{0:T(1024)S(1)}, f32[768]{0:T(1024)}, u32[]{:S(2)}) copy-start(f32[768]{0:T(1024)} %rate_ref.1) | copy-start | bytes 9220
  13.7 21.9 %copy-start.4 = (f32[768]{0:T(1024)S(1)}, f32[768]{0:T(1024)}, u32[]{:S(2)}) copy-start(f32[768]{0:T(1024)} %barrier_ref.1) | copy-start | bytes 9220
  13.7 21.9 %copy-start.5 = (f32[768]{0:T(1024)S(1)}, f32[768]{0:T(1024)}, u32[]{:S(2)}) copy-start(f32[768]{0:T(1024)} %photo_ref.1) | copy-start | bytes 9220
  21.0 14.2 %collective-permute-start.2 = (f32[512,128]{1,0:T(8,128)S(1)}, f32[512,128]{1,0:T(8,128)S(1)}, u32[]{:S(2)}, u32[]{:S(2)}) collective-permute-start(f32[512,128]{1,0:T(8,128)S(1)} %get-tuple-element.29), channel_id=1, source_target_pairs={{0,1},{1,0},{2,3},{3,2},{4,5},{5,4},{6,7},{7,6},{8,9},{9,8},{10,11... | collective-permute-start | bytes 786440 | tf_op jit(solution)/shard_map/ppermute | solution.py:485
  22.6 16.8 %collective-permute-start.3 = (f32[512,128]{1,0:T(8,128)S(1)}, f32[512,128]{1,0:T(8,128)S(1)}, u32[]{:S(2)}, u32[]{:S(2)}) collective-permute-start(f32[512,128]{1,0:T(8,128)S(1)} %get-tuple-element.30), channel_id=1, source_target_pairs={{0,2},{1,3},{2,0},{3,1},{4,6},{5,7},{6,4},{7,5},{8,10},{9,11},{10,... | collective-permute-start | bytes 786440 | tf_op jit(solution)/shard_map/ppermute | solution.py:485
  24.2 15.2 %collective-permute-start.4 = (f32[512,128]{1,0:T(8,128)S(1)}, f32[512,128]{1,0:T(8,128)S(1)}, u32[]{:S(2)}, u32[]{:S(2)}) collective-permute-start(f32[512,128]{1,0:T(8,128)S(1)} %get-tuple-element.31), channel_id=1, source_target_pairs={{0,3},{1,2},{2,1},{3,0},{4,7},{5,6},{6,5},{7,4},{8,11},{9,10},{10,... | collective-permute-start | bytes 786440 | tf_op jit(solution)/shard_map/ppermute | solution.py:485
  31.9 9.7 %collective-permute-start.7 = (f32[512,128]{1,0:T(8,128)S(1)}, f32[512,128]{1,0:T(8,128)S(1)}, u32[]{:S(2)}, u32[]{:S(2)}) collective-permute-start(f32[512,128]{1,0:T(8,128)S(1)} %get-tuple-element.38), channel_id=1, source_target_pairs={{0,1},{1,0},{2,3},{3,2},{4,5},{5,4},{6,7},{7,6},{8,9},{9,8},{10,11... | collective-permute-start | bytes 786440 | tf_op jit(solution)/shard_map/ppermute | solution.py:485
  33.4 13.9 %collective-permute-start.8 = (f32[512,128]{1,0:T(8,128)S(1)}, f32[512,128]{1,0:T(8,128)S(1)}, u32[]{:S(2)}, u32[]{:S(2)}) collective-permute-start(f32[512,128]{1,0:T(8,128)S(1)} %get-tuple-element.39), channel_id=1, source_target_pairs={{0,2},{1,3},{2,0},{3,1},{4,6},{5,7},{6,4},{7,5},{8,10},{9,11},{10,... | collective-permute-start | bytes 786440 | tf_op jit(solution)/shard_map/ppermute | solution.py:485
  35.2 12.9 %collective-permute-start.9 = (f32[512,128]{1,0:T(8,128)S(1)}, f32[512,128]{1,0:T(8,128)S(1)}, u32[]{:S(2)}, u32[]{:S(2)}) collective-permute-start(f32[512,128]{1,0:T(8,128)S(1)} %get-tuple-element.40), channel_id=1, source_target_pairs={{0,3},{1,2},{2,1},{3,0},{4,7},{5,6},{6,5},{7,4},{8,11},{9,10},{10,... | collective-permute-start | bytes 786440 | tf_op jit(solution)/shard_map/ppermute | solution.py:485

commit v9 on v8

--- a/solution.py
+++ b/solution.py
@@ -108,8 +108,7 @@
     def some(index, carry):
         strips = CHUNK * z.levels
         size = strips * z.tiles * z.rows
-        start = pl.multiple_of((part * (z.count // CHUNK) + index) * size, SUB)
-        values = spread(x_ref[pl.ds(start, size), :], strips)
+        values = spread(x_ref[pl.ds(pl.multiple_of(index * size, SUB), size), :], strips)
         for strip in range(strips):
             for tile in range(z.tiles):
                 at = pl.multiple_of(index * size + (strip * z.tiles + tile) * z.rows, SUB)
@@ -275,10 +274,13 @@
 def chemistry_kernel(z, species, number, *refs):
     pieces = z.slab // SUB
     total = PARTS * z.groups
-    sources, (lit_ref, k_ref, table_ref) = refs[:total], refs[total : total + 3]
+    sources, (lit_ref, k_ref, table_in) = refs[:total], refs[total : total + 3]
     out_hbm, result, state = refs[total + 3 + (number > 0) :][:3]
     made, lost_a, lost_b = [refs[-1 - (3 - i) * WAYS :][:WAYS] for i in range(3)]
     sems = refs[-1]
+    table_ref = refs[-2 - 3 * WAYS]
+    table_load = pltpu.make_async_copy(table_in, table_ref, sems.at[BATCHES])
+    table_load.start()
     reactions = k_ref.shape[0] // z.blocks
     base = number * z.slab
 
@@ -311,6 +313,8 @@
         return carry
 
     lax.fori_loop(0, z.count, begin, 0)
+
+    table_load.wait()
 
     def react(r, way):
         first, second, product = table_ref[r], table_ref[reactions + r], table_ref[2 * reactions + r]
@@ -425,11 +429,13 @@
     more = () if out is None else (out,)
     args = (*arrived, lit, k, table, *more)
     scratch = [pltpu.VMEM((species, z.slab, LANES), jnp.float32)]
-    scratch += [pltpu.VMEM((size, LANES), jnp.float32)] * (1 + 3 * WAYS) + [pltpu.SemaphoreType.DMA((BATCHES,))]
+    buffer = pltpu.VMEM((size, LANES), jnp.float32)
+    scratch += [buffer, pltpu.SMEM(table.shape, jnp.int32)] + [buffer] * (3 * WAYS)
+    scratch += [pltpu.SemaphoreType.DMA((BATCHES + 1,))]
     return pl.pallas_call(
         functools.partial(chemistry_kernel, z, species, number),
         out_shape=jax.ShapeDtypeStruct((species, z.blocks, LANES), jnp.float32),
-        in_specs=[VMEM] * (len(arrived) + 2) + [SMEM] + [ANY] * len(more),
+        in_specs=[VMEM] * (len(arrived) + 2) + [ANY] * (1 + len(more)),
         out_specs=ANY,
         scratch_shapes=scratch,
         input_output_aliases={len(args) - 1: 0} if more else {},
@@ -456,16 +462,16 @@
     strips = lax.axis_size("space")
     z = Sizes(mixing_ratio_field, groups)
     courant = flat_rows(jnp.stack([eastward_face_cfl, northward_face_cfl, upward_face_cfl]))
-    field = flat_rows(mixing_ratio_field)
+    whole = mixing_ratio_field
     near_pairs = [(i, i ^ 1) for i in range(strips) if i ^ 1 < strips]
     far_pairs = [(i, ((i + 1) ^ 1) - 1) for i in range(strips) if 0 <= ((i + 1) ^ 1) - 1 < strips]
     fields, halos = [], []
     for part in range(PARTS):
         if part == 0:
-            near, far, ready, courant = pack(z, part, field, courant)
+            near, far, ready, courant = pack(z, part, flat_rows(whole[: z.count]), courant)
         else:
-            field, _ = lax.optimization_barrier((field, ready))
-            near, far, ready = pack(z, part, field)
+            whole, _ = lax.optimization_barrier((whole, ready))
+            near, far, ready = pack(z, part, flat_rows(whole[part * z.count : (part + 1) * z.count]))
         far = lax.ppermute(far, "space", far_pairs)
         near = lax.ppermute(near, "space", near_pairs)
         fields.append(ready)

time: 58.4 us -> 57.5 us (0.985)
  Pallas kernels: 31 us -> 30.4 us
    unnamed x16, local copies, waits for them, and re-layouts: 1.63 us -> 0.04 us
    slice x0 -> x2, local copies, waits for them, and re-layouts: none -> 1.57 us  [the longest x1 1.47 us: body(): whole[:z.count]]
    pallas_call x1, Pallas kernels: 9.84 us -> 9.17 us  [chemistry(): pl.pallas_call(functools.partial(chemistry_kernel, z, species, number), o...]
where the time goes in v9:
time: 57.5 us; the launch traced here: 57.2 us
  Pallas kernels  30.4 us (53%)
  starting transfers between devices  12.8 us (22%)
  waiting for transfers between devices  11.2 us (19%)
  local copies, waits for them, and re-layouts  1.79 us (3%)
  other arithmetic  0.81 us (1%)
    pallas_call x2, Pallas kernels, transport(): pl.pallas_call(functools.partial(transport_kernel, z, slices), out_shape=...  14.6 us
    pallas_call x1, Pallas kernels, chemistry(): pl.pallas_call(functools.partial(chemistry_kernel, z, species, number), o...  9.17 us
    ppermute x6, waiting for transfers between devices, body(): block = lax.ppermute(block, 'tracer', [(i, i ^ k) for i in range(groups)])  8.71 us
    ppermute x6, starting transfers between devices, body(): block = lax.ppermute(block, 'tracer', [(i, i ^ k) for i in range(groups)])  7.11 us
    ppermute x2, starting transfers between devices, body(): far = lax.ppermute(far, 'space', far_pairs)  4.42 us
    pallas_call x1, Pallas kernels, rates(): pl.pallas_call(functools.partial(rates_kernel, z.blocks // SUB), out_shap...  3.76 us
    pallas_call x2, Pallas kernels, pack(): pl.pallas_call(functools.partial(pack_kernel, z, part), out_shape=tuple((...  2.84 us
    ppermute x2, waiting for transfers between devices, body(): far = lax.ppermute(far, 'space', far_pairs)  2.53 us
  transfers between devices with their start and end apart: 10, of which 4 were waited for; matrix products, arithmetic and copies ran while one was open for 0% of the time, Pallas kernels for 34%

profile of v9, /device:TPU:16, one launch (start us, length us, event | category | flops | bytes accessed | tf_op | source)
XLA Modules:
  0.0 57.2 jit_solution(11760564241870201790)
XLA Ops:
  0.0 0.0 copy-start.5
  0.0 1.5 %slice.12 = f32[32,2,16,256]{3,2,1,0:T(8,128)S(1)} slice(f32[64,2,16,256]{3,2,1,0:T(8,128)} %param.11), slice={[0:32], [0:2], [0:16], [0:256]} | slice | bytes 2097152 | tf_op jit(solution)/shard_map/slice | solution.py:471
  1.5 0.8 %pad_maximum_fusion = f32[3,2,2,8,2,128]{5,3,4,2,1,0:T(8,128)S(1)} fusion(f32[1,2,2,8,2,128]{5,3,4,2,1,0:T(8,128)} %bitcast.37, f32[1,2,2,8,2,128]{5,3,4,2,1,0:T(8,128)} %bitcast.38, f32[1,2,2,8,2,128]{5,3,4,2,1,0:T(8,128)} %bitcast.39), kind=kLoop, calls=%fused_computation | loop fusion | flops 49152 | bytes 196608 | tf_op jit(solution)/shard_map/stack | solution.py:464
  2.3 1.5 %pack.2 = (f32[864,128]{1,0:T(8,128)S(1)}, f32[864,128]{1,0:T(8,128)S(1)}, f32[2048,128]{1,0:T(8,128)S(1)}, f32[192,128]{1,0:T(8,128)S(1)}) custom-call(f32[2048,128]{1,0:T(8,128)S(1)} %bitcast.32, f32[192,128]{1,0:T(8,128)S(1)} %bitcast.34), custom_call_target="tpu_custom_call" | custom-call | flops 26214400 | tf_op jit(solution)/shard_map/pack/pallas_call | solution.py:385
  3.8 0.1 collective-permute-start
  3.9 2.4 %collective-permute-start.1 = (f32[864,128]{1,0:T(8,128)S(1)}, f32[864,128]{1,0:T(8,128)S(1)}, u32[]{:S(2)}, u32[]{:S(2)}) collective-permute-start(f32[864,128]{1,0:T(8,128)S(1)} %get-tuple-element.27), channel_id=1, source_target_pairs={{4,8},{8,4},{12,16},{16,12},{20,24},{24,20},{5,9},{9,5},{13,17},{1... | collective-permute-start | bytes 1327112 | tf_op jit(solution)/shard_map/ppermute | solution.py:475
  6.4 0.0 copy-done.5
  6.4 0.1 slice.15
  6.5 1.3 %pack.3 = (f32[768,128]{1,0:T(8,128)S(1)}, f32[768,128]{1,0:T(8,128)S(1)}, f32[2048,128]{1,0:T(8,128)S(1)}) custom-call(f32[2048,128]{1,0:T(8,128)S(1)} %bitcast.33), custom_call_target="tpu_custom_call" | custom-call | flops 26214400 | tf_op jit(solution)/shard_map/pack/pallas_call | solution.py:385
  7.8 1.2 %collective-permute-start.5 = (f32[768,128]{1,0:T(8,128)S(1)}, f32[768,128]{1,0:T(8,128)S(1)}, u32[]{:S(2)}, u32[]{:S(2)}) collective-permute-start(f32[768,128]{1,0:T(8,128)S(1)} %get-tuple-element.35), channel_id=1, source_target_pairs={{0,4},{4,0},{8,12},{12,8},{16,20},{20,16},{24,28},{28,24},{1,5},{5... | collective-permute-start | bytes 1179656 | tf_op jit(solution)/shard_map/ppermute | solution.py:476
  9.0 2.0 %collective-permute-start.6 = (f32[768,128]{1,0:T(8,128)S(1)}, f32[768,128]{1,0:T(8,128)S(1)}, u32[]{:S(2)}, u32[]{:S(2)}) collective-permute-start(f32[768,128]{1,0:T(8,128)S(1)} %get-tuple-element.36), channel_id=1, source_target_pairs={{4,8},{8,4},{12,16},{16,12},{20,24},{24,20},{5,9},{9,5},{13,17},{1... | collective-permute-start | bytes 1179656 | tf_op jit(solution)/shard_map/ppermute | solution.py:475
  11.0 0.0 collective-permute-done.near_ref
  11.0 2.5 %collective-permute-done.1.far_ref = f32[864,128]{1,0:T(8,128)S(1)} collective-permute-done((f32[864,128]{1,0:T(8,128)S(1)}, f32[864,128]{1,0:T(8,128)S(1)}, u32[]{:S(2)}, u32[]{:S(2)}) %collective-permute-start.1) | collective-permute-done | bytes 442400 | tf_op jit(solution)/shard_map/ppermute | solution.py:475
  13.5 0.0 copy-start.7
  13.5 0.0 copy-start.6
  13.6 0.0 copy-start
  13.6 0.0 copy-start.1
  13.6 0.0 copy-start.2
  13.6 0.0 copy-start.3
  13.6 0.0 copy-start.4
  13.6 7.3 %transport.2 = (f32[512,128]{1,0:T(8,128)S(1)}, f32[512,128]{1,0:T(8,128)S(1)}, f32[512,128]{1,0:T(8,128)S(1)}, f32[512,128]{1,0:T(8,128)S(1)}) custom-call(f32[2048,128]{1,0:T(8,128)S(1)} %get-tuple-element.24.field_ref, f32[192,128]{1,0:T(8,128)S(1)} %get-tuple-element.25.courant_ref, f32[96,128]{1,0:T(8,128)S(1)} %slice.16.near_edge, ...), custom_call_target="tpu_custom_call" | custom-call | flops 104857600 | tf_op jit(solution)/shard_map/transport/pallas_call | solution.py:400
  20.9 1.5 %collective-permute-start.2 = (f32[512,128]{1,0:T(8,128)S(1)}, f32[512,128]{1,0:T(8,128)S(1)}, u32[]{:S(2)}, u32[]{:S(2)}) collective-permute-start(f32[512,128]{1,0:T(8,128)S(1)} %get-tuple-element.29), channel_id=1, source_target_pairs={{0,1},{1,0},{2,3},{3,2},{4,5},{5,4},{6,7},{7,6},{8,9},{9,8},{10,11... | collective-permute-start | bytes 786440 | tf_op jit(solution)/shard_map/ppermute | solution.py:491
  22.5 1.6 %collective-permute-start.3 = (f32[512,128]{1,0:T(8,128)S(1)}, f32[512,128]{1,0:T(8,128)S(1)}, u32[]{:S(2)}, u32[]{:S(2)}) collective-permute-start(f32[512,128]{1,0:T(8,128)S(1)} %get-tuple-element.30), channel_id=1, source_target_pairs={{0,2},{1,3},{2,0},{3,1},{4,6},{5,7},{6,4},{7,5},{8,10},{9,11},{10,... | collective-permute-start | bytes 786440 | tf_op jit(solution)/shard_map/ppermute | solution.py:491
  24.1 0.4 collective-permute-start.4
  24.5 0.0 collective-permute-done.5.near_ref
  24.5 0.0 collective-permute-done.6.far_ref
  24.5 7.3 %transport.3 = (f32[512,128]{1,0:T(8,128)S(1)}, f32[512,128]{1,0:T(8,128)S(1)}, f32[512,128]{1,0:T(8,128)S(1)}, f32[512,128]{1,0:T(8,128)S(1)}) custom-call(f32[2048,128]{1,0:T(8,128)S(1)} %get-tuple-element.34.field_ref, f32[192,128]{1,0:T(8,128)S(1)} %get-tuple-element.25.courant_ref, f32[96,128]{1,0:T(8,128)S(1)} %slice.16.near_edge, ...), custom_call_target="tpu_custom_call" | custom-call | flops 104857600 | tf_op jit(solution)/shard_map/transport/pallas_call | solution.py:400
  31.8 1.5 %collective-permute-start.7 = (f32[512,128]{1,0:T(8,128)S(1)}, f32[512,128]{1,0:T(8,128)S(1)}, u32[]{:S(2)}, u32[]{:S(2)}) collective-permute-start(f32[512,128]{1,0:T(8,128)S(1)} %get-tuple-element.38), channel_id=1, source_target_pairs={{0,1},{1,0},{2,3},{3,2},{4,5},{5,4},{6,7},{7,6},{8,9},{9,8},{10,11... | collective-permute-start | bytes 786440 | tf_op jit(solution)/shard_map/ppermute | solution.py:491
  33.3 1.8 %collective-permute-start.8 = (f32[512,128]{1,0:T(8,128)S(1)}, f32[512,128]{1,0:T(8,128)S(1)}, u32[]{:S(2)}, u32[]{:S(2)}) collective-permute-start(f32[512,128]{1,0:T(8,128)S(1)} %get-tuple-element.39), channel_id=1, source_target_pairs={{0,2},{1,3},{2,0},{3,1},{4,6},{5,7},{6,4},{7,5},{8,10},{9,11},{10,... | collective-permute-start | bytes 786440 | tf_op jit(solution)/shard_map/ppermute | solution.py:491
  35.1 0.0 collective-permute-done.2.refs_1_
  35.1 0.2 collective-permute-start.9
  35.3 0.0 copy-done.7
  35.3 0.1 broadcast_in_dim.7
  35.4 0.0 copy-done.6
  35.4 0.1 broadcast_in_dim.8.lit_ref.refs_8_
  35.5 0.0 copy-done
  35.5 0.0 copy-done.1
  35.5 0.0 copy-done.2
  35.5 0.0 copy-done.3
  35.5 0.0 copy-done.4
  35.5 3.8 %rates.1.refs_9_ = f32[12288,128]{1,0:T(8,128)S(1)} custom-call(f32[16,128]{1,0:T(8,128)S(1)} %bitcast.35, f32[16,128]{1,0:T(8,128)S(1)} %bitcast.36, s32[16,128]{1,0:T(8,128)S(1)} %broadcast_in_dim.8.lit_ref.refs_8_, f32[768]{0:T(1024)S(1)} %copy-done.2, f32[768]{0:T(1024)S(1)} %copy-done.3, f32[768]{0:T(1024)S(1)} %copy-done.4), custom_call_target="tpu_custom_call" | custom-call | flops 62914560 | tf_op jit(solution)/shard_map/rates/pallas_call | solution.py:414
  39.3 0.0 collective-permute-done.3.refs_2_
  39.3 0.0 collective-permute-done.4.refs_3_
  39.3 2.1 %collective-permute-done.7.refs_5_ = f32[512,128]{1,0:T(8,128)S(1)} collective-permute-done((f32[512,128]{1,0:T(8,128)S(1)}, f32[512,128]{1,0:T(8,128)S(1)}, u32[]{:S(2)}, u32[]{:S(2)}) %collective-permute-start.7) | collective-permute-done | bytes 262176 | tf_op jit(solution)/shard_map/ppermute | solution.py:491
  41.5 5.8 %collective-permute-done.8.refs_6_ = f32[512,128]{1,0:T(8,128)S(1)} collective-permute-done((f32[512,128]{1,0:T(8,128)S(1)}, f32[512,128]{1,0:T(8,128)S(1)}, u32[]{:S(2)}, u32[]{:S(2)}) %collective-permute-start.8) | collective-permute-done | bytes 262176 | tf_op jit(solution)/shard_map/ppermute | solution.py:491
  47.2 0.8 %collective-permute-done.9.refs_7_ = f32[512,128]{1,0:T(8,128)S(1)} collective-permute-done((f32[512,128]{1,0:T(8,128)S(1)}, f32[512,128]{1,0:T(8,128)S(1)}, u32[]{:S(2)}, u32[]{:S(2)}) %collective-permute-start.9) | collective-permute-done | bytes 262176 | tf_op jit(solution)/shard_map/ppermute | solution.py:491
  48.0 9.2 %chemistry.1 = f32[256,16,128]{2,1,0:T(8,128)} custom-call(f32[512,128]{1,0:T(8,128)S(1)} %get-tuple-element.28.refs_0_, f32[512,128]{1,0:T(8,128)S(1)} %collective-permute-done.2.refs_1_, f32[512,128]{1,0:T(8,128)S(1)} %collective-permute-done.3.refs_2_, f32[512,128]{1,0:T(8,128)S(1)} %collective-permute-done.4.refs_3_, ...), custom_call_target="tpu_custom_call" | custom-call | flops 209715200 | tf_op jit(solution)/shard_map/chemistry/pallas_call | solution.py:435
  (4 shorter events, 0.0 us)
Async XLA Ops:
  0.0 6.4 %copy-start.5 = (f32[64,2,16,256]{3,2,1,0:T(8,128)S(1)}, f32[64,2,16,256]{3,2,1,0:T(8,128)}, u32[]{:S(2)}) copy-start(f32[64,2,16,256]{3,2,1,0:T(8,128)} %param.11) | copy-start | bytes 6291460
  3.8 7.2 %collective-permute-start = (f32[864,128]{1,0:T(8,128)S(1)}, f32[864,128]{1,0:T(8,128)S(1)}, u32[]{:S(2)}, u32[]{:S(2)}) collective-permute-start(f32[864,128]{1,0:T(8,128)S(1)} %get-tuple-element.26), channel_id=1, source_target_pairs={{0,4},{4,0},{8,12},{12,8},{16,20},{20,16},{24,28},{28,24},{1,5},{5... | collective-permute-start | bytes 1327112 | tf_op jit(solution)/shard_map/ppermute | solution.py:476
  3.9 9.6 %collective-permute-start.1 = (f32[864,128]{1,0:T(8,128)S(1)}, f32[864,128]{1,0:T(8,128)S(1)}, u32[]{:S(2)}, u32[]{:S(2)}) collective-permute-start(f32[864,128]{1,0:T(8,128)S(1)} %get-tuple-element.27), channel_id=1, source_target_pairs={{4,8},{8,4},{12,16},{16,12},{20,24},{24,20},{5,9},{9,5},{13,17},{1... | collective-permute-start | bytes 1327112 | tf_op jit(solution)/shard_map/ppermute | solution.py:475
  7.8 16.7 %collective-permute-start.5 = (f32[768,128]{1,0:T(8,128)S(1)}, f32[768,128]{1,0:T(8,128)S(1)}, u32[]{:S(2)}, u32[]{:S(2)}) collective-permute-start(f32[768,128]{1,0:T(8,128)S(1)} %get-tuple-element.35), channel_id=1, source_target_pairs={{0,4},{4,0},{8,12},{12,8},{16,20},{20,16},{24,28},{28,24},{1,5},{5... | collective-permute-start | bytes 1179656 | tf_op jit(solution)/shard_map/ppermute | solution.py:476
  9.0 15.5 %collective-permute-start.6 = (f32[768,128]{1,0:T(8,128)S(1)}, f32[768,128]{1,0:T(8,128)S(1)}, u32[]{:S(2)}, u32[]{:S(2)}) collective-permute-start(f32[768,128]{1,0:T(8,128)S(1)} %get-tuple-element.36), channel_id=1, source_target_pairs={{4,8},{8,4},{12,16},{16,12},{20,24},{24,20},{5,9},{9,5},{13,17},{1... | collective-permute-start | bytes 1179656 | tf_op jit(solution)/shard_map/ppermute | solution.py:475
  13.5 21.8 %copy-start.7 = (s32[2,4,2]{1,2,0:T(2,128)S(1)}, s32[2,4,2]{1,2,0:T(2,128)}, u32[]{:S(2)}) copy-start(s32[2,4,2]{1,2,0:T(2,128)} %param.17) | copy-start | bytes 196
  13.5 21.9 %copy-start.6 = (s32[3,768]{1,0:T(4,128)S(1)}, s32[3,768]{1,0:T(4,128)}, u32[]{:S(2)}) copy-start(s32[3,768]{1,0:T(4,128)} %param.21) | copy-start | bytes 27652
  13.6 22.0 %copy-start = (f32[2,4,256]{2,1,0:T(4,128)S(1)}, f32[2,4,256]{2,1,0:T(4,128)}, u32[]{:S(2)}) copy-start(f32[2,4,256]{2,1,0:T(4,128)} %param.15) | copy-start | bytes 24580
  13.6 22.0 %copy-start.1 = (f32[2,4,256]{2,1,0:T(4,128)S(1)}, f32[2,4,256]{2,1,0:T(4,128)}, u32[]{:S(2)}) copy-start(f32[2,4,256]{2,1,0:T(4,128)} %param.16) | copy-start | bytes 24580
  13.6 21.9 %copy-start.2 = (f32[768]{0:T(1024)S(1)}, f32[768]{0:T(1024)}, u32[]{:S(2)}) copy-start(f32[768]{0:T(1024)} %rate_ref.1) | copy-start | bytes 9220
  13.6 21.9 %copy-start.3 = (f32[768]{0:T(1024)S(1)}, f32[768]{0:T(1024)}, u32[]{:S(2)}) copy-start(f32[768]{0:T(1024)} %barrier_ref.1) | copy-start | bytes 9220
  13.6 21.9 %copy-start.4 = (f32[768]{0:T(1024)S(1)}, f32[768]{0:T(1024)}, u32[]{:S(2)}) copy-start(f32[768]{0:T(1024)} %photo_ref.1) | copy-start | bytes 9220
  20.9 14.2 %collective-permute-start.2 = (f32[512,128]{1,0:T(8,128)S(1)}, f32[512,128]{1,0:T(8,128)S(1)}, u32[]{:S(2)}, u32[]{:S(2)}) collective-permute-start(f32[512,128]{1,0:T(8,128)S(1)} %get-tuple-element.29), channel_id=1, source_target_pairs={{0,1},{1,0},{2,3},{3,2},{4,5},{5,4},{6,7},{7,6},{8,9},{9,8},{10,11... | collective-permute-start | bytes 786440 | tf_op jit(solution)/shard_map/ppermute | solution.py:491
  22.5 16.8 %collective-permute-start.3 = (f32[512,128]{1,0:T(8,128)S(1)}, f32[512,128]{1,0:T(8,128)S(1)}, u32[]{:S(2)}, u32[]{:S(2)}) collective-permute-start(f32[512,128]{1,0:T(8,128)S(1)} %get-tuple-element.30), channel_id=1, source_target_pairs={{0,2},{1,3},{2,0},{3,1},{4,6},{5,7},{6,4},{7,5},{8,10},{9,11},{10,... | collective-permute-start | bytes 786440 | tf_op jit(solution)/shard_map/ppermute | solution.py:491
  24.1 15.2 %collective-permute-start.4 = (f32[512,128]{1,0:T(8,128)S(1)}, f32[512,128]{1,0:T(8,128)S(1)}, u32[]{:S(2)}, u32[]{:S(2)}) collective-permute-start(f32[512,128]{1,0:T(8,128)S(1)} %get-tuple-element.31), channel_id=1, source_target_pairs={{0,3},{1,2},{2,1},{3,0},{4,7},{5,6},{6,5},{7,4},{8,11},{9,10},{10,... | collective-permute-start | bytes 786440 | tf_op jit(solution)/shard_map/ppermute | solution.py:491
  31.8 9.7 %collective-permute-start.7 = (f32[512,128]{1,0:T(8,128)S(1)}, f32[512,128]{1,0:T(8,128)S(1)}, u32[]{:S(2)}, u32[]{:S(2)}) collective-permute-start(f32[512,128]{1,0:T(8,128)S(1)} %get-tuple-element.38), channel_id=1, source_target_pairs={{0,1},{1,0},{2,3},{3,2},{4,5},{5,4},{6,7},{7,6},{8,9},{9,8},{10,11... | collective-permute-start | bytes 786440 | tf_op jit(solution)/shard_map/ppermute | solution.py:491
  33.3 13.9 %collective-permute-start.8 = (f32[512,128]{1,0:T(8,128)S(1)}, f32[512,128]{1,0:T(8,128)S(1)}, u32[]{:S(2)}, u32[]{:S(2)}) collective-permute-start(f32[512,128]{1,0:T(8,128)S(1)} %get-tuple-element.39), channel_id=1, source_target_pairs={{0,2},{1,3},{2,0},{3,1},{4,6},{5,7},{6,4},{7,5},{8,10},{9,11},{10,... | collective-permute-start | bytes 786440 | tf_op jit(solution)/shard_map/ppermute | solution.py:491
  35.1 12.9 %collective-permute-start.9 = (f32[512,128]{1,0:T(8,128)S(1)}, f32[512,128]{1,0:T(8,128)S(1)}, u32[]{:S(2)}, u32[]{:S(2)}) collective-permute-start(f32[512,128]{1,0:T(8,128)S(1)} %get-tuple-element.40), channel_id=1, source_target_pairs={{0,3},{1,2},{2,1},{3,0},{4,7},{5,6},{6,5},{7,4},{8,11},{9,10},{10,... | collective-permute-start | bytes 786440 | tf_op jit(solution)/shard_map/ppermute | solution.py:491

commit v10 on v9

--- a/solution.py
+++ b/solution.py
@@ -18,7 +18,7 @@
 SPLIT_LEVELS = False
 WAYS = 2
 TOGETHER = 8
-CHUNK = 8
+CHUNK = 16
 BATCHES = 4
 LOG2E = 1.4426950408889634
 
@@ -85,7 +85,7 @@
 def pack_kernel(z, part, x_ref, *refs):
     forth = spread_matrix(z.tiles, False)
     if part == 0:
-        courant_ref, near_ref, far_ref, field, courant_out = refs
+        winds, (near_ref, far_ref, field, courant_out) = refs[:3], refs[3:]
     else:
         near_ref, far_ref, field = refs
     odd = lax.rem(lax.axis_index("space"), 2)
@@ -96,7 +96,7 @@
         return reorder([split[:, :, t].reshape(strips * z.rows, LANES) for t in range(z.tiles)], forth)
 
     if part == 0:
-        parts = spread(courant_ref[...], 3 * z.levels)
+        parts = spread(jnp.concatenate([wind[...] for wind in winds]), 3 * z.levels)
         shifted = shift_columns(parts, -1)
         for strip in range(3 * z.levels):
             rows = slice(strip * z.rows, (strip + 1) * z.rows)
@@ -461,14 +461,14 @@
     groups = lax.axis_size("tracer")
     strips = lax.axis_size("space")
     z = Sizes(mixing_ratio_field, groups)
-    courant = flat_rows(jnp.stack([eastward_face_cfl, northward_face_cfl, upward_face_cfl]))
+    winds = [flat_rows(a) for a in (eastward_face_cfl, northward_face_cfl, upward_face_cfl)]
     whole = mixing_ratio_field
     near_pairs = [(i, i ^ 1) for i in range(strips) if i ^ 1 < strips]
     far_pairs = [(i, ((i + 1) ^ 1) - 1) for i in range(strips) if 0 <= ((i + 1) ^ 1) - 1 < strips]
     fields, halos = [], []
     for part in range(PARTS):
         if part == 0:
-            near, far, ready, courant = pack(z, part, flat_rows(whole[: z.count]), courant)
+            near, far, ready, courant = pack(z, part, flat_rows(whole[: z.count]), *winds)
         else:
             whole, _ = lax.optimization_barrier((whole, ready))
             near, far, ready = pack(z, part, flat_rows(whole[part * z.count : (part + 1) * z.count]))

time: 57.5 us -> 56 us (0.974)
  Pallas kernels: 30.4 us -> 28.9 us
  waiting for transfers between devices: 11.2 us -> 12 us
  other arithmetic: 0.81 us -> 0.01 us
    another operation x1 -> x0, other arithmetic: 0.8 us -> none  [body(): jnp.stack([eastward_face_cfl, northward_face_cfl, upward_face_cfl])]
    pallas_call x2, Pallas kernels: 14.6 us -> 13.8 us  [transport(): pl.pallas_call(functools.partial(transport_kernel, z, slices), out_shape=...]
    pallas_call x2, Pallas kernels: 2.84 us -> 2.13 us  [pack(): pl.pallas_call(functools.partial(pack_kernel, z, part), out_shape=tuple((...]
  transfers between devices with their start and end apart: 10 -> 10, of which waited for: 4 -> 4; matrix products, arithmetic and copies ran while one was open for 0% -> 1% of each run, Pallas kernels for 34% -> 33%
where the time goes in v10:
time: 56 us; the launch traced here: 55.7 us
  Pallas kernels  28.9 us (52%)
  starting transfers between devices  12.8 us (23%)
  waiting for transfers between devices  12 us (21%)
  local copies, waits for them, and re-layouts  1.8 us (3%)
    pallas_call x2, Pallas kernels, transport(): pl.pallas_call(functools.partial(transport_kernel, z, slices), out_shape=...  13.8 us
    pallas_call x1, Pallas kernels, chemistry(): pl.pallas_call(functools.partial(chemistry_kernel, z, species, number), o...  9.17 us
    ppermute x6, waiting for transfers between devices, body(): block = lax.ppermute(block, 'tracer', [(i, i ^ k) for i in range(groups)])  9.08 us
    ppermute x6, starting transfers between devices, body(): block = lax.ppermute(block, 'tracer', [(i, i ^ k) for i in range(groups)])  7.11 us
    ppermute x2, starting transfers between devices, body(): far = lax.ppermute(far, 'space', far_pairs)  4.42 us
    pallas_call x1, Pallas kernels, rates(): pl.pallas_call(functools.partial(rates_kernel, z.blocks // SUB), out_shap...  3.76 us
    ppermute x2, waiting for transfers between devices, body(): far = lax.ppermute(far, 'space', far_pairs)  2.87 us
    pallas_call x2, Pallas kernels, pack(): pl.pallas_call(functools.partial(pack_kernel, z, part), out_shape=tuple((...  2.13 us
  transfers between devices with their start and end apart: 10, of which 4 were waited for; matrix products, arithmetic and copies ran while one was open for 1% of the time, Pallas kernels for 33%

profile of v10, /device:TPU:16, one launch (start us, length us, event | category | flops | bytes accessed | tf_op | source)
XLA Modules:
  0.0 55.7 jit_solution(8512914679133963870)
XLA Ops:
  0.0 0.0 copy-start.2
  0.0 0.0 copy-start.8
  0.0 1.5 %slice.12 = f32[32,2,16,256]{3,2,1,0:T(8,128)S(1)} slice(f32[64,2,16,256]{3,2,1,0:T(8,128)} %param.11), slice={[0:32], [0:2], [0:16], [0:256]} | slice | bytes 2097152 | tf_op jit(solution)/shard_map/slice | solution.py:471
  1.5 0.0 copy-done.2
  1.5 0.0 copy-done.1
  1.5 0.0 copy-done
  1.5 1.2 %pack.2 = (f32[864,128]{1,0:T(8,128)S(1)}, f32[864,128]{1,0:T(8,128)S(1)}, f32[2048,128]{1,0:T(8,128)S(1)}, f32[192,128]{1,0:T(8,128)S(1)}) custom-call(f32[2048,128]{1,0:T(8,128)S(1)} %bitcast.41, f32[64,128]{1,0:T(8,128)S(1)} %bitcast.43, f32[64,128]{1,0:T(8,128)S(1)} %bitcast.44, f32[64,128]{1,0:T(8,128)S(1)} %bitcast.45), custom_call_target="tpu_custom_call" | custom-call | flops 26214400 | tf_op jit(solution)/shard_map/pack/pallas_call | solution.py:385
  2.7 0.1 collective-permute-start
  2.8 2.4 %collective-permute-start.1 = (f32[864,128]{1,0:T(8,128)S(1)}, f32[864,128]{1,0:T(8,128)S(1)}, u32[]{:S(2)}, u32[]{:S(2)}) collective-permute-start(f32[864,128]{1,0:T(8,128)S(1)} %get-tuple-element.27), channel_id=1, source_target_pairs={{4,8},{8,4},{12,16},{16,12},{20,24},{24,20},{5,9},{9,5},{13,17},{1... | collective-permute-start | bytes 1327112 | tf_op jit(solution)/shard_map/ppermute | solution.py:475
  5.3 0.0 copy-done.8
  5.3 0.1 slice.15
  5.4 0.9 %pack.3 = (f32[768,128]{1,0:T(8,128)S(1)}, f32[768,128]{1,0:T(8,128)S(1)}, f32[2048,128]{1,0:T(8,128)S(1)}) custom-call(f32[2048,128]{1,0:T(8,128)S(1)} %bitcast.42), custom_call_target="tpu_custom_call" | custom-call | flops 26214400 | tf_op jit(solution)/shard_map/pack/pallas_call | solution.py:385
  6.3 1.2 %collective-permute-start.5 = (f32[768,128]{1,0:T(8,128)S(1)}, f32[768,128]{1,0:T(8,128)S(1)}, u32[]{:S(2)}, u32[]{:S(2)}) collective-permute-start(f32[768,128]{1,0:T(8,128)S(1)} %get-tuple-element.35), channel_id=1, source_target_pairs={{0,4},{4,0},{8,12},{12,8},{16,20},{20,16},{24,28},{28,24},{1,5},{5... | collective-permute-start | bytes 1179656 | tf_op jit(solution)/shard_map/ppermute | solution.py:476
  7.5 2.0 %collective-permute-start.6 = (f32[768,128]{1,0:T(8,128)S(1)}, f32[768,128]{1,0:T(8,128)S(1)}, u32[]{:S(2)}, u32[]{:S(2)}) collective-permute-start(f32[768,128]{1,0:T(8,128)S(1)} %get-tuple-element.36), channel_id=1, source_target_pairs={{4,8},{8,4},{12,16},{16,12},{20,24},{24,20},{5,9},{9,5},{13,17},{1... | collective-permute-start | bytes 1179656 | tf_op jit(solution)/shard_map/ppermute | solution.py:475
  9.5 0.0 collective-permute-done.near_ref
  9.6 2.9 %collective-permute-done.1.far_ref = f32[864,128]{1,0:T(8,128)S(1)} collective-permute-done((f32[864,128]{1,0:T(8,128)S(1)}, f32[864,128]{1,0:T(8,128)S(1)}, u32[]{:S(2)}, u32[]{:S(2)}) %collective-permute-start.1) | collective-permute-done | bytes 442400 | tf_op jit(solution)/shard_map/ppermute | solution.py:475
  12.4 0.0 copy-start.3
  12.4 0.0 copy-start.4
  12.5 0.0 copy-start.5
  12.5 0.0 copy-start.6
  12.5 0.0 copy-start.7
  12.5 6.9 %transport.2 = (f32[512,128]{1,0:T(8,128)S(1)}, f32[512,128]{1,0:T(8,128)S(1)}, f32[512,128]{1,0:T(8,128)S(1)}, f32[512,128]{1,0:T(8,128)S(1)}) custom-call(f32[2048,128]{1,0:T(8,128)S(1)} %get-tuple-element.24.field_ref, f32[192,128]{1,0:T(8,128)S(1)} %get-tuple-element.25.courant_ref, f32[96,128]{1,0:T(8,128)S(1)} %slice.16.near_edge, ...), custom_call_target="tpu_custom_call" | custom-call | flops 104857600 | tf_op jit(solution)/shard_map/transport/pallas_call | solution.py:400
  19.4 1.6 %collective-permute-start.2 = (f32[512,128]{1,0:T(8,128)S(1)}, f32[512,128]{1,0:T(8,128)S(1)}, u32[]{:S(2)}, u32[]{:S(2)}) collective-permute-start(f32[512,128]{1,0:T(8,128)S(1)} %get-tuple-element.29), channel_id=1, source_target_pairs={{0,1},{1,0},{2,3},{3,2},{4,5},{5,4},{6,7},{7,6},{8,9},{9,8},{10,11... | collective-permute-start | bytes 786440 | tf_op jit(solution)/shard_map/ppermute | solution.py:491
  21.0 1.7 %collective-permute-start.3 = (f32[512,128]{1,0:T(8,128)S(1)}, f32[512,128]{1,0:T(8,128)S(1)}, u32[]{:S(2)}, u32[]{:S(2)}) collective-permute-start(f32[512,128]{1,0:T(8,128)S(1)} %get-tuple-element.30), channel_id=1, source_target_pairs={{0,2},{1,3},{2,0},{3,1},{4,6},{5,7},{6,4},{7,5},{8,10},{9,11},{10,... | collective-permute-start | bytes 786440 | tf_op jit(solution)/shard_map/ppermute | solution.py:491
  22.6 0.3 collective-permute-start.4
  23.0 0.0 collective-permute-done.5.near_ref
  23.0 0.0 collective-permute-done.6.far_ref
  23.0 6.9 %transport.3 = (f32[512,128]{1,0:T(8,128)S(1)}, f32[512,128]{1,0:T(8,128)S(1)}, f32[512,128]{1,0:T(8,128)S(1)}, f32[512,128]{1,0:T(8,128)S(1)}) custom-call(f32[2048,128]{1,0:T(8,128)S(1)} %get-tuple-element.34.field_ref, f32[192,128]{1,0:T(8,128)S(1)} %get-tuple-element.25.courant_ref, f32[96,128]{1,0:T(8,128)S(1)} %slice.16.near_edge, ...), custom_call_target="tpu_custom_call" | custom-call | flops 104857600 | tf_op jit(solution)/shard_map/transport/pallas_call | solution.py:400
  29.9 1.6 %collective-permute-start.7 = (f32[512,128]{1,0:T(8,128)S(1)}, f32[512,128]{1,0:T(8,128)S(1)}, u32[]{:S(2)}, u32[]{:S(2)}) collective-permute-start(f32[512,128]{1,0:T(8,128)S(1)} %get-tuple-element.38), channel_id=1, source_target_pairs={{0,1},{1,0},{2,3},{3,2},{4,5},{5,4},{6,7},{7,6},{8,9},{9,8},{10,11... | collective-permute-start | bytes 786440 | tf_op jit(solution)/shard_map/ppermute | solution.py:491
  31.5 1.8 %collective-permute-start.8 = (f32[512,128]{1,0:T(8,128)S(1)}, f32[512,128]{1,0:T(8,128)S(1)}, u32[]{:S(2)}, u32[]{:S(2)}) collective-permute-start(f32[512,128]{1,0:T(8,128)S(1)} %get-tuple-element.39), channel_id=1, source_target_pairs={{0,2},{1,3},{2,0},{3,1},{4,6},{5,7},{6,4},{7,5},{8,10},{9,11},{10,... | collective-permute-start | bytes 786440 | tf_op jit(solution)/shard_map/ppermute | solution.py:491
  33.3 0.0 collective-permute-done.2.refs_1_
  33.3 0.2 collective-permute-start.9
  33.5 0.0 copy-done.10
  33.5 0.1 broadcast_in_dim.7
  33.6 0.0 copy-done.9
  33.6 0.1 broadcast_in_dim.8.lit_ref.refs_8_
  33.7 0.0 copy-done.3
  33.7 0.0 copy-done.4
  33.7 0.0 copy-done.5
  33.7 0.0 copy-done.6
  33.7 0.0 copy-done.7
  33.7 3.8 %rates.1.refs_9_ = f32[12288,128]{1,0:T(8,128)S(1)} custom-call(f32[16,128]{1,0:T(8,128)S(1)} %bitcast.46, f32[16,128]{1,0:T(8,128)S(1)} %bitcast.47, s32[16,128]{1,0:T(8,128)S(1)} %broadcast_in_dim.8.lit_ref.refs_8_, f32[768]{0:T(1024)S(1)} %copy-done.5, f32[768]{0:T(1024)S(1)} %copy-done.6, f32[768]{0:T(1024)S(1)} %copy-done.7), custom_call_target="tpu_custom_call" | custom-call | flops 62914560 | tf_op jit(solution)/shard_map/rates/pallas_call | solution.py:414
  37.5 0.0 collective-permute-done.3.refs_2_
  37.5 0.0 collective-permute-done.4.refs_3_
  37.5 2.5 %collective-permute-done.7.refs_5_ = f32[512,128]{1,0:T(8,128)S(1)} collective-permute-done((f32[512,128]{1,0:T(8,128)S(1)}, f32[512,128]{1,0:T(8,128)S(1)}, u32[]{:S(2)}, u32[]{:S(2)}) %collective-permute-start.7) | collective-permute-done | bytes 262176 | tf_op jit(solution)/shard_map/ppermute | solution.py:491
  40.0 5.8 %collective-permute-done.8.refs_6_ = f32[512,128]{1,0:T(8,128)S(1)} collective-permute-done((f32[512,128]{1,0:T(8,128)S(1)}, f32[512,128]{1,0:T(8,128)S(1)}, u32[]{:S(2)}, u32[]{:S(2)}) %collective-permute-start.8) | collective-permute-done | bytes 262176 | tf_op jit(solution)/shard_map/ppermute | solution.py:491
  45.7 0.8 %collective-permute-done.9.refs_7_ = f32[512,128]{1,0:T(8,128)S(1)} collective-permute-done((f32[512,128]{1,0:T(8,128)S(1)}, f32[512,128]{1,0:T(8,128)S(1)}, u32[]{:S(2)}, u32[]{:S(2)}) %collective-permute-start.9) | collective-permute-done | bytes 262176 | tf_op jit(solution)/shard_map/ppermute | solution.py:491
  46.6 9.2 %chemistry.1 = f32[256,16,128]{2,1,0:T(8,128)} custom-call(f32[512,128]{1,0:T(8,128)S(1)} %get-tuple-element.28.refs_0_, f32[512,128]{1,0:T(8,128)S(1)} %collective-permute-done.2.refs_1_, f32[512,128]{1,0:T(8,128)S(1)} %collective-permute-done.3.refs_2_, f32[512,128]{1,0:T(8,128)S(1)} %collective-permute-done.4.refs_3_, ...), custom_call_target="tpu_custom_call" | custom-call | flops 209715200 | tf_op jit(solution)/shard_map/chemistry/pallas_call | solution.py:435
  (8 shorter events, 0.0 us)
Async XLA Ops:
  0.0 1.5 %copy-start.2 = (f32[2,16,256]{2,1,0:T(8,128)S(1)}, f32[2,16,256]{2,1,0:T(8,128)}, u32[]{:S(2)}) copy-start(f32[2,16,256]{2,1,0:T(8,128)} %param.14) | copy-start | bytes 98308
  0.0 1.5 %copy-start.1 = (f32[2,16,256]{2,1,0:T(8,128)S(1)}, f32[2,16,256]{2,1,0:T(8,128)}, u32[]{:S(2)}) copy-start(f32[2,16,256]{2,1,0:T(8,128)} %param.13) | copy-start | bytes 98308
  0.0 1.5 %copy-start = (f32[2,16,256]{2,1,0:T(8,128)S(1)}, f32[2,16,256]{2,1,0:T(8,128)}, u32[]{:S(2)}) copy-start(f32[2,16,256]{2,1,0:T(8,128)} %param.12) | copy-start | bytes 98308
  0.0 5.2 %copy-start.8 = (f32[64,2,16,256]{3,2,1,0:T(8,128)S(1)}, f32[64,2,16,256]{3,2,1,0:T(8,128)}, u32[]{:S(2)}) copy-start(f32[64,2,16,256]{3,2,1,0:T(8,128)} %param.11) | copy-start | bytes 6291460
  2.7 6.8 %collective-permute-start = (f32[864,128]{1,0:T(8,128)S(1)}, f32[864,128]{1,0:T(8,128)S(1)}, u32[]{:S(2)}, u32[]{:S(2)}) collective-permute-start(f32[864,128]{1,0:T(8,128)S(1)} %get-tuple-element.26), channel_id=1, source_target_pairs={{0,4},{4,0},{8,12},{12,8},{16,20},{20,16},{24,28},{28,24},{1,5},{5... | collective-permute-start | bytes 1327112 | tf_op jit(solution)/shard_map/ppermute | solution.py:476
  2.8 9.6 %collective-permute-start.1 = (f32[864,128]{1,0:T(8,128)S(1)}, f32[864,128]{1,0:T(8,128)S(1)}, u32[]{:S(2)}, u32[]{:S(2)}) collective-permute-start(f32[864,128]{1,0:T(8,128)S(1)} %get-tuple-element.27), channel_id=1, source_target_pairs={{4,8},{8,4},{12,16},{16,12},{20,24},{24,20},{5,9},{9,5},{13,17},{1... | collective-permute-start | bytes 1327112 | tf_op jit(solution)/shard_map/ppermute | solution.py:475
  6.3 16.7 %collective-permute-start.5 = (f32[768,128]{1,0:T(8,128)S(1)}, f32[768,128]{1,0:T(8,128)S(1)}, u32[]{:S(2)}, u32[]{:S(2)}) collective-permute-start(f32[768,128]{1,0:T(8,128)S(1)} %get-tuple-element.35), channel_id=1, source_target_pairs={{0,4},{4,0},{8,12},{12,8},{16,20},{20,16},{24,28},{28,24},{1,5},{5... | collective-permute-start | bytes 1179656 | tf_op jit(solution)/shard_map/ppermute | solution.py:476
  7.5 15.5 %collective-permute-start.6 = (f32[768,128]{1,0:T(8,128)S(1)}, f32[768,128]{1,0:T(8,128)S(1)}, u32[]{:S(2)}, u32[]{:S(2)}) collective-permute-start(f32[768,128]{1,0:T(8,128)S(1)} %get-tuple-element.36), channel_id=1, source_target_pairs={{4,8},{8,4},{12,16},{16,12},{20,24},{24,20},{5,9},{9,5},{13,17},{1... | collective-permute-start | bytes 1179656 | tf_op jit(solution)/shard_map/ppermute | solution.py:475
  12.4 21.1 %copy-start.10 = (s32[2,4,2]{1,2,0:T(2,128)S(1)}, s32[2,4,2]{1,2,0:T(2,128)}, u32[]{:S(2)}) copy-start(s32[2,4,2]{1,2,0:T(2,128)} %param.17) | copy-start | bytes 196
  12.4 21.1 %copy-start.9 = (s32[3,768]{1,0:T(4,128)S(1)}, s32[3,768]{1,0:T(4,128)}, u32[]{:S(2)}) copy-start(s32[3,768]{1,0:T(4,128)} %param.21) | copy-start | bytes 27652
  12.4 21.2 %copy-start.3 = (f32[2,4,256]{2,1,0:T(4,128)S(1)}, f32[2,4,256]{2,1,0:T(4,128)}, u32[]{:S(2)}) copy-start(f32[2,4,256]{2,1,0:T(4,128)} %param.15) | copy-start | bytes 24580
  12.4 21.2 %copy-start.4 = (f32[2,4,256]{2,1,0:T(4,128)S(1)}, f32[2,4,256]{2,1,0:T(4,128)}, u32[]{:S(2)}) copy-start(f32[2,4,256]{2,1,0:T(4,128)} %param.16) | copy-start | bytes 24580
  12.5 21.2 %copy-start.5 = (f32[768]{0:T(1024)S(1)}, f32[768]{0:T(1024)}, u32[]{:S(2)}) copy-start(f32[768]{0:T(1024)} %rate_ref.1) | copy-start | bytes 9220
  12.5 21.2 %copy-start.6 = (f32[768]{0:T(1024)S(1)}, f32[768]{0:T(1024)}, u32[]{:S(2)}) copy-start(f32[768]{0:T(1024)} %barrier_ref.1) | copy-start | bytes 9220
  12.5 21.2 %copy-start.7 = (f32[768]{0:T(1024)S(1)}, f32[768]{0:T(1024)}, u32[]{:S(2)}) copy-start(f32[768]{0:T(1024)} %photo_ref.1) | copy-start | bytes 9220
  19.4 13.8 %collective-permute-start.2 = (f32[512,128]{1,0:T(8,128)S(1)}, f32[512,128]{1,0:T(8,128)S(1)}, u32[]{:S(2)}, u32[]{:S(2)}) collective-permute-start(f32[512,128]{1,0:T(8,128)S(1)} %get-tuple-element.29), channel_id=1, source_target_pairs={{0,1},{1,0},{2,3},{3,2},{4,5},{5,4},{6,7},{7,6},{8,9},{9,8},{10,11... | collective-permute-start | bytes 786440 | tf_op jit(solution)/shard_map/ppermute | solution.py:491
  21.0 16.5 %collective-permute-start.3 = (f32[512,128]{1,0:T(8,128)S(1)}, f32[512,128]{1,0:T(8,128)S(1)}, u32[]{:S(2)}, u32[]{:S(2)}) collective-permute-start(f32[512,128]{1,0:T(8,128)S(1)} %get-tuple-element.30), channel_id=1, source_target_pairs={{0,2},{1,3},{2,0},{3,1},{4,6},{5,7},{6,4},{7,5},{8,10},{9,11},{10,... | collective-permute-start | bytes 786440 | tf_op jit(solution)/shard_map/ppermute | solution.py:491
  22.6 14.8 %collective-permute-start.4 = (f32[512,128]{1,0:T(8,128)S(1)}, f32[512,128]{1,0:T(8,128)S(1)}, u32[]{:S(2)}, u32[]{:S(2)}) collective-permute-start(f32[512,128]{1,0:T(8,128)S(1)} %get-tuple-element.31), channel_id=1, source_target_pairs={{0,3},{1,2},{2,1},{3,0},{4,7},{5,6},{6,5},{7,4},{8,11},{9,10},{10,... | collective-permute-start | bytes 786440 | tf_op jit(solution)/shard_map/ppermute | solution.py:491
  29.9 10.0 %collective-permute-start.7 = (f32[512,128]{1,0:T(8,128)S(1)}, f32[512,128]{1,0:T(8,128)S(1)}, u32[]{:S(2)}, u32[]{:S(2)}) collective-permute-start(f32[512,128]{1,0:T(8,128)S(1)} %get-tuple-element.38), channel_id=1, source_target_pairs={{0,1},{1,0},{2,3},{3,2},{4,5},{5,4},{6,7},{7,6},{8,9},{9,8},{10,11... | collective-permute-start | bytes 786440 | tf_op jit(solution)/shard_map/ppermute | solution.py:491
  31.5 14.3 %collective-permute-start.8 = (f32[512,128]{1,0:T(8,128)S(1)}, f32[512,128]{1,0:T(8,128)S(1)}, u32[]{:S(2)}, u32[]{:S(2)}) collective-permute-start(f32[512,128]{1,0:T(8,128)S(1)} %get-tuple-element.39), channel_id=1, source_target_pairs={{0,2},{1,3},{2,0},{3,1},{4,6},{5,7},{6,4},{7,5},{8,10},{9,11},{10,... | collective-permute-start | bytes 786440 | tf_op jit(solution)/shard_map/ppermute | solution.py:491
  33.3 13.3 %collective-permute-start.9 = (f32[512,128]{1,0:T(8,128)S(1)}, f32[512,128]{1,0:T(8,128)S(1)}, u32[]{:S(2)}, u32[]{:S(2)}) collective-permute-start(f32[512,128]{1,0:T(8,128)S(1)} %get-tuple-element.40), channel_id=1, source_target_pairs={{0,3},{1,2},{2,1},{3,0},{4,7},{5,6},{6,5},{7,4},{8,11},{9,10},{10,... | collective-permute-start | bytes 786440 | tf_op jit(solution)/shard_map/ppermute | solution.py:491
